TPU v7x, 256 devices: a whole 4x4x8 slice. The times are simulated.
256 devices in a mesh: gene: 64 (over x, z, core), cell: 4 (over y).
Axes of the slice: x: 4, y: 4, z: 8, core: 2. Of those that a mesh axis runs over, the one named last changes fastest.
Arguments:
- pool_counts: bfloat16 [20480, 16384], P('gene', 'cell'), may hold values from 0 to 6.5
- cell_picks: int32 [7, 4096], P(None, 'cell'), may hold values from 0 to 16383, as said below
- loadings_init: float32 [64, 20480], P(None, 'gene'), may hold values from -0.0390625 to 0.0390625
Outputs:
- scaled_loadings: float32 [64, 20480], P(None, 'gene')
Inputs may be any that keep to these rules, and one draw needn't show every extreme that they name: `cell_picks`: column b of every row names a pool cell in [(b // 1024) * 4096, (b // 1024 + 1) * 4096); no cell is named twice in one row.
All inputs are finite; a program needn't handle non-finite values.
Results may differ from a plain program's by a relative error of at most 0.018.
Values may be sent and summed in bfloat16 or wider, within the bound.
No kernel may reach another device: no remote copies, remote signals or barrier semaphores. Data moves between devices by JAX's collectives and lax.ppermute only.
A program may use at most 64 MiB of HBM per device.

v0:
```python
import math

import jax
import jax.numpy as jnp
from jax import lax
from jax.experimental import pallas as pl
from jax.experimental.pallas import tpu as pltpu
from jax.sharding import PartitionSpec as P

f32 = jnp.float32
bf16 = jnp.bfloat16
STEP_RATE = 1.0
HIGH = lax.Precision.HIGHEST
NT = (((1,), (1,)), ((), ()))
NN = (((1,), (0,)), ((), ()))


def vmem_call(kernel, outs, count, flops=0, name=None, core=True):
    spec = pl.BlockSpec(memory_space=pltpu.VMEM)
    call = pl.pallas_call(
        kernel,
        out_shape=jax.tree.map(lambda s: pltpu.VMEM(s.shape, s.dtype), outs),
        in_specs=[pl.BlockSpec(memory_space=pltpu.SMEM)] * core + [spec] * count,
        out_specs=jax.tree.map(lambda _: spec, outs),
        cost_estimate=pl.CostEstimate(flops=flops, transcendentals=0, bytes_accessed=0),
        name=name,
    )

    def run(*args):
        held = [pltpu.with_memory_space_constraint(a, pltpu.VMEM) for a in args[core:]]
        return call(*args[:core], *held)

    return run


def split_pair(value):
    high = value.astype(bf16)
    low = (value - high.astype(f32)).astype(bf16)
    return jnp.concatenate([high, low], axis=0)


def gram_of(stepped):
    return lax.dot_general(stepped, stepped, NT, precision=HIGH, preferred_element_type=f32)


def by_core(first, mine, other):
    return jnp.concatenate([jnp.where(first, mine, other), jnp.where(first, other, mine)], axis=0)


def pack_partial(stepped, tile, shift, first, keep_ref, send_ref):
    comps = stepped.shape[0]
    half = comps // 2
    both = lax.dot_general(split_pair(stepped), tile, NT, preferred_element_type=f32)
    scores = both[:comps] + both[comps:]
    if shift is not None:
        scores = scores - shift
    gram = jnp.concatenate([gram_of(stepped), jnp.zeros((comps, 128 - comps), f32)], axis=1)
    rows = scores.shape[1] // 128 + 1
    for j in range(rows):
        chunk = scores[:, j * 128 : (j + 1) * 128] if j + 1 < rows else gram
        top, bottom = chunk[:half], chunk[half:]
        keep_ref[pl.ds(j, half, stride=rows), :] = jnp.where(first, top, bottom)
        send_ref[pl.ds(j, half, stride=rows), :] = jnp.where(first, bottom, top)


def first_kernel(core_ref, loadings_ref, tile_ref, keep_ref, send_ref):
    pack_partial(loadings_ref[...], tile_ref[...], None, core_ref[0] == 0, keep_ref, send_ref)


def stepped_from(parts, previous, inverse, batch):
    comps, genes = previous.shape
    total = sum(part[:comps, :genes].astype(f32) for part in parts)
    stepped = previous + STEP_RATE * (total * (1.0 / batch))
    if inverse is not None:
        stepped = lax.dot_general(inverse, stepped, NN, precision=HIGH, preferred_element_type=f32)
    return stepped


def make_middle(batch, normalised):
    def kernel(core_ref, a, b, c, d, previous_ref, *refs):
        inverse = refs[0][...] if normalised else None
        tile_ref, keep_ref, send_ref, stepped_ref, mean_ref = refs[-5:]
        comps, genes = previous_ref.shape
        parts = (a, b, c, d)
        stepped = stepped_from(parts, previous_ref[...], inverse, batch)
        stepped_ref[...] = stepped
        sums = sum(part[comps : comps + 2, :genes].astype(f32) for part in parts)
        mean = (sums[:1] + sums[1:]) * (1.0 / batch)
        mean_ref[...] = mean
        shift = jnp.sum(stepped * mean, axis=1, keepdims=True)
        pack_partial(stepped, tile_ref[...], shift, core_ref[0] == 0, keep_ref, send_ref)

    return kernel


def make_last(batch):
    def kernel(a, b, c, d, previous_ref, inverse_ref, gram_ref, stepped_ref):
        stepped = stepped_from((a, b, c, d), previous_ref[...], inverse_ref[...], batch)
        stepped_ref[...] = stepped
        gram = gram_of(stepped)
        half = gram.shape[0] // 2
        gram_ref[...] = jnp.concatenate([gram[:half], gram[half:]], axis=1)

    return kernel


def make_sum(count, rows):
    def kernel(in_ref, out_ref):
        for j in range(rows):
            total = jnp.sum(in_ref[pl.ds(j, count, stride=rows), :], axis=0, keepdims=True)
            out_ref[pl.ds(j, count, stride=rows), :] = jnp.broadcast_to(total, (count, 128))

    return kernel


def make_update(half, rows):
    def kernel(core_ref, mine_ref, other_ref, tile_ref, mean_ref, next_ref, out_ref):
        genes = tile_ref.shape[1]
        comps = 2 * half
        width = out_ref.shape[1]
        chunks = [
            by_core(
                core_ref[0] == 0,
                mine_ref[pl.ds(j, half, stride=rows), :],
                other_ref[pl.ds(j, half, stride=rows), :],
            )
            for j in range(rows - 1)
        ]
        scores = jnp.concatenate(chunks, axis=1)
        both = lax.dot_general(split_pair(scores), tile_ref[...], NN, preferred_element_type=f32)
        totals = jnp.sum(scores, axis=1, keepdims=True)
        raw = both[:comps] + both[comps:] - totals * mean_ref[...]
        rest = out_ref.shape[0] - comps - 2
        tall = jnp.concatenate(
            [raw.astype(bf16), split_pair(next_ref[...]), jnp.zeros((rest, genes), bf16)], axis=0
        )
        out_ref[...] = jnp.concatenate([tall, jnp.zeros((tall.shape[0], width - genes), bf16)], axis=1)

    return kernel


def inverse_factor(gram):
    size = gram.shape[0]
    shape = (8, 2 * size)
    rows = lax.broadcasted_iota(jnp.int32, shape, 0)
    lanes = lax.broadcasted_iota(jnp.int32, shape, 1)
    blocks = []
    for b in range(size // 8):
        eye = jnp.where(lanes == rows + (b * 8 + size), 1.0, 0.0).astype(f32)
        left = jnp.concatenate([gram[b * 8 : b * 8 + 8, :], jnp.zeros((8, size), f32)], axis=1)
        blocks.append(left + eye)
    results = list(blocks)
    for k in range(0, size, 2):
        b, r = divmod(k, 8)
        upper = blocks[b][r : r + 1, :]
        lower = blocks[b][r + 1 : r + 2, :]
        columns = [
            tuple(jnp.broadcast_to(blocks[i][:, k + h : k + h + 1], shape) for h in range(2))
            for i in range(b, size // 8)
        ]
        p = columns[0][0][r : r + 1, :]
        q = columns[0][0][r + 1 : r + 2, :]
        t = columns[0][1][r + 1 : r + 2, :]
        over = 1.0 / (p * t - q * q)
        first = (t * upper - q * lower) * over
        second = (p * lower - q * upper) * over
        inverse_p = 1.0 / p
        slope = q * inverse_p
        top = upper * lax.rsqrt(p)
        low = (lower - slope * upper) * lax.rsqrt(t - slope * q)
        results[b] = jnp.where(rows == r, top, jnp.where(rows == r + 1, low, results[b]))
        for i in range(b, size // 8):
            x, y = columns[i - b]
            change = x * first + y * second
            if i == b:
                change = jnp.where(rows > r + 1, change, 0.0)
            blocks[i] = blocks[i] - change
    return jnp.concatenate(results, axis=0)[:, size:]


def make_factor(half, rows):
    def kernel(core_ref, mine_ref, other_ref, out_ref):
        gram = by_core(
            core_ref[0] == 0,
            mine_ref[pl.ds(rows - 1, half, stride=rows), :],
            other_ref[pl.ds(rows - 1, half, stride=rows), :],
        )
        out_ref[...] = inverse_factor(gram[:, : 2 * half])

    return kernel


def make_finish(scale):
    def kernel(in_ref, stepped_ref, out_ref):
        comps = stepped_ref.shape[0]
        total = jnp.sum(in_ref[...], axis=0)
        gram = jnp.concatenate([total[:, :comps], total[:, comps:]], axis=0)
        out_ref[...] = scale * lax.dot_general(
            inverse_factor(gram), stepped_ref[...], NN, precision=HIGH, preferred_element_type=f32
        )

    return kernel


def shards(pool_counts, cell_picks, loadings_init):
    comps, genes = loadings_init.shape
    steps, cells = cell_picks.shape
    half = comps // 2
    local_pool = pool_counts.shape[1]
    cell_devices = lax.axis_size("cell")
    gene_devices = lax.axis_size("gene")
    chips = gene_devices // 2
    batch = cells * cell_devices
    rows = cells // 128 + 1
    width = genes + 128 - genes % 128
    core = (lax.axis_index("gene") % 2).astype(jnp.int32).reshape(1)
    chosen = cell_picks - lax.axis_index("cell") * local_pool
    pool_by_cell = pool_counts.T
    same_core = [[2 * chip + which for chip in range(chips)] for which in range(2)]

    def tile_of(step):
        return jnp.take(pool_by_cell, chosen[step], axis=0, mode="clip")

    def sums_of(tile):
        return jnp.sum(tile, axis=0, dtype=f32, keepdims=True)

    def swap_cores(value):
        return lax.ppermute(value, "gene", [(i, i ^ 1) for i in range(gene_devices)])

    def round_cells(value):
        return [value] + [
            lax.ppermute(value, "cell", [(i, (i + k) % cell_devices) for i in range(cell_devices)])
            for k in range(1, cell_devices)
        ]

    def exchange(value):
        pieces = value.reshape(chips, 1, value.size // chips)
        arrived = lax.all_to_all(pieces, "gene", 0, 0, tiled=True, axis_index_groups=same_core)
        return arrived.reshape(value.shape)

    packed = jax.ShapeDtypeStruct((half * rows, 128), f32)
    square = jax.ShapeDtypeStruct((comps, comps), f32)
    local = jax.ShapeDtypeStruct((comps, genes), f32)
    row = jax.ShapeDtypeStruct((1, genes), f32)
    shared = jax.ShapeDtypeStruct((comps + 8, width), bf16)

    tile = tile_of(0)
    mean = sum(round_cells(sums_of(tile))) * (1.0 / batch)
    keep, send = vmem_call(first_kernel, (packed, packed), 2, name="first")(core, loadings_init, tile)

    def scores_of(keep, send):
        chip_sum = keep + swap_cores(send)
        copies = vmem_call(make_sum(chips, rows), packed, 1, name="add_up", core=False)(exchange(chip_sum))
        mine = exchange(copies)
        return mine, swap_cores(mine)

    def change_of(mine, other, tile, mean, next_sums):
        change = vmem_call(make_update(half, rows), shared, 5, name="update")(
            core, mine, other, tile, mean, next_sums
        )
        return round_cells(change)

    def factor_of(mine, other):
        return vmem_call(make_factor(half, rows), square, 2, flops=10**9, name="factor")(core, mine, other)

    def advance(parts, stepped, inverse, next_tile):
        inputs = [*parts, stepped, *inverse, next_tile]
        return vmem_call(
            make_middle(batch, bool(inverse)), (packed, packed, local, row), len(inputs), name="middle"
        )(core, *inputs)

    def one_step(step, state):
        keep, send, stepped, mean, tile = state
        next_tile = tile_of(step + 1)
        mine, other = scores_of(keep, send)
        parts = change_of(mine, other, tile, mean, sums_of(next_tile))
        inverse = (factor_of(mine, other),)
        return (*advance(parts, stepped, inverse, next_tile), next_tile)

    next_tile = tile_of(1)
    mine, other = scores_of(keep, send)
    parts = change_of(mine, other, tile, mean, sums_of(next_tile))
    state = (*advance(parts, loadings_init, (), next_tile), next_tile)
    keep, send, stepped, mean, tile = lax.fori_loop(1, steps - 1, one_step, state)
    mine, other = scores_of(keep, send)
    parts = change_of(mine, other, tile, mean, mean)
    inverse = factor_of(mine, other)
    gram, stepped = vmem_call(
        make_last(batch),
        (jax.ShapeDtypeStruct((half, 2 * comps), f32), local),
        len(parts) + 2,
        name="last",
        core=False,
    )(*parts, stepped, inverse)
    gram = gram + swap_cores(gram)
    depth = 8
    planes = chips // depth
    gram = sum(
        [gram]
        + [
            lax.ppermute(gram, "gene", [(i, (i + k * 2 * depth) % gene_devices) for i in range(gene_devices)])
            for k in range(1, planes)
        ]
    )
    columns = [
        [(plane * depth + level) * 2 + which for level in range(depth)]
        for plane in range(planes)
        for which in range(2)
    ]
    grams = lax.all_to_all(
        jnp.broadcast_to(gram[None], (depth, *gram.shape)), "gene", 0, 0, tiled=True, axis_index_groups=columns
    )
    scale = math.sqrt(genes * gene_devices)
    return vmem_call(make_finish(scale), local, 2, name="finish", core=False)(grams, stepped)


def solution(mesh):
    placed = (P("gene", "cell"), P(None, "cell"), P(None, "gene"))
    return jax.shard_map(
        shards, mesh=mesh, in_specs=placed, out_specs=P(None, "gene"), check_vma=False
    )
```

profile of v0, /device:TPU:1, one launch (start us, length us, event | category | flops | bytes accessed | tf_op | source)
XLA Modules:
  0.0 345.9 jit_solution(14605033306564190821)
XLA Ops:
  5.4 6.1 %gather_fusion.1 = bf16[1024,320]{1,0:T(8,128)(2,1)S(1)} fusion(bf16[4096,320]{1,0:T(8,128)(2,1)} %bitcast.39, s32[1024]{0:T(1024)S(1)} %broadcast_clamp_fusion.2), kind=kCustom, calls=%fused_computation.1 | custom fusion | bytes 1314816 | tf_op jit(solution)/shard_map/jit(_take)/gather | solution.py:222
  16.9 9.3 %all-to-all-start.2 = ((f32[32,1,1152]{2,1,0:T(1,128)}), f32[32,1,1152]{2,1,0:T(1,128)S(1)}, u32[]{:S(2)}, u32[]{:S(2)}) async-start(f32[32,1,1152]{2,1,0:T(1,128)} %bitcast.8), calls=%async_computation.2 | async-start | bytes 294912 | tf_op jit(solution)/shard_map/all_to_all | solution.py:238
  40.8 6.1 %gather_fusion.2 = bf16[1024,320]{1,0:T(8,128)(2,1)S(1)} fusion(bf16[4096,320]{1,0:T(8,128)(2,1)} %bitcast.40, s32[1024]{0:T(1024)S(1)} %broadcast_clamp_fusion.1), kind=kCustom, calls=%fused_computation.2 | custom fusion | bytes 1314816 | tf_op jit(solution)/shard_map/jit(_take)/gather | solution.py:222
  63.0 218.2 %while.27 = (s32[]{:T(128)}, f32[288,128]{1,0:T(8,128)S(1)}, f32[288,128]{1,0:T(8,128)S(1)}, f32[64,320]{1,0:T(8,128)S(1)}, f32[1,320]{1,0:T(1,128)S(1)}, /*inde...) while((s32[]{:T(128)}, f32[288,128]{1,0:T(8,128)S(1)}, ...), condition=%wide.region_4.5_spmd, body=%wide.region_2.4_spmd.sunk | while | flops 1000692928 | bytes 6635711 | solution.py:284
  66.2 5.3 %all-to-all-start = ((f32[32,1,1152]{2,1,0:T(1,128)}), f32[32,1,1152]{2,1,0:T(1,128)S(1)}, u32[]{:S(2)}, u32[]{:S(2)}) async-start(f32[32,1,1152]{2,1,0:T(1,128)} %bitcast.22), calls=%async_computation | async-start | bytes 294912 | tf_op jit(solution)/shard_map/while/body/eval_jaxpr/all_to_all | solution.py:238
  71.6 9.2 %all-to-all-done = f32[32,1,1152]{2,1,0:T(1,128)S(1)} async-done(((f32[32,1,1152]{2,1,0:T(1,128)}), f32[32,1,1152]{2,1,0:T(1,128)S(1)}, u32[]{:S(2)}, u32[]{:S(2)}) %all-to-all-start) | async-done | bytes 147488 | tf_op jit(solution)/shard_map/while/body/eval_jaxpr/all_to_all | solution.py:238
  81.4 4.7 %all-to-all-start.1 = ((f32[32,1,1152]{2,1,0:T(1,128)}), f32[32,1,1152]{2,1,0:T(1,128)S(1)}, u32[]{:S(2)}, u32[]{:S(2)}) async-start(f32[32,1,1152]{2,1,0:T(1,128)} %bitcast.24), calls=%async_computation.1 | async-start | bytes 294912 | tf_op jit(solution)/shard_map/while/body/eval_jaxpr/all_to_all | solution.py:238
  86.2 6.1 %gather_fusion = bf16[1024,320]{1,0:T(8,128)(2,1)S(1)} fusion(bf16[4096,320]{1,0:T(8,128)(2,1)} %get-tuple-element.535, s32[1024]{0:T(1024)S(1)} %broadcast_clamp_fusion.4), kind=kCustom, calls=%fused_computation.clone.1 | custom fusion | bytes 1314816 | tf_op jit(solution)/shard_map/while/body/eval_jaxpr/jit(_take)/gather | solution.py:222
  109.3 5.2 %all-to-all-start = ((f32[32,1,1152]{2,1,0:T(1,128)}), f32[32,1,1152]{2,1,0:T(1,128)S(1)}, u32[]{:S(2)}, u32[]{:S(2)}) async-start(f32[32,1,1152]{2,1,0:T(1,128)} %bitcast.22), calls=%async_computation | async-start | bytes 294912 | tf_op jit(solution)/shard_map/while/body/eval_jaxpr/all_to_all | solution.py:238
  114.5 9.2 %all-to-all-done = f32[32,1,1152]{2,1,0:T(1,128)S(1)} async-done(((f32[32,1,1152]{2,1,0:T(1,128)}), f32[32,1,1152]{2,1,0:T(1,128)S(1)}, u32[]{:S(2)}, u32[]{:S(2)}) %all-to-all-start) | async-done | bytes 147488 | tf_op jit(solution)/shard_map/while/body/eval_jaxpr/all_to_all | solution.py:238
  124.3 4.7 %all-to-all-start.1 = ((f32[32,1,1152]{2,1,0:T(1,128)}), f32[32,1,1152]{2,1,0:T(1,128)S(1)}, u32[]{:S(2)}, u32[]{:S(2)}) async-start(f32[32,1,1152]{2,1,0:T(1,128)} %bitcast.24), calls=%async_computation.1 | async-start | bytes 294912 | tf_op jit(solution)/shard_map/while/body/eval_jaxpr/all_to_all | solution.py:238
  129.1 6.1 %gather_fusion = bf16[1024,320]{1,0:T(8,128)(2,1)S(1)} fusion(bf16[4096,320]{1,0:T(8,128)(2,1)} %get-tuple-element.535, s32[1024]{0:T(1024)S(1)} %broadcast_clamp_fusion.4), kind=kCustom, calls=%fused_computation.clone.1 | custom fusion | bytes 1314816 | tf_op jit(solution)/shard_map/while/body/eval_jaxpr/jit(_take)/gather | solution.py:222
  153.5 5.2 %all-to-all-start = ((f32[32,1,1152]{2,1,0:T(1,128)}), f32[32,1,1152]{2,1,0:T(1,128)S(1)}, u32[]{:S(2)}, u32[]{:S(2)}) async-start(f32[32,1,1152]{2,1,0:T(1,128)} %bitcast.22), calls=%async_computation | async-start | bytes 294912 | tf_op jit(solution)/shard_map/while/body/eval_jaxpr/all_to_all | solution.py:238
  158.7 9.2 %all-to-all-done = f32[32,1,1152]{2,1,0:T(1,128)S(1)} async-done(((f32[32,1,1152]{2,1,0:T(1,128)}), f32[32,1,1152]{2,1,0:T(1,128)S(1)}, u32[]{:S(2)}, u32[]{:S(2)}) %all-to-all-start) | async-done | bytes 147488 | tf_op jit(solution)/shard_map/while/body/eval_jaxpr/all_to_all | solution.py:238
  173.3 6.1 %gather_fusion = bf16[1024,320]{1,0:T(8,128)(2,1)S(1)} fusion(bf16[4096,320]{1,0:T(8,128)(2,1)} %get-tuple-element.535, s32[1024]{0:T(1024)S(1)} %broadcast_clamp_fusion.4), kind=kCustom, calls=%fused_computation.clone.1 | custom fusion | bytes 1314816 | tf_op jit(solution)/shard_map/while/body/eval_jaxpr/jit(_take)/gather | solution.py:222
  197.2 5.2 %all-to-all-start = ((f32[32,1,1152]{2,1,0:T(1,128)}), f32[32,1,1152]{2,1,0:T(1,128)S(1)}, u32[]{:S(2)}, u32[]{:S(2)}) async-start(f32[32,1,1152]{2,1,0:T(1,128)} %bitcast.22), calls=%async_computation | async-start | bytes 294912 | tf_op jit(solution)/shard_map/while/body/eval_jaxpr/all_to_all | solution.py:238
  202.4 9.2 %all-to-all-done = f32[32,1,1152]{2,1,0:T(1,128)S(1)} async-done(((f32[32,1,1152]{2,1,0:T(1,128)}), f32[32,1,1152]{2,1,0:T(1,128)S(1)}, u32[]{:S(2)}, u32[]{:S(2)}) %all-to-all-start) | async-done | bytes 147488 | tf_op jit(solution)/shard_map/while/body/eval_jaxpr/all_to_all | solution.py:238
  217.0 6.1 %gather_fusion = bf16[1024,320]{1,0:T(8,128)(2,1)S(1)} fusion(bf16[4096,320]{1,0:T(8,128)(2,1)} %get-tuple-element.535, s32[1024]{0:T(1024)S(1)} %broadcast_clamp_fusion.4), kind=kCustom, calls=%fused_computation.clone.1 | custom fusion | bytes 1314816 | tf_op jit(solution)/shard_map/while/body/eval_jaxpr/jit(_take)/gather | solution.py:222
  240.8 5.2 %all-to-all-start = ((f32[32,1,1152]{2,1,0:T(1,128)}), f32[32,1,1152]{2,1,0:T(1,128)S(1)}, u32[]{:S(2)}, u32[]{:S(2)}) async-start(f32[32,1,1152]{2,1,0:T(1,128)} %bitcast.22), calls=%async_computation | async-start | bytes 294912 | tf_op jit(solution)/shard_map/while/body/eval_jaxpr/all_to_all | solution.py:238
  246.1 9.2 %all-to-all-done = f32[32,1,1152]{2,1,0:T(1,128)S(1)} async-done(((f32[32,1,1152]{2,1,0:T(1,128)}), f32[32,1,1152]{2,1,0:T(1,128)S(1)}, u32[]{:S(2)}, u32[]{:S(2)}) %all-to-all-start) | async-done | bytes 147488 | tf_op jit(solution)/shard_map/while/body/eval_jaxpr/all_to_all | solution.py:238
  260.6 6.1 %gather_fusion = bf16[1024,320]{1,0:T(8,128)(2,1)S(1)} fusion(bf16[4096,320]{1,0:T(8,128)(2,1)} %get-tuple-element.535, s32[1024]{0:T(1024)S(1)} %broadcast_clamp_fusion.4), kind=kCustom, calls=%fused_computation.clone.1 | custom fusion | bytes 1314816 | tf_op jit(solution)/shard_map/while/body/eval_jaxpr/jit(_take)/gather | solution.py:222
  284.0 14.2 %all_to_all.63 = f32[32,1,1152]{2,1,0:T(1,128)S(1)} all-to-all(f32[32,1,1152]{2,1,0:T(1,128)S(1)} %bitcast.42), channel_id=1, replica_groups={{0,8,16,24,32,40,48,56,64,72,80,88,96,104,112,120,128,136,144,152,160,1..., dimensions={0} | all-to-all | bytes 294912 | tf_op jit(solution)/shard_map/all_to_all | solution.py:238
  298.2 13.7 %all_to_all.64 = f32[32,1,1152]{2,1,0:T(1,128)S(1)} all-to-all(f32[32,1,1152]{2,1,0:T(1,128)S(1)} %bitcast.38), channel_id=1, replica_groups={{0,8,16,24,32,40,48,56,64,72,80,88,96,104,112,120,128,136,144,152,160,1..., dimensions={0} | all-to-all | bytes 294912 | tf_op jit(solution)/shard_map/all_to_all | solution.py:238
  331.6 10.3 %all_to_all.65.in_ref = f32[8,32,128]{2,1,0:T(8,128)S(1)} all-to-all(f32[8,32,128]{2,1,0:T(8,128)S(1)} %broadcast_in_dim.42), channel_id=1, replica_groups={{0,8,16,24,32,40,48,56},{4,12,20,28,36,44,52,60},{64,72,80,88,96,104,11..., dimensions={0} | all-to-all | bytes 262144 | tf_op jit(solution)/shard_map/all_to_all | solution.py:310
  (177 shorter events, 174.0 us)
Async XLA Ops:
  16.9 18.5 %all-to-all-start.2 = ((f32[32,1,1152]{2,1,0:T(1,128)}), f32[32,1,1152]{2,1,0:T(1,128)S(1)}, u32[]{:S(2)}, u32[]{:S(2)}) async-start(f32[32,1,1152]{2,1,0:T(1,128)} %bitcast.8), calls=%async_computation.2 | async-start | bytes 294912 | tf_op jit(solution)/shard_map/all_to_all | solution.py:238
  26.4 26.9 %collective-permute-start.8 = (f32[1,320]{1,0:T(1,128)S(1)}, f32[1,320]{1,0:T(1,128)S(1)}, u32[]{:S(2)}, u32[]{:S(2)}) collective-permute-start(f32[1,320]{1,0:T(1,128)S(1)} %broadcast_in_dim.39), channel_id=1, source_target_pairs={{0,2},{1,3},{2,0},{3,1},{4,6},{5,7},{6,4},{7,5},{8,10},{9,11},{10,... | collective-permute-start | bytes 3848 | tf_op jit(solution)/shard_map/ppermute | solution.py:232
  29.4 23.9 %collective-permute-start.9 = (f32[1,320]{1,0:T(1,128)S(1)}, f32[1,320]{1,0:T(1,128)S(1)}, u32[]{:S(2)}, u32[]{:S(2)}) collective-permute-start(f32[1,320]{1,0:T(1,128)S(1)} %broadcast_in_dim.39), channel_id=1, source_target_pairs={{0,3},{1,0},{2,1},{3,2},{4,7},{5,4},{6,5},{7,6},{8,11},{9,8},{10,9... | collective-permute-start | bytes 3848 | tf_op jit(solution)/shard_map/ppermute | solution.py:232
  30.2 23.1 %collective-permute-start.7 = (f32[1,320]{1,0:T(1,128)S(1)}, f32[1,320]{1,0:T(1,128)S(1)}, u32[]{:S(2)}, u32[]{:S(2)}) collective-permute-start(f32[1,320]{1,0:T(1,128)S(1)} %broadcast_in_dim.39), channel_id=1, source_target_pairs={{0,1},{1,2},{2,3},{3,0},{4,5},{5,6},{6,7},{7,4},{8,9},{9,10},{10,1... | collective-permute-start | bytes 3848 | tf_op jit(solution)/shard_map/ppermute | solution.py:232
  36.1 13.9 %all-to-all-start.3 = ((f32[32,1,1152]{2,1,0:T(1,128)}), f32[32,1,1152]{2,1,0:T(1,128)S(1)}, u32[]{:S(2)}, u32[]{:S(2)}) async-start(f32[32,1,1152]{2,1,0:T(1,128)} %bitcast.10), calls=%async_computation.3 | async-start | bytes 294912 | tf_op jit(solution)/shard_map/all_to_all | solution.py:238
  57.3 5.1 %collective-permute-start.10 = (bf16[72,384]{1,0:T(8,128)(2,1)S(1)}, bf16[72,384]{1,0:T(8,128)(2,1)S(1)}, u32[]{:S(2)}, u32[]{:S(2)}) collective-permute-start(bf16[72,384]{1,0:T(8,128)(2,1)S(1)} %update.3.a), channel_id=1, source_target_pairs={{0,1},{1,2},{2,3},{3,0},{4,5},{5,6},{6,7},{7,4},{8,9},{9,10},{10,1... | collective-permute-start | bytes 165896 | tf_op jit(solution)/shard_map/ppermute | solution.py:232
  66.2 14.5 %all-to-all-start = ((f32[32,1,1152]{2,1,0:T(1,128)}), f32[32,1,1152]{2,1,0:T(1,128)S(1)}, u32[]{:S(2)}, u32[]{:S(2)}) async-start(f32[32,1,1152]{2,1,0:T(1,128)} %bitcast.22), calls=%async_computation | async-start | bytes 294912 | tf_op jit(solution)/shard_map/while/body/eval_jaxpr/all_to_all | solution.py:238
  81.4 13.9 %all-to-all-start.1 = ((f32[32,1,1152]{2,1,0:T(1,128)}), f32[32,1,1152]{2,1,0:T(1,128)S(1)}, u32[]{:S(2)}, u32[]{:S(2)}) async-start(f32[32,1,1152]{2,1,0:T(1,128)} %bitcast.24), calls=%async_computation.1 | async-start | bytes 294912 | tf_op jit(solution)/shard_map/while/body/eval_jaxpr/all_to_all | solution.py:238
  99.5 5.1 %collective-permute-start.4 = (bf16[72,384]{1,0:T(8,128)(2,1)S(1)}, bf16[72,384]{1,0:T(8,128)(2,1)S(1)}, u32[]{:S(2)}, u32[]{:S(2)}) collective-permute-start(bf16[72,384]{1,0:T(8,128)(2,1)S(1)} %update.5.a), channel_id=1, source_target_pairs={{0,3},{1,0},{2,1},{3,2},{4,7},{5,4},{6,5},{7,6},{8,11},{9,8},{10,9... | collective-permute-start | bytes 165896 | tf_op jit(solution)/shard_map/while/body/eval_jaxpr/ppermute | solution.py:232
  109.3 14.4 %all-to-all-start = ((f32[32,1,1152]{2,1,0:T(1,128)}), f32[32,1,1152]{2,1,0:T(1,128)S(1)}, u32[]{:S(2)}, u32[]{:S(2)}) async-start(f32[32,1,1152]{2,1,0:T(1,128)} %bitcast.22), calls=%async_computation | async-start | bytes 294912 | tf_op jit(solution)/shard_map/while/body/eval_jaxpr/all_to_all | solution.py:238
  124.3 13.9 %all-to-all-start.1 = ((f32[32,1,1152]{2,1,0:T(1,128)}), f32[32,1,1152]{2,1,0:T(1,128)S(1)}, u32[]{:S(2)}, u32[]{:S(2)}) async-start(f32[32,1,1152]{2,1,0:T(1,128)} %bitcast.24), calls=%async_computation.1 | async-start | bytes 294912 | tf_op jit(solution)/shard_map/while/body/eval_jaxpr/all_to_all | solution.py:238
  142.4 6.2 %collective-permute-start.4 = (bf16[72,384]{1,0:T(8,128)(2,1)S(1)}, bf16[72,384]{1,0:T(8,128)(2,1)S(1)}, u32[]{:S(2)}, u32[]{:S(2)}) collective-permute-start(bf16[72,384]{1,0:T(8,128)(2,1)S(1)} %update.5.a), channel_id=1, source_target_pairs={{0,3},{1,0},{2,1},{3,2},{4,7},{5,4},{6,5},{7,6},{8,11},{9,8},{10,9... | collective-permute-start | bytes 165896 | tf_op jit(solution)/shard_map/while/body/eval_jaxpr/ppermute | solution.py:232
  153.5 14.4 %all-to-all-start = ((f32[32,1,1152]{2,1,0:T(1,128)}), f32[32,1,1152]{2,1,0:T(1,128)S(1)}, u32[]{:S(2)}, u32[]{:S(2)}) async-start(f32[32,1,1152]{2,1,0:T(1,128)} %bitcast.22), calls=%async_computation | async-start | bytes 294912 | tf_op jit(solution)/shard_map/while/body/eval_jaxpr/all_to_all | solution.py:238
  168.6 13.9 %all-to-all-start.1 = ((f32[32,1,1152]{2,1,0:T(1,128)}), f32[32,1,1152]{2,1,0:T(1,128)S(1)}, u32[]{:S(2)}, u32[]{:S(2)}) async-start(f32[32,1,1152]{2,1,0:T(1,128)} %bitcast.24), calls=%async_computation.1 | async-start | bytes 294912 | tf_op jit(solution)/shard_map/while/body/eval_jaxpr/all_to_all | solution.py:238
  186.6 5.1 %collective-permute-start.4 = (bf16[72,384]{1,0:T(8,128)(2,1)S(1)}, bf16[72,384]{1,0:T(8,128)(2,1)S(1)}, u32[]{:S(2)}, u32[]{:S(2)}) collective-permute-start(bf16[72,384]{1,0:T(8,128)(2,1)S(1)} %update.5.a), channel_id=1, source_target_pairs={{0,3},{1,0},{2,1},{3,2},{4,7},{5,4},{6,5},{7,6},{8,11},{9,8},{10,9... | collective-permute-start | bytes 165896 | tf_op jit(solution)/shard_map/while/body/eval_jaxpr/ppermute | solution.py:232
  188.5 5.1 %collective-permute-start.2 = (bf16[72,384]{1,0:T(8,128)(2,1)S(1)}, bf16[72,384]{1,0:T(8,128)(2,1)S(1)}, u32[]{:S(2)}, u32[]{:S(2)}) collective-permute-start(bf16[72,384]{1,0:T(8,128)(2,1)S(1)} %update.5.a), channel_id=1, source_target_pairs={{0,1},{1,2},{2,3},{3,0},{4,5},{5,6},{6,7},{7,4},{8,9},{9,10},{10,1... | collective-permute-start | bytes 165896 | tf_op jit(solution)/shard_map/while/body/eval_jaxpr/ppermute | solution.py:232
  197.2 14.4 %all-to-all-start = ((f32[32,1,1152]{2,1,0:T(1,128)}), f32[32,1,1152]{2,1,0:T(1,128)S(1)}, u32[]{:S(2)}, u32[]{:S(2)}) async-start(f32[32,1,1152]{2,1,0:T(1,128)} %bitcast.22), calls=%async_computation | async-start | bytes 294912 | tf_op jit(solution)/shard_map/while/body/eval_jaxpr/all_to_all | solution.py:238
  212.3 13.9 %all-to-all-start.1 = ((f32[32,1,1152]{2,1,0:T(1,128)}), f32[32,1,1152]{2,1,0:T(1,128)S(1)}, u32[]{:S(2)}, u32[]{:S(2)}) async-start(f32[32,1,1152]{2,1,0:T(1,128)} %bitcast.24), calls=%async_computation.1 | async-start | bytes 294912 | tf_op jit(solution)/shard_map/while/body/eval_jaxpr/all_to_all | solution.py:238
  230.3 5.4 %collective-permute-start.4 = (bf16[72,384]{1,0:T(8,128)(2,1)S(1)}, bf16[72,384]{1,0:T(8,128)(2,1)S(1)}, u32[]{:S(2)}, u32[]{:S(2)}) collective-permute-start(bf16[72,384]{1,0:T(8,128)(2,1)S(1)} %update.5.a), channel_id=1, source_target_pairs={{0,3},{1,0},{2,1},{3,2},{4,7},{5,4},{6,5},{7,6},{8,11},{9,8},{10,9... | collective-permute-start | bytes 165896 | tf_op jit(solution)/shard_map/while/body/eval_jaxpr/ppermute | solution.py:232
  231.9 5.0 %collective-permute-start.2 = (bf16[72,384]{1,0:T(8,128)(2,1)S(1)}, bf16[72,384]{1,0:T(8,128)(2,1)S(1)}, u32[]{:S(2)}, u32[]{:S(2)}) collective-permute-start(bf16[72,384]{1,0:T(8,128)(2,1)S(1)} %update.5.a), channel_id=1, source_target_pairs={{0,1},{1,2},{2,3},{3,0},{4,5},{5,6},{6,7},{7,4},{8,9},{9,10},{10,1... | collective-permute-start | bytes 165896 | tf_op jit(solution)/shard_map/while/body/eval_jaxpr/ppermute | solution.py:232
  240.8 14.4 %all-to-all-start = ((f32[32,1,1152]{2,1,0:T(1,128)}), f32[32,1,1152]{2,1,0:T(1,128)S(1)}, u32[]{:S(2)}, u32[]{:S(2)}) async-start(f32[32,1,1152]{2,1,0:T(1,128)} %bitcast.22), calls=%async_computation | async-start | bytes 294912 | tf_op jit(solution)/shard_map/while/body/eval_jaxpr/all_to_all | solution.py:238
  255.9 13.9 %all-to-all-start.1 = ((f32[32,1,1152]{2,1,0:T(1,128)}), f32[32,1,1152]{2,1,0:T(1,128)S(1)}, u32[]{:S(2)}, u32[]{:S(2)}) async-start(f32[32,1,1152]{2,1,0:T(1,128)} %bitcast.24), calls=%async_computation.1 | async-start | bytes 294912 | tf_op jit(solution)/shard_map/while/body/eval_jaxpr/all_to_all | solution.py:238
  273.9 5.5 %collective-permute-start.4 = (bf16[72,384]{1,0:T(8,128)(2,1)S(1)}, bf16[72,384]{1,0:T(8,128)(2,1)S(1)}, u32[]{:S(2)}, u32[]{:S(2)}) collective-permute-start(bf16[72,384]{1,0:T(8,128)(2,1)S(1)} %update.5.a), channel_id=1, source_target_pairs={{0,3},{1,0},{2,1},{3,2},{4,7},{5,4},{6,5},{7,6},{8,11},{9,8},{10,9... | collective-permute-start | bytes 165896 | tf_op jit(solution)/shard_map/while/body/eval_jaxpr/ppermute | solution.py:232
  315.9 5.2 %collective-permute-start.17 = (bf16[72,384]{1,0:T(8,128)(2,1)S(1)}, bf16[72,384]{1,0:T(8,128)(2,1)S(1)}, u32[]{:S(2)}, u32[]{:S(2)}) collective-permute-start(bf16[72,384]{1,0:T(8,128)(2,1)S(1)} %update.4.a), channel_id=1, source_target_pairs={{0,3},{1,0},{2,1},{3,2},{4,7},{5,4},{6,5},{7,6},{8,11},{9,8},{10,9... | collective-permute-start | bytes 165896 | tf_op jit(solution)/shard_map/ppermute | solution.py:232
  (31 other events, 121.1 us)
where the time goes:
time: 347 us; the launch traced here: 346 us
  starting transfers between devices  122 us (35%)
  waiting for transfers between devices  98.4 us (28%)
  local copies, waits for them, and re-layouts  48.3 us (14%)
  blocking collectives  38.2 us (11%)
  Pallas kernels  32.5 us (9%)
  other arithmetic  6.02 us (2%)
    all_to_all x12, waiting for transfers between devices, exchange(): lax.all_to_all(pieces, 'gene', 0, 0, tiled=True, axis_index_groups=same_c...  68.8 us
    all_to_all x12, starting transfers between devices, exchange(): lax.all_to_all(pieces, 'gene', 0, 0, tiled=True, axis_index_groups=same_c...  63.4 us
    gather x7, local copies, waits for them, and re-layouts, tile_of(): return jnp.take(pool_by_cell, chosen[step], axis=0, mode='clip')  42.5 us
    ppermute x15, starting transfers between devices, swap_cores(): lax.ppermute(value, 'gene', [(i, i ^ 1) for i in range(gene_devices)])  34.6 us
    pallas_call x29, Pallas kernels, run(): return call(*args[:core], *held)  32.5 us
    all_to_all x2, blocking collectives, exchange(): lax.all_to_all(pieces, 'gene', 0, 0, tiled=True, axis_index_groups=same_c...  27.9 us
    ppermute x24, starting transfers between devices, round_cells(): lax.ppermute(value, 'cell', [(i, (i + k) % cell_devices) for i in range(c...  21.7 us
    ppermute x15, waiting for transfers between devices, swap_cores(): lax.ppermute(value, 'gene', [(i, i ^ 1) for i in range(gene_devices)])  14 us
  transfers between devices with their start and end apart: 54, of which 44 were waited for; matrix products, arithmetic and copies ran while one was open for 11% of the time, Pallas kernels for 5%

commit v1 on v0

--- a/solution.py
+++ b/solution.py
@@ -15,20 +15,24 @@
 NN = (((1,), (0,)), ((), ()))
 
 
-def vmem_call(kernel, outs, count, flops=0, name=None, core=True):
+def vmem_call(kernel, outs, count, flops=0, name=None, core=True, pool=0, scratch=(), held=True):
     spec = pl.BlockSpec(memory_space=pltpu.VMEM)
     call = pl.pallas_call(
         kernel,
-        out_shape=jax.tree.map(lambda s: pltpu.VMEM(s.shape, s.dtype), outs),
-        in_specs=[pl.BlockSpec(memory_space=pltpu.SMEM)] * core + [spec] * count,
+        out_shape=jax.tree.map(lambda s: pltpu.VMEM(s.shape, s.dtype), outs) if held else outs,
+        in_specs=[pl.BlockSpec(memory_space=pltpu.SMEM)] * core
+        + [spec] * count
+        + [pl.BlockSpec(memory_space=pl.ANY)] * pool,
         out_specs=jax.tree.map(lambda _: spec, outs),
         cost_estimate=pl.CostEstimate(flops=flops, transcendentals=0, bytes_accessed=0),
+        scratch_shapes=scratch,
         name=name,
     )
 
     def run(*args):
-        held = [pltpu.with_memory_space_constraint(a, pltpu.VMEM) for a in args[core:]]
-        return call(*args[:core], *held)
+        last = core + count
+        near = [pltpu.with_memory_space_constraint(a, pltpu.VMEM) for a in args[core:last]]
+        return call(*args[:core], *near, *args[last:])
 
     return run
 
@@ -47,14 +51,10 @@
     return jnp.concatenate([jnp.where(first, mine, other), jnp.where(first, other, mine)], axis=0)
 
 
-def pack_partial(stepped, tile, shift, first, keep_ref, send_ref):
-    comps = stepped.shape[0]
+def spread(scores, gram, first, keep_ref, send_ref):
+    comps = scores.shape[0]
     half = comps // 2
-    both = lax.dot_general(split_pair(stepped), tile, NT, preferred_element_type=f32)
-    scores = both[:comps] + both[comps:]
-    if shift is not None:
-        scores = scores - shift
-    gram = jnp.concatenate([gram_of(stepped), jnp.zeros((comps, 128 - comps), f32)], axis=1)
+    gram = jnp.concatenate([gram, jnp.zeros((comps, 128 - comps), f32)], axis=1)
     rows = scores.shape[1] // 128 + 1
     for j in range(rows):
         chunk = scores[:, j * 128 : (j + 1) * 128] if j + 1 < rows else gram
@@ -63,8 +63,37 @@
         send_ref[pl.ds(j, half, stride=rows), :] = jnp.where(first, bottom, top)
 
 
-def first_kernel(core_ref, loadings_ref, tile_ref, keep_ref, send_ref):
-    pack_partial(loadings_ref[...], tile_ref[...], None, core_ref[0] == 0, keep_ref, send_ref)
+def pack_partial(stepped, tile, shift, first, keep_ref, send_ref):
+    comps = stepped.shape[0]
+    both = lax.dot_general(split_pair(stepped), tile, NT, preferred_element_type=f32)
+    spread(both[:comps] + both[comps:] - shift, gram_of(stepped), first, keep_ref, send_ref)
+
+
+def first_kernel(core_ref, loadings_ref, picks_ref, pool_ref, keep_ref, send_ref, buffer_ref, sems):
+    chunks, _, size = buffer_ref.shape
+    copies = [
+        pltpu.make_async_copy(pool_ref.at[:, pl.ds(i * size, size)], buffer_ref.at[i], sems.at[i])
+        for i in range(chunks)
+    ]
+    for copy in copies:
+        copy.start()
+    loadings = loadings_ref[...]
+    comps = loadings.shape[0]
+    pair = split_pair(loadings)
+    picks = picks_ref[...]
+    places = lax.broadcasted_iota(jnp.int32, (size, picks.shape[1]), 0)
+    chosen = jnp.zeros((2 * comps, picks.shape[1]), f32)
+    for i, copy in enumerate(copies):
+        copy.wait()
+        both = lax.dot_general(pair, buffer_ref[i], NN, preferred_element_type=f32)
+        every = split_pair(both[:comps] + both[comps:])
+        one_hot = jnp.where(places == picks - i * size, 1.0, 0.0).astype(bf16)
+        chosen = chosen + lax.dot_general(every, one_hot, NN, preferred_element_type=f32)
+    spread(chosen[:comps] + chosen[comps:], gram_of(loadings), core_ref[0] == 0, keep_ref, send_ref)
+
+
+def add_kernel(a, b, out_ref):
+    out_ref[...] = a[...] + b[...]
 
 
 def stepped_from(parts, previous, inverse, batch):
@@ -230,7 +259,7 @@
     def round_cells(value):
         return [value] + [
             lax.ppermute(value, "cell", [(i, (i + k) % cell_devices) for i in range(cell_devices)])
-            for k in range(1, cell_devices)
+            for k in (2, 1, 3)
         ]
 
     def exchange(value):
@@ -246,10 +275,18 @@
 
     tile = tile_of(0)
     mean = sum(round_cells(sums_of(tile))) * (1.0 / batch)
-    keep, send = vmem_call(first_kernel, (packed, packed), 2, name="first")(core, loadings_init, tile)
+    chunk = local_pool // 8
+    keep, send = vmem_call(
+        first_kernel,
+        (packed, packed),
+        2,
+        name="first",
+        pool=1,
+        scratch=[pltpu.VMEM((8, genes, chunk), bf16), pltpu.SemaphoreType.DMA((8,))],
+    )(core, loadings_init, chosen[:1], pool_counts)
 
     def scores_of(keep, send):
-        chip_sum = keep + swap_cores(send)
+        chip_sum = vmem_call(add_kernel, packed, 2, name="pair", core=False)(keep, swap_cores(send))
         copies = vmem_call(make_sum(chips, rows), packed, 1, name="add_up", core=False)(exchange(chip_sum))
         mine = exchange(copies)
         return mine, swap_cores(mine)
@@ -311,7 +348,7 @@
         jnp.broadcast_to(gram[None], (depth, *gram.shape)), "gene", 0, 0, tiled=True, axis_index_groups=columns
     )
     scale = math.sqrt(genes * gene_devices)
-    return vmem_call(make_finish(scale), local, 2, name="finish", core=False)(grams, stepped)
+    return vmem_call(make_finish(scale), local, 2, name="finish", core=False, held=False)(grams, stepped)
 
 
 def solution(mesh):

time: 347 us -> 356 us (1.026)
  starting transfers between devices: 122 us -> 135 us
  waiting for transfers between devices: 98.4 us -> 89.5 us
  Pallas kernels: 32.5 us -> 41.4 us
  other arithmetic: 6.02 us -> 2.04 us
    pallas_call x29 -> x36, Pallas kernels: 32.5 us -> 41.4 us  [run(): return call(*args[:core], *near, *args[last:])]
    ppermute x24, starting transfers between devices: 21.7 us -> 30.3 us  [round_cells(): lax.ppermute(value, 'cell', [(i, (i + k) % cell_devices) for i in range(c...]
    all_to_all x12, starting transfers between devices: 63.4 us -> 68 us  [exchange(): lax.all_to_all(pieces, 'gene', 0, 0, tiled=True, axis_index_groups=same_c...]
    all_to_all x12, waiting for transfers between devices: 68.8 us -> 64.2 us  [exchange(): lax.all_to_all(pieces, 'gene', 0, 0, tiled=True, axis_index_groups=same_c...]
    add x7 -> x0, other arithmetic: 3.99 us -> none  [scores_of(): chip_sum = keep + swap_cores(send)]
  transfers between devices with their start and end apart: 54 -> 54, of which waited for: 44 -> 37; matrix products, arithmetic and copies ran while one was open for 11% -> 13% of each run, Pallas kernels for 5% -> 5%
where the time goes in v1:
time: 356 us; the launch traced here: 354 us
  starting transfers between devices  135 us (38%)
  waiting for transfers between devices  89.5 us (25%)
  local copies, waits for them, and re-layouts  46.8 us (13%)
  Pallas kernels  41.4 us (12%)
  blocking collectives  38.2 us (11%)
    all_to_all x12, starting transfers between devices, exchange(): lax.all_to_all(pieces, 'gene', 0, 0, tiled=True, axis_index_groups=same_c...  68 us
    all_to_all x12, waiting for transfers between devices, exchange(): lax.all_to_all(pieces, 'gene', 0, 0, tiled=True, axis_index_groups=same_c...  64.2 us
    gather x7, local copies, waits for them, and re-layouts, tile_of(): return jnp.take(pool_by_cell, chosen[step], axis=0, mode='clip')  42.5 us
    pallas_call x36, Pallas kernels, run(): return call(*args[:core], *near, *args[last:])  41.4 us
    ppermute x15, starting transfers between devices, swap_cores(): lax.ppermute(value, 'gene', [(i, i ^ 1) for i in range(gene_devices)])  34.7 us
    ppermute x24, starting transfers between devices, round_cells(): lax.ppermute(value, 'cell', [(i, (i + k) % cell_devices) for i in range(c...  30.3 us
    all_to_all x2, blocking collectives, exchange(): lax.all_to_all(pieces, 'gene', 0, 0, tiled=True, axis_index_groups=same_c...  27.9 us
    ppermute x15, waiting for transfers between devices, swap_cores(): lax.ppermute(value, 'gene', [(i, i ^ 1) for i in range(gene_devices)])  13 us
  transfers between devices with their start and end apart: 54, of which 37 were waited for; matrix products, arithmetic and copies ran while one was open for 13% of the time, Pallas kernels for 5%

profile of v1, /device:TPU:1, one launch (start us, length us, event | category | flops | bytes accessed | tf_op | source)
XLA Modules:
  0.0 353.7 jit_solution(5116669768651934925)
XLA Ops:
  1.7 4.7 %first.1 = (f32[288,128]{1,0:T(8,128)S(1)}, f32[288,128]{1,0:T(8,128)S(1)}) custom-call(s32[1]{0:T(128)} %bitcast.5.core_ref, f32[64,320]{1,0:T(8,128)S(1)} %copy-done, s32[1,1024]{1,0:T(1,128)S(1)} %get-tuple-element.435.picks_ref, bf16[320,4096]{1,0:T(8,128)(2,1)} %pool_ref.1), custom_call_target="tpu_custom_call" | custom-call | tf_op jit(solution)/shard_map/first/pallas_call | solution.py:35
  13.2 9.3 %all-to-all-start.2 = ((f32[32,1,1152]{2,1,0:T(1,128)}), f32[32,1,1152]{2,1,0:T(1,128)S(1)}, u32[]{:S(2)}, u32[]{:S(2)}) async-start(f32[32,1,1152]{2,1,0:T(1,128)} %bitcast.6), calls=%async_computation.2 | async-start | bytes 294912 | tf_op jit(solution)/shard_map/all_to_all | solution.py:267
  22.5 6.1 %gather_fusion.1 = bf16[1024,320]{1,0:T(8,128)(2,1)S(1)} fusion(bf16[4096,320]{1,0:T(8,128)(2,1)} %bitcast.41, s32[1024]{0:T(1024)S(1)} %broadcast_clamp_fusion.2), kind=kCustom, calls=%fused_computation.1 | custom fusion | bytes 1314816 | tf_op jit(solution)/shard_map/jit(_take)/gather | solution.py:251
  33.9 9.2 %all-to-all-start.3 = ((f32[32,1,1152]{2,1,0:T(1,128)}), f32[32,1,1152]{2,1,0:T(1,128)S(1)}, u32[]{:S(2)}, u32[]{:S(2)}) async-start(f32[32,1,1152]{2,1,0:T(1,128)} %bitcast.8), calls=%async_computation.3 | async-start | bytes 294912 | tf_op jit(solution)/shard_map/all_to_all | solution.py:267
  43.1 6.1 %gather_fusion.2 = bf16[1024,320]{1,0:T(8,128)(2,1)S(1)} fusion(bf16[4096,320]{1,0:T(8,128)(2,1)} %bitcast.42, s32[1024]{0:T(1024)S(1)} %broadcast_clamp_fusion.1), kind=kCustom, calls=%fused_computation.2 | custom fusion | bytes 1314816 | tf_op jit(solution)/shard_map/jit(_take)/gather | solution.py:251
  63.3 224.6 %while.27 = (s32[]{:T(128)}, f32[288,128]{1,0:T(8,128)S(1)}, f32[288,128]{1,0:T(8,128)S(1)}, f32[64,320]{1,0:T(8,128)S(1)}, f32[1,320]{1,0:T(1,128)S(1)}, /*inde...) while((s32[]{:T(128)}, f32[288,128]{1,0:T(8,128)S(1)}, ...), condition=%wide.region_4.5_spmd, body=%wide.region_2.4_spmd.sunk | while | flops 1000656064 | bytes 6193343 | solution.py:321
  67.1 5.4 %all-to-all-start = ((f32[32,1,1152]{2,1,0:T(1,128)}), f32[32,1,1152]{2,1,0:T(1,128)S(1)}, u32[]{:S(2)}, u32[]{:S(2)}) async-start(f32[32,1,1152]{2,1,0:T(1,128)} %bitcast.22), calls=%async_computation | async-start | bytes 294912 | tf_op jit(solution)/shard_map/while/body/eval_jaxpr/all_to_all | solution.py:267
  72.5 9.2 %all-to-all-done = f32[32,1,1152]{2,1,0:T(1,128)S(1)} async-done(((f32[32,1,1152]{2,1,0:T(1,128)}), f32[32,1,1152]{2,1,0:T(1,128)S(1)}, u32[]{:S(2)}, u32[]{:S(2)}) %all-to-all-start) | async-done | bytes 147488 | tf_op jit(solution)/shard_map/while/body/eval_jaxpr/all_to_all | solution.py:267
  87.1 6.1 %gather_fusion = bf16[1024,320]{1,0:T(8,128)(2,1)S(1)} fusion(bf16[4096,320]{1,0:T(8,128)(2,1)} %get-tuple-element.532, s32[1024]{0:T(1024)S(1)} %broadcast_clamp_fusion.4), kind=kCustom, calls=%fused_computation.clone.1 | custom fusion | bytes 1314816 | tf_op jit(solution)/shard_map/while/body/eval_jaxpr/jit(_take)/gather | solution.py:251
  111.6 5.2 %all-to-all-start = ((f32[32,1,1152]{2,1,0:T(1,128)}), f32[32,1,1152]{2,1,0:T(1,128)S(1)}, u32[]{:S(2)}, u32[]{:S(2)}) async-start(f32[32,1,1152]{2,1,0:T(1,128)} %bitcast.22), calls=%async_computation | async-start | bytes 294912 | tf_op jit(solution)/shard_map/while/body/eval_jaxpr/all_to_all | solution.py:267
  116.8 9.2 %all-to-all-done = f32[32,1,1152]{2,1,0:T(1,128)S(1)} async-done(((f32[32,1,1152]{2,1,0:T(1,128)}), f32[32,1,1152]{2,1,0:T(1,128)S(1)}, u32[]{:S(2)}, u32[]{:S(2)}) %all-to-all-start) | async-done | bytes 147488 | tf_op jit(solution)/shard_map/while/body/eval_jaxpr/all_to_all | solution.py:267
  131.4 6.1 %gather_fusion = bf16[1024,320]{1,0:T(8,128)(2,1)S(1)} fusion(bf16[4096,320]{1,0:T(8,128)(2,1)} %get-tuple-element.532, s32[1024]{0:T(1024)S(1)} %broadcast_clamp_fusion.4), kind=kCustom, calls=%fused_computation.clone.1 | custom fusion | bytes 1314816 | tf_op jit(solution)/shard_map/while/body/eval_jaxpr/jit(_take)/gather | solution.py:251
  156.5 5.2 %all-to-all-start = ((f32[32,1,1152]{2,1,0:T(1,128)}), f32[32,1,1152]{2,1,0:T(1,128)S(1)}, u32[]{:S(2)}, u32[]{:S(2)}) async-start(f32[32,1,1152]{2,1,0:T(1,128)} %bitcast.22), calls=%async_computation | async-start | bytes 294912 | tf_op jit(solution)/shard_map/while/body/eval_jaxpr/all_to_all | solution.py:267
  161.7 9.2 %all-to-all-done = f32[32,1,1152]{2,1,0:T(1,128)S(1)} async-done(((f32[32,1,1152]{2,1,0:T(1,128)}), f32[32,1,1152]{2,1,0:T(1,128)S(1)}, u32[]{:S(2)}, u32[]{:S(2)}) %all-to-all-start) | async-done | bytes 147488 | tf_op jit(solution)/shard_map/while/body/eval_jaxpr/all_to_all | solution.py:267
  176.3 6.1 %gather_fusion = bf16[1024,320]{1,0:T(8,128)(2,1)S(1)} fusion(bf16[4096,320]{1,0:T(8,128)(2,1)} %get-tuple-element.532, s32[1024]{0:T(1024)S(1)} %broadcast_clamp_fusion.4), kind=kCustom, calls=%fused_computation.clone.1 | custom fusion | bytes 1314816 | tf_op jit(solution)/shard_map/while/body/eval_jaxpr/jit(_take)/gather | solution.py:251
  201.4 5.2 %all-to-all-start = ((f32[32,1,1152]{2,1,0:T(1,128)}), f32[32,1,1152]{2,1,0:T(1,128)S(1)}, u32[]{:S(2)}, u32[]{:S(2)}) async-start(f32[32,1,1152]{2,1,0:T(1,128)} %bitcast.22), calls=%async_computation | async-start | bytes 294912 | tf_op jit(solution)/shard_map/while/body/eval_jaxpr/all_to_all | solution.py:267
  206.6 9.2 %all-to-all-done = f32[32,1,1152]{2,1,0:T(1,128)S(1)} async-done(((f32[32,1,1152]{2,1,0:T(1,128)}), f32[32,1,1152]{2,1,0:T(1,128)S(1)}, u32[]{:S(2)}, u32[]{:S(2)}) %all-to-all-start) | async-done | bytes 147488 | tf_op jit(solution)/shard_map/while/body/eval_jaxpr/all_to_all | solution.py:267
  221.1 6.1 %gather_fusion = bf16[1024,320]{1,0:T(8,128)(2,1)S(1)} fusion(bf16[4096,320]{1,0:T(8,128)(2,1)} %get-tuple-element.532, s32[1024]{0:T(1024)S(1)} %broadcast_clamp_fusion.4), kind=kCustom, calls=%fused_computation.clone.1 | custom fusion | bytes 1314816 | tf_op jit(solution)/shard_map/while/body/eval_jaxpr/jit(_take)/gather | solution.py:251
  246.2 5.2 %all-to-all-start = ((f32[32,1,1152]{2,1,0:T(1,128)}), f32[32,1,1152]{2,1,0:T(1,128)S(1)}, u32[]{:S(2)}, u32[]{:S(2)}) async-start(f32[32,1,1152]{2,1,0:T(1,128)} %bitcast.22), calls=%async_computation | async-start | bytes 294912 | tf_op jit(solution)/shard_map/while/body/eval_jaxpr/all_to_all | solution.py:267
  251.5 9.2 %all-to-all-done = f32[32,1,1152]{2,1,0:T(1,128)S(1)} async-done(((f32[32,1,1152]{2,1,0:T(1,128)}), f32[32,1,1152]{2,1,0:T(1,128)S(1)}, u32[]{:S(2)}, u32[]{:S(2)}) %all-to-all-start) | async-done | bytes 147488 | tf_op jit(solution)/shard_map/while/body/eval_jaxpr/all_to_all | solution.py:267
  266.0 6.1 %gather_fusion = bf16[1024,320]{1,0:T(8,128)(2,1)S(1)} fusion(bf16[4096,320]{1,0:T(8,128)(2,1)} %get-tuple-element.532, s32[1024]{0:T(1024)S(1)} %broadcast_clamp_fusion.4), kind=kCustom, calls=%fused_computation.clone.1 | custom fusion | bytes 1314816 | tf_op jit(solution)/shard_map/while/body/eval_jaxpr/jit(_take)/gather | solution.py:251
  290.5 14.2 %all_to_all.63 = f32[32,1,1152]{2,1,0:T(1,128)S(1)} all-to-all(f32[32,1,1152]{2,1,0:T(1,128)S(1)} %bitcast.36), channel_id=1, replica_groups={{0,8,16,24,32,40,48,56,64,72,80,88,96,104,112,120,128,136,144,152,160,1..., dimensions={0} | all-to-all | bytes 294912 | tf_op jit(solution)/shard_map/all_to_all | solution.py:267
  304.7 13.7 %all_to_all.64 = f32[32,1,1152]{2,1,0:T(1,128)S(1)} all-to-all(f32[32,1,1152]{2,1,0:T(1,128)S(1)} %bitcast.39), channel_id=1, replica_groups={{0,8,16,24,32,40,48,56,64,72,80,88,96,104,112,120,128,136,144,152,160,1..., dimensions={0} | all-to-all | bytes 294912 | tf_op jit(solution)/shard_map/all_to_all | solution.py:267
  339.4 10.3 %all_to_all.65.in_ref = f32[8,32,128]{2,1,0:T(8,128)S(1)} all-to-all(f32[8,32,128]{2,1,0:T(8,128)S(1)} %broadcast_in_dim.42), channel_id=1, replica_groups={{0,8,16,24,32,40,48,56},{4,12,20,28,36,44,52,60},{64,72,80,88,96,104,11..., dimensions={0} | all-to-all | bytes 262144 | tf_op jit(solution)/shard_map/all_to_all | solution.py:347
  (180 shorter events, 177.1 us)
Async XLA Ops:
  6.4 6.1 %collective-permute-start.5 = (f32[288,128]{1,0:T(8,128)S(1)}, f32[288,128]{1,0:T(8,128)S(1)}, u32[]{:S(2)}, u32[]{:S(2)}) collective-permute-start(f32[288,128]{1,0:T(8,128)S(1)} %get-tuple-element.404), channel_id=1, source_target_pairs={{0,4},{4,0},{8,12},{12,8},{16,20},{20,16},{24,28},{28,24},{32,36},... | collective-permute-start | bytes 442376 | tf_op jit(solution)/shard_map/ppermute | solution.py:257
  13.2 20.0 %all-to-all-start.2 = ((f32[32,1,1152]{2,1,0:T(1,128)}), f32[32,1,1152]{2,1,0:T(1,128)S(1)}, u32[]{:S(2)}, u32[]{:S(2)}) async-start(f32[32,1,1152]{2,1,0:T(1,128)} %bitcast.6), calls=%async_computation.2 | async-start | bytes 294912 | tf_op jit(solution)/shard_map/all_to_all | solution.py:267
  28.8 26.6 %collective-permute-start.8 = (f32[1,320]{1,0:T(1,128)S(1)}, f32[1,320]{1,0:T(1,128)S(1)}, u32[]{:S(2)}, u32[]{:S(2)}) collective-permute-start(f32[1,320]{1,0:T(1,128)S(1)} %broadcast_in_dim.39), channel_id=1, source_target_pairs={{0,1},{1,2},{2,3},{3,0},{4,5},{5,6},{6,7},{7,4},{8,9},{9,10},{10,1... | collective-permute-start | bytes 3848 | tf_op jit(solution)/shard_map/ppermute | solution.py:261
  30.1 25.2 %collective-permute-start.9 = (f32[1,320]{1,0:T(1,128)S(1)}, f32[1,320]{1,0:T(1,128)S(1)}, u32[]{:S(2)}, u32[]{:S(2)}) collective-permute-start(f32[1,320]{1,0:T(1,128)S(1)} %broadcast_in_dim.39), channel_id=1, source_target_pairs={{0,3},{1,0},{2,1},{3,2},{4,7},{5,4},{6,5},{7,6},{8,11},{9,8},{10,9... | collective-permute-start | bytes 3848 | tf_op jit(solution)/shard_map/ppermute | solution.py:261
  31.7 23.7 %collective-permute-start.7 = (f32[1,320]{1,0:T(1,128)S(1)}, f32[1,320]{1,0:T(1,128)S(1)}, u32[]{:S(2)}, u32[]{:S(2)}) collective-permute-start(f32[1,320]{1,0:T(1,128)S(1)} %broadcast_in_dim.39), channel_id=1, source_target_pairs={{0,2},{1,3},{2,0},{3,1},{4,6},{5,7},{6,4},{7,5},{8,10},{9,11},{10,... | collective-permute-start | bytes 3848 | tf_op jit(solution)/shard_map/ppermute | solution.py:261
  33.9 18.4 %all-to-all-start.3 = ((f32[32,1,1152]{2,1,0:T(1,128)}), f32[32,1,1152]{2,1,0:T(1,128)S(1)}, u32[]{:S(2)}, u32[]{:S(2)}) async-start(f32[32,1,1152]{2,1,0:T(1,128)} %bitcast.8), calls=%async_computation.3 | async-start | bytes 294912 | tf_op jit(solution)/shard_map/all_to_all | solution.py:267
  67.1 14.6 %all-to-all-start = ((f32[32,1,1152]{2,1,0:T(1,128)}), f32[32,1,1152]{2,1,0:T(1,128)S(1)}, u32[]{:S(2)}, u32[]{:S(2)}) async-start(f32[32,1,1152]{2,1,0:T(1,128)} %bitcast.22), calls=%async_computation | async-start | bytes 294912 | tf_op jit(solution)/shard_map/while/body/eval_jaxpr/all_to_all | solution.py:267
  82.4 13.9 %all-to-all-start.1 = ((f32[32,1,1152]{2,1,0:T(1,128)}), f32[32,1,1152]{2,1,0:T(1,128)S(1)}, u32[]{:S(2)}, u32[]{:S(2)}) async-start(f32[32,1,1152]{2,1,0:T(1,128)} %bitcast.24), calls=%async_computation.1 | async-start | bytes 294912 | tf_op jit(solution)/shard_map/while/body/eval_jaxpr/all_to_all | solution.py:267
  100.4 6.5 %collective-permute-start.4 = (bf16[72,384]{1,0:T(8,128)(2,1)S(1)}, bf16[72,384]{1,0:T(8,128)(2,1)S(1)}, u32[]{:S(2)}, u32[]{:S(2)}) collective-permute-start(bf16[72,384]{1,0:T(8,128)(2,1)S(1)} %update.5.a), channel_id=1, source_target_pairs={{0,3},{1,0},{2,1},{3,2},{4,7},{5,4},{6,5},{7,6},{8,11},{9,8},{10,9... | collective-permute-start | bytes 165896 | tf_op jit(solution)/shard_map/while/body/eval_jaxpr/ppermute | solution.py:261
  111.6 14.4 %all-to-all-start = ((f32[32,1,1152]{2,1,0:T(1,128)}), f32[32,1,1152]{2,1,0:T(1,128)S(1)}, u32[]{:S(2)}, u32[]{:S(2)}) async-start(f32[32,1,1152]{2,1,0:T(1,128)} %bitcast.22), calls=%async_computation | async-start | bytes 294912 | tf_op jit(solution)/shard_map/while/body/eval_jaxpr/all_to_all | solution.py:267
  126.7 13.9 %all-to-all-start.1 = ((f32[32,1,1152]{2,1,0:T(1,128)}), f32[32,1,1152]{2,1,0:T(1,128)S(1)}, u32[]{:S(2)}, u32[]{:S(2)}) async-start(f32[32,1,1152]{2,1,0:T(1,128)} %bitcast.24), calls=%async_computation.1 | async-start | bytes 294912 | tf_op jit(solution)/shard_map/while/body/eval_jaxpr/all_to_all | solution.py:267
  144.7 7.0 %collective-permute-start.4 = (bf16[72,384]{1,0:T(8,128)(2,1)S(1)}, bf16[72,384]{1,0:T(8,128)(2,1)S(1)}, u32[]{:S(2)}, u32[]{:S(2)}) collective-permute-start(bf16[72,384]{1,0:T(8,128)(2,1)S(1)} %update.5.a), channel_id=1, source_target_pairs={{0,3},{1,0},{2,1},{3,2},{4,7},{5,4},{6,5},{7,6},{8,11},{9,8},{10,9... | collective-permute-start | bytes 165896 | tf_op jit(solution)/shard_map/while/body/eval_jaxpr/ppermute | solution.py:261
  156.5 14.4 %all-to-all-start = ((f32[32,1,1152]{2,1,0:T(1,128)}), f32[32,1,1152]{2,1,0:T(1,128)S(1)}, u32[]{:S(2)}, u32[]{:S(2)}) async-start(f32[32,1,1152]{2,1,0:T(1,128)} %bitcast.22), calls=%async_computation | async-start | bytes 294912 | tf_op jit(solution)/shard_map/while/body/eval_jaxpr/all_to_all | solution.py:267
  171.5 13.9 %all-to-all-start.1 = ((f32[32,1,1152]{2,1,0:T(1,128)}), f32[32,1,1152]{2,1,0:T(1,128)S(1)}, u32[]{:S(2)}, u32[]{:S(2)}) async-start(f32[32,1,1152]{2,1,0:T(1,128)} %bitcast.24), calls=%async_computation.1 | async-start | bytes 294912 | tf_op jit(solution)/shard_map/while/body/eval_jaxpr/all_to_all | solution.py:267
  189.6 7.0 %collective-permute-start.4 = (bf16[72,384]{1,0:T(8,128)(2,1)S(1)}, bf16[72,384]{1,0:T(8,128)(2,1)S(1)}, u32[]{:S(2)}, u32[]{:S(2)}) collective-permute-start(bf16[72,384]{1,0:T(8,128)(2,1)S(1)} %update.5.a), channel_id=1, source_target_pairs={{0,3},{1,0},{2,1},{3,2},{4,7},{5,4},{6,5},{7,6},{8,11},{9,8},{10,9... | collective-permute-start | bytes 165896 | tf_op jit(solution)/shard_map/while/body/eval_jaxpr/ppermute | solution.py:261
  192.2 5.2 %collective-permute-start.3 = (bf16[72,384]{1,0:T(8,128)(2,1)S(1)}, bf16[72,384]{1,0:T(8,128)(2,1)S(1)}, u32[]{:S(2)}, u32[]{:S(2)}) collective-permute-start(bf16[72,384]{1,0:T(8,128)(2,1)S(1)} %update.5.a), channel_id=1, source_target_pairs={{0,1},{1,2},{2,3},{3,0},{4,5},{5,6},{6,7},{7,4},{8,9},{9,10},{10,1... | collective-permute-start | bytes 165896 | tf_op jit(solution)/shard_map/while/body/eval_jaxpr/ppermute | solution.py:261
  192.2 5.2 %collective-permute-start.2 = (bf16[72,384]{1,0:T(8,128)(2,1)S(1)}, bf16[72,384]{1,0:T(8,128)(2,1)S(1)}, u32[]{:S(2)}, u32[]{:S(2)}) collective-permute-start(bf16[72,384]{1,0:T(8,128)(2,1)S(1)} %update.5.a), channel_id=1, source_target_pairs={{0,2},{1,3},{2,0},{3,1},{4,6},{5,7},{6,4},{7,5},{8,10},{9,11},{10,... | collective-permute-start | bytes 165896 | tf_op jit(solution)/shard_map/while/body/eval_jaxpr/ppermute | solution.py:261
  201.4 14.4 %all-to-all-start = ((f32[32,1,1152]{2,1,0:T(1,128)}), f32[32,1,1152]{2,1,0:T(1,128)S(1)}, u32[]{:S(2)}, u32[]{:S(2)}) async-start(f32[32,1,1152]{2,1,0:T(1,128)} %bitcast.22), calls=%async_computation | async-start | bytes 294912 | tf_op jit(solution)/shard_map/while/body/eval_jaxpr/all_to_all | solution.py:267
  216.4 13.9 %all-to-all-start.1 = ((f32[32,1,1152]{2,1,0:T(1,128)}), f32[32,1,1152]{2,1,0:T(1,128)S(1)}, u32[]{:S(2)}, u32[]{:S(2)}) async-start(f32[32,1,1152]{2,1,0:T(1,128)} %bitcast.24), calls=%async_computation.1 | async-start | bytes 294912 | tf_op jit(solution)/shard_map/while/body/eval_jaxpr/all_to_all | solution.py:267
  234.4 7.0 %collective-permute-start.4 = (bf16[72,384]{1,0:T(8,128)(2,1)S(1)}, bf16[72,384]{1,0:T(8,128)(2,1)S(1)}, u32[]{:S(2)}, u32[]{:S(2)}) collective-permute-start(bf16[72,384]{1,0:T(8,128)(2,1)S(1)} %update.5.a), channel_id=1, source_target_pairs={{0,3},{1,0},{2,1},{3,2},{4,7},{5,4},{6,5},{7,6},{8,11},{9,8},{10,9... | collective-permute-start | bytes 165896 | tf_op jit(solution)/shard_map/while/body/eval_jaxpr/ppermute | solution.py:261
  246.2 14.4 %all-to-all-start = ((f32[32,1,1152]{2,1,0:T(1,128)}), f32[32,1,1152]{2,1,0:T(1,128)S(1)}, u32[]{:S(2)}, u32[]{:S(2)}) async-start(f32[32,1,1152]{2,1,0:T(1,128)} %bitcast.22), calls=%async_computation | async-start | bytes 294912 | tf_op jit(solution)/shard_map/while/body/eval_jaxpr/all_to_all | solution.py:267
  261.3 13.9 %all-to-all-start.1 = ((f32[32,1,1152]{2,1,0:T(1,128)}), f32[32,1,1152]{2,1,0:T(1,128)S(1)}, u32[]{:S(2)}, u32[]{:S(2)}) async-start(f32[32,1,1152]{2,1,0:T(1,128)} %bitcast.24), calls=%async_computation.1 | async-start | bytes 294912 | tf_op jit(solution)/shard_map/while/body/eval_jaxpr/all_to_all | solution.py:267
  279.3 7.0 %collective-permute-start.4 = (bf16[72,384]{1,0:T(8,128)(2,1)S(1)}, bf16[72,384]{1,0:T(8,128)(2,1)S(1)}, u32[]{:S(2)}, u32[]{:S(2)}) collective-permute-start(bf16[72,384]{1,0:T(8,128)(2,1)S(1)} %update.5.a), channel_id=1, source_target_pairs={{0,3},{1,0},{2,1},{3,2},{4,7},{5,4},{6,5},{7,6},{8,11},{9,8},{10,9... | collective-permute-start | bytes 165896 | tf_op jit(solution)/shard_map/while/body/eval_jaxpr/ppermute | solution.py:261
  322.4 7.0 %collective-permute-start.17 = (bf16[72,384]{1,0:T(8,128)(2,1)S(1)}, bf16[72,384]{1,0:T(8,128)(2,1)S(1)}, u32[]{:S(2)}, u32[]{:S(2)}) collective-permute-start(bf16[72,384]{1,0:T(8,128)(2,1)S(1)} %update.4.a), channel_id=1, source_target_pairs={{0,3},{1,0},{2,1},{3,2},{4,7},{5,4},{6,5},{7,6},{8,11},{9,8},{10,9... | collective-permute-start | bytes 165896 | tf_op jit(solution)/shard_map/ppermute | solution.py:261
  (33 other events, 148.4 us)

commit v2 on v1

--- a/solution.py
+++ b/solution.py
@@ -96,13 +96,27 @@
     out_ref[...] = a[...] + b[...]
 
 
-def stepped_from(parts, previous, inverse, batch):
+def stepped_from(parts, previous, inverse, batch, left=0.0):
     comps, genes = previous.shape
-    total = sum(part[:comps, :genes].astype(f32) for part in parts)
+    total = sum(part[:comps, :genes].astype(f32) for part in parts) + left
     stepped = previous + STEP_RATE * (total * (1.0 / batch))
     if inverse is not None:
         stepped = lax.dot_general(inverse, stepped, NN, precision=HIGH, preferred_element_type=f32)
     return stepped
+
+
+def pair_rows(part, start, genes):
+    return part[start : start + 1, :genes].astype(f32) + part[start + 1 : start + 2, :genes].astype(f32)
+
+
+def between_groups(parts, comps, genes, batch):
+    sums = [pair_rows(part, comps + 2, genes) for part in parts]
+    mean = sum(sums) * (1.0 / batch)
+    total = jnp.zeros((comps, genes), f32)
+    for part, own in zip(parts, sums):
+        totals = part[:comps, genes : genes + 1].astype(f32) + part[:comps, genes + 1 : genes + 2].astype(f32)
+        total = total + totals * (own * (len(parts) / batch) - mean)
+    return total
 
 
 def make_middle(batch, normalised):
@@ -111,10 +125,10 @@
         tile_ref, keep_ref, send_ref, stepped_ref, mean_ref = refs[-5:]
         comps, genes = previous_ref.shape
         parts = (a, b, c, d)
-        stepped = stepped_from(parts, previous_ref[...], inverse, batch)
+        left = 0.0 if normalised else between_groups(parts, comps, genes, batch)
+        stepped = stepped_from(parts, previous_ref[...], inverse, batch, left)
         stepped_ref[...] = stepped
-        sums = sum(part[comps : comps + 2, :genes].astype(f32) for part in parts)
-        mean = (sums[:1] + sums[1:]) * (1.0 / batch)
+        mean = sum(pair_rows(part, comps, genes) for part in parts) * (1.0 / batch)
         mean_ref[...] = mean
         shift = jnp.sum(stepped * mean, axis=1, keepdims=True)
         pack_partial(stepped, tile_ref[...], shift, core_ref[0] == 0, keep_ref, send_ref)
@@ -142,7 +156,7 @@
     return kernel
 
 
-def make_update(half, rows):
+def make_update(half, rows, cells=None):
     def kernel(core_ref, mine_ref, other_ref, tile_ref, mean_ref, next_ref, out_ref):
         genes = tile_ref.shape[1]
         comps = 2 * half
@@ -158,12 +172,23 @@
         scores = jnp.concatenate(chunks, axis=1)
         both = lax.dot_general(split_pair(scores), tile_ref[...], NN, preferred_element_type=f32)
         totals = jnp.sum(scores, axis=1, keepdims=True)
-        raw = both[:comps] + both[comps:] - totals * mean_ref[...]
-        rest = out_ref.shape[0] - comps - 2
+        mean = mean_ref[...] * (1.0 / cells) if cells else mean_ref[...]
+        raw = both[:comps] + both[comps:] - totals * mean
+        rest = out_ref.shape[0] - comps - 4
         tall = jnp.concatenate(
-            [raw.astype(bf16), split_pair(next_ref[...]), jnp.zeros((rest, genes), bf16)], axis=0
+            [
+                raw.astype(bf16),
+                split_pair(next_ref[...]),
+                split_pair(mean_ref[...]),
+                jnp.zeros((rest, genes), bf16),
+            ],
+            axis=0,
         )
-        out_ref[...] = jnp.concatenate([tall, jnp.zeros((tall.shape[0], width - genes), bf16)], axis=1)
+        high = totals.astype(bf16)
+        low = (totals - high.astype(f32)).astype(bf16)
+        side = jnp.concatenate([high, low, jnp.zeros((comps, width - genes - 2), bf16)], axis=1)
+        side = jnp.concatenate([side, jnp.zeros((tall.shape[0] - comps, width - genes), bf16)], axis=0)
+        out_ref[...] = jnp.concatenate([tall, side], axis=1)
 
     return kernel
 
@@ -247,8 +272,8 @@
     pool_by_cell = pool_counts.T
     same_core = [[2 * chip + which for chip in range(chips)] for which in range(2)]
 
-    def tile_of(step):
-        return jnp.take(pool_by_cell, chosen[step], axis=0, mode="clip")
+    def tile_of(picks):
+        return jnp.take(pool_by_cell, picks, axis=0, mode="clip")
 
     def sums_of(tile):
         return jnp.sum(tile, axis=0, dtype=f32, keepdims=True)
@@ -259,7 +284,7 @@
     def round_cells(value):
         return [value] + [
             lax.ppermute(value, "cell", [(i, (i + k) % cell_devices) for i in range(cell_devices)])
-            for k in (2, 1, 3)
+            for k in range(1, cell_devices)
         ]
 
     def exchange(value):
@@ -273,8 +298,7 @@
     row = jax.ShapeDtypeStruct((1, genes), f32)
     shared = jax.ShapeDtypeStruct((comps + 8, width), bf16)
 
-    tile = tile_of(0)
-    mean = sum(round_cells(sums_of(tile))) * (1.0 / batch)
+    tile = tile_of(chosen[0])
     chunk = local_pool // 8
     keep, send = vmem_call(
         first_kernel,
@@ -291,8 +315,8 @@
         mine = exchange(copies)
         return mine, swap_cores(mine)
 
-    def change_of(mine, other, tile, mean, next_sums):
-        change = vmem_call(make_update(half, rows), shared, 5, name="update")(
+    def change_of(mine, other, tile, mean, next_sums, own=None):
+        change = vmem_call(make_update(half, rows, own), shared, 5, name="update")(
             core, mine, other, tile, mean, next_sums
         )
         return round_cells(change)
@@ -306,19 +330,24 @@
             make_middle(batch, bool(inverse)), (packed, packed, local, row), len(inputs), name="middle"
         )(core, *inputs)
 
-    def one_step(step, state):
-        keep, send, stepped, mean, tile = state
-        next_tile = tile_of(step + 1)
+    def one_step(state):
+        step, keep, send, stepped, mean, tile = state
+        following = step + 1
+        picks = lax.dynamic_index_in_dim(chosen, following, keepdims=False)
+        following, picks, send = lax.optimization_barrier((following, picks, send))
+        next_tile = tile_of(picks)
         mine, other = scores_of(keep, send)
         parts = change_of(mine, other, tile, mean, sums_of(next_tile))
         inverse = (factor_of(mine, other),)
-        return (*advance(parts, stepped, inverse, next_tile), next_tile)
-
-    next_tile = tile_of(1)
+        return (following, *advance(parts, stepped, inverse, next_tile), next_tile)
+
+    next_tile = tile_of(chosen[1])
     mine, other = scores_of(keep, send)
-    parts = change_of(mine, other, tile, mean, sums_of(next_tile))
+    parts = change_of(mine, other, tile, sums_of(tile), sums_of(next_tile), cells)
     state = (*advance(parts, loadings_init, (), next_tile), next_tile)
-    keep, send, stepped, mean, tile = lax.fori_loop(1, steps - 1, one_step, state)
+    _, keep, send, stepped, mean, tile = lax.while_loop(
+        lambda state: state[0] < steps - 1, one_step, (jnp.int32(1), *state)
+    )
     mine, other = scores_of(keep, send)
     parts = change_of(mine, other, tile, mean, mean)
     inverse = factor_of(mine, other)

time: 356 us -> 343 us (0.963)
  blocking collectives: 38.2 us -> 109 us
  waiting for transfers between devices: 89.5 us -> 47.8 us
  starting transfers between devices: 135 us -> 95.5 us
    all_to_all x2 -> x7, blocking collectives: 27.9 us -> 99 us  [exchange(): lax.all_to_all(pieces, 'gene', 0, 0, tiled=True, axis_index_groups=same_c...]
    all_to_all x12 -> x7, waiting for transfers between devices: 64.2 us -> 18.4 us  [exchange(): lax.all_to_all(pieces, 'gene', 0, 0, tiled=True, axis_index_groups=same_c...]
    all_to_all x12 -> x7, starting transfers between devices: 68 us -> 41.9 us  [exchange(): lax.all_to_all(pieces, 'gene', 0, 0, tiled=True, axis_index_groups=same_c...]
    ppermute x24 -> x21, starting transfers between devices: 30.3 us -> 17.7 us  [round_cells(): lax.ppermute(value, 'cell', [(i, (i + k) % cell_devices) for i in range(c...]
    ppermute x24 -> x21, waiting for transfers between devices: 8.16 us -> 11.5 us  [round_cells(): lax.ppermute(value, 'cell', [(i, (i + k) % cell_devices) for i in range(c...]
  transfers between devices with their start and end apart: 54 -> 46, of which waited for: 37 -> 38; matrix products, arithmetic and copies ran while one was open for 13% -> 14% of each run, Pallas kernels for 5% -> 5%
where the time goes in v2:
time: 343 us; the launch traced here: 342 us
  blocking collectives  109 us (32%)
  starting transfers between devices  95.5 us (28%)
  local copies, waits for them, and re-layouts  48.5 us (14%)
  waiting for transfers between devices  47.8 us (14%)
  Pallas kernels  38.1 us (11%)
    all_to_all x7, blocking collectives, exchange(): lax.all_to_all(pieces, 'gene', 0, 0, tiled=True, axis_index_groups=same_c...  99 us
    gather x7, local copies, waits for them, and re-layouts, tile_of(): return jnp.take(pool_by_cell, picks, axis=0, mode='clip')  42.5 us
    all_to_all x7, starting transfers between devices, exchange(): lax.all_to_all(pieces, 'gene', 0, 0, tiled=True, axis_index_groups=same_c...  41.9 us
    pallas_call x36, Pallas kernels, run(): return call(*args[:core], *near, *args[last:])  38.1 us
    ppermute x15, starting transfers between devices, swap_cores(): lax.ppermute(value, 'gene', [(i, i ^ 1) for i in range(gene_devices)])  33.7 us
    all_to_all x7, waiting for transfers between devices, exchange(): lax.all_to_all(pieces, 'gene', 0, 0, tiled=True, axis_index_groups=same_c...  18.4 us
    ppermute x21, starting transfers between devices, round_cells(): lax.ppermute(value, 'cell', [(i, (i + k) % cell_devices) for i in range(c...  17.7 us
    ppermute x15, waiting for transfers between devices, swap_cores(): lax.ppermute(value, 'gene', [(i, i ^ 1) for i in range(gene_devices)])  13.9 us
  transfers between devices with their start and end apart: 46, of which 38 were waited for; matrix products, arithmetic and copies ran while one was open for 14% of the time, Pallas kernels for 5%

profile of v2, /device:TPU:1, one launch (start us, length us, event | category | flops | bytes accessed | tf_op | source)
XLA Modules:
  0.0 341.9 jit_solution(4457079673661824578)
XLA Ops:
  1.7 4.6 %first.1 = (f32[288,128]{1,0:T(8,128)S(1)}, f32[288,128]{1,0:T(8,128)S(1)}) custom-call(s32[1]{0:T(128)} %bitcast.5.core_ref, f32[64,320]{1,0:T(8,128)S(1)} %copy-done, s32[1,1024]{1,0:T(1,128)S(1)} %get-tuple-element.170.picks_ref, bf16[320,4096]{1,0:T(8,128)(2,1)} %pool_ref.1), custom_call_target="tpu_custom_call" | custom-call | tf_op jit(solution)/shard_map/first/pallas_call | solution.py:35
  11.2 9.3 %all-to-all-start.2 = ((f32[32,1,1152]{2,1,0:T(1,128)}), f32[32,1,1152]{2,1,0:T(1,128)S(1)}, u32[]{:S(2)}, u32[]{:S(2)}) async-start(f32[32,1,1152]{2,1,0:T(1,128)} %bitcast.6), calls=%async_computation.2 | async-start | bytes 294912 | tf_op jit(solution)/shard_map/all_to_all | solution.py:292
  25.1 6.1 %gather_fusion.2 = bf16[1024,320]{1,0:T(8,128)(2,1)S(1)} fusion(bf16[4096,320]{1,0:T(8,128)(2,1)} %bitcast.42, s32[1024]{0:T(1024)S(1)} %broadcast_clamp_fusion.1), kind=kCustom, calls=%fused_computation.2 | custom fusion | bytes 1314816 | tf_op jit(solution)/shard_map/jit(_take)/gather | solution.py:276
  31.9 9.2 %all-to-all-start.3 = ((f32[32,1,1152]{2,1,0:T(1,128)}), f32[32,1,1152]{2,1,0:T(1,128)S(1)}, u32[]{:S(2)}, u32[]{:S(2)}) async-start(f32[32,1,1152]{2,1,0:T(1,128)} %bitcast.8), calls=%async_computation.3 | async-start | bytes 294912 | tf_op jit(solution)/shard_map/all_to_all | solution.py:292
  41.3 6.1 %gather_fusion.1 = bf16[1024,320]{1,0:T(8,128)(2,1)S(1)} fusion(bf16[4096,320]{1,0:T(8,128)(2,1)} %bitcast.43, s32[1024]{0:T(1024)S(1)} %broadcast_clamp_fusion.2), kind=kCustom, calls=%fused_computation.1 | custom fusion | bytes 1314816 | tf_op jit(solution)/shard_map/jit(_take)/gather | solution.py:276
  63.0 214.2 %while.20 = (s32[]{:T(128)}, f32[288,128]{1,0:T(8,128)S(1)}, f32[288,128]{1,0:T(8,128)S(1)}, f32[64,320]{1,0:T(8,128)S(1)}, f32[1,320]{1,0:T(1,128)S(1)}, /*inde...) while((s32[]{:T(128)}, f32[288,128]{1,0:T(8,128)S(1)}, ...), condition=%wide.region_4.5_spmd, body=%wide.region_2.4_spmd.sunk | while | flops 1000656064 | bytes 6045827 | solution.py:348
  65.6 14.5 %all_to_all.46 = f32[32,1,1152]{2,1,0:T(1,128)S(1)} all-to-all(f32[32,1,1152]{2,1,0:T(1,128)S(1)} %bitcast.30), channel_id=1, replica_groups={{0,8,16,24,32,40,48,56,64,72,80,88,96,104,112,120,128,136,144,152,160,1..., dimensions={0} | all-to-all | bytes 294912 | tf_op jit(solution)/shard_map/while/body/all_to_all | solution.py:292
  80.8 4.7 %all-to-all-start.1 = ((f32[32,1,1152]{2,1,0:T(1,128)}), f32[32,1,1152]{2,1,0:T(1,128)S(1)}, u32[]{:S(2)}, u32[]{:S(2)}) async-start(f32[32,1,1152]{2,1,0:T(1,128)} %bitcast.25), calls=%async_computation.1 | async-start | bytes 294912 | tf_op jit(solution)/shard_map/while/body/all_to_all | solution.py:292
  85.5 6.1 %gather_fusion = bf16[1024,320]{1,0:T(8,128)(2,1)S(1)} fusion(bf16[4096,320]{1,0:T(8,128)(2,1)} %get-tuple-element.271, s32[1024]{0:T(1024)S(1)} %broadcast_clamp_fusion.4), kind=kCustom, calls=%fused_computation.clone.1 | custom fusion | bytes 1314816 | tf_op jit(solution)/shard_map/while/body/jit(_take)/gather | solution.py:276
  108.0 14.2 %all_to_all.46 = f32[32,1,1152]{2,1,0:T(1,128)S(1)} all-to-all(f32[32,1,1152]{2,1,0:T(1,128)S(1)} %bitcast.30), channel_id=1, replica_groups={{0,8,16,24,32,40,48,56,64,72,80,88,96,104,112,120,128,136,144,152,160,1..., dimensions={0} | all-to-all | bytes 294912 | tf_op jit(solution)/shard_map/while/body/all_to_all | solution.py:292
  122.8 4.7 %all-to-all-start.1 = ((f32[32,1,1152]{2,1,0:T(1,128)}), f32[32,1,1152]{2,1,0:T(1,128)S(1)}, u32[]{:S(2)}, u32[]{:S(2)}) async-start(f32[32,1,1152]{2,1,0:T(1,128)} %bitcast.25), calls=%async_computation.1 | async-start | bytes 294912 | tf_op jit(solution)/shard_map/while/body/all_to_all | solution.py:292
  127.5 6.1 %gather_fusion = bf16[1024,320]{1,0:T(8,128)(2,1)S(1)} fusion(bf16[4096,320]{1,0:T(8,128)(2,1)} %get-tuple-element.271, s32[1024]{0:T(1024)S(1)} %broadcast_clamp_fusion.4), kind=kCustom, calls=%fused_computation.clone.1 | custom fusion | bytes 1314816 | tf_op jit(solution)/shard_map/while/body/jit(_take)/gather | solution.py:276
  151.4 14.2 %all_to_all.46 = f32[32,1,1152]{2,1,0:T(1,128)S(1)} all-to-all(f32[32,1,1152]{2,1,0:T(1,128)S(1)} %bitcast.30), channel_id=1, replica_groups={{0,8,16,24,32,40,48,56,64,72,80,88,96,104,112,120,128,136,144,152,160,1..., dimensions={0} | all-to-all | bytes 294912 | tf_op jit(solution)/shard_map/while/body/all_to_all | solution.py:292
  166.3 4.7 %all-to-all-start.1 = ((f32[32,1,1152]{2,1,0:T(1,128)}), f32[32,1,1152]{2,1,0:T(1,128)S(1)}, u32[]{:S(2)}, u32[]{:S(2)}) async-start(f32[32,1,1152]{2,1,0:T(1,128)} %bitcast.25), calls=%async_computation.1 | async-start | bytes 294912 | tf_op jit(solution)/shard_map/while/body/all_to_all | solution.py:292
  171.0 6.1 %gather_fusion = bf16[1024,320]{1,0:T(8,128)(2,1)S(1)} fusion(bf16[4096,320]{1,0:T(8,128)(2,1)} %get-tuple-element.271, s32[1024]{0:T(1024)S(1)} %broadcast_clamp_fusion.4), kind=kCustom, calls=%fused_computation.clone.1 | custom fusion | bytes 1314816 | tf_op jit(solution)/shard_map/while/body/jit(_take)/gather | solution.py:276
  194.3 14.2 %all_to_all.46 = f32[32,1,1152]{2,1,0:T(1,128)S(1)} all-to-all(f32[32,1,1152]{2,1,0:T(1,128)S(1)} %bitcast.30), channel_id=1, replica_groups={{0,8,16,24,32,40,48,56,64,72,80,88,96,104,112,120,128,136,144,152,160,1..., dimensions={0} | all-to-all | bytes 294912 | tf_op jit(solution)/shard_map/while/body/all_to_all | solution.py:292
  209.1 4.7 %all-to-all-start.1 = ((f32[32,1,1152]{2,1,0:T(1,128)}), f32[32,1,1152]{2,1,0:T(1,128)S(1)}, u32[]{:S(2)}, u32[]{:S(2)}) async-start(f32[32,1,1152]{2,1,0:T(1,128)} %bitcast.25), calls=%async_computation.1 | async-start | bytes 294912 | tf_op jit(solution)/shard_map/while/body/all_to_all | solution.py:292
  213.8 6.1 %gather_fusion = bf16[1024,320]{1,0:T(8,128)(2,1)S(1)} fusion(bf16[4096,320]{1,0:T(8,128)(2,1)} %get-tuple-element.271, s32[1024]{0:T(1024)S(1)} %broadcast_clamp_fusion.4), kind=kCustom, calls=%fused_computation.clone.1 | custom fusion | bytes 1314816 | tf_op jit(solution)/shard_map/while/body/jit(_take)/gather | solution.py:276
  237.1 14.2 %all_to_all.46 = f32[32,1,1152]{2,1,0:T(1,128)S(1)} all-to-all(f32[32,1,1152]{2,1,0:T(1,128)S(1)} %bitcast.30), channel_id=1, replica_groups={{0,8,16,24,32,40,48,56,64,72,80,88,96,104,112,120,128,136,144,152,160,1..., dimensions={0} | all-to-all | bytes 294912 | tf_op jit(solution)/shard_map/while/body/all_to_all | solution.py:292
  251.9 4.7 %all-to-all-start.1 = ((f32[32,1,1152]{2,1,0:T(1,128)}), f32[32,1,1152]{2,1,0:T(1,128)S(1)}, u32[]{:S(2)}, u32[]{:S(2)}) async-start(f32[32,1,1152]{2,1,0:T(1,128)} %bitcast.25), calls=%async_computation.1 | async-start | bytes 294912 | tf_op jit(solution)/shard_map/while/body/all_to_all | solution.py:292
  256.6 6.1 %gather_fusion = bf16[1024,320]{1,0:T(8,128)(2,1)S(1)} fusion(bf16[4096,320]{1,0:T(8,128)(2,1)} %get-tuple-element.271, s32[1024]{0:T(1024)S(1)} %broadcast_clamp_fusion.4), kind=kCustom, calls=%fused_computation.clone.1 | custom fusion | bytes 1314816 | tf_op jit(solution)/shard_map/while/body/jit(_take)/gather | solution.py:276
  280.0 14.2 %all_to_all.43 = f32[32,1,1152]{2,1,0:T(1,128)S(1)} all-to-all(f32[32,1,1152]{2,1,0:T(1,128)S(1)} %bitcast.37), channel_id=1, replica_groups={{0,8,16,24,32,40,48,56,64,72,80,88,96,104,112,120,128,136,144,152,160,1..., dimensions={0} | all-to-all | bytes 294912 | tf_op jit(solution)/shard_map/all_to_all | solution.py:292
  294.2 13.7 %all_to_all.44 = f32[32,1,1152]{2,1,0:T(1,128)S(1)} all-to-all(f32[32,1,1152]{2,1,0:T(1,128)S(1)} %bitcast.40), channel_id=1, replica_groups={{0,8,16,24,32,40,48,56,64,72,80,88,96,104,112,120,128,136,144,152,160,1..., dimensions={0} | all-to-all | bytes 294912 | tf_op jit(solution)/shard_map/all_to_all | solution.py:292
  327.7 10.3 %all_to_all.45.in_ref = f32[8,32,128]{2,1,0:T(8,128)S(1)} all-to-all(f32[8,32,128]{2,1,0:T(8,128)S(1)} %broadcast_in_dim.33), channel_id=1, replica_groups={{0,8,16,24,32,40,48,56},{4,12,20,28,36,44,52,60},{64,72,80,88,96,104,11..., dimensions={0} | all-to-all | bytes 262144 | tf_op jit(solution)/shard_map/all_to_all | solution.py:376
  (166 shorter events, 143.0 us)
Async XLA Ops:
  11.2 20.0 %all-to-all-start.2 = ((f32[32,1,1152]{2,1,0:T(1,128)}), f32[32,1,1152]{2,1,0:T(1,128)S(1)}, u32[]{:S(2)}, u32[]{:S(2)}) async-start(f32[32,1,1152]{2,1,0:T(1,128)} %bitcast.6), calls=%async_computation.2 | async-start | bytes 294912 | tf_op jit(solution)/shard_map/all_to_all | solution.py:292
  31.9 18.4 %all-to-all-start.3 = ((f32[32,1,1152]{2,1,0:T(1,128)}), f32[32,1,1152]{2,1,0:T(1,128)S(1)}, u32[]{:S(2)}, u32[]{:S(2)}) async-start(f32[32,1,1152]{2,1,0:T(1,128)} %bitcast.8), calls=%async_computation.3 | async-start | bytes 294912 | tf_op jit(solution)/shard_map/all_to_all | solution.py:292
  56.9 4.6 %collective-permute-start.8 = (bf16[72,384]{1,0:T(8,128)(2,1)S(1)}, bf16[72,384]{1,0:T(8,128)(2,1)S(1)}, u32[]{:S(2)}, u32[]{:S(2)}) collective-permute-start(bf16[72,384]{1,0:T(8,128)(2,1)S(1)} %update.3.a), channel_id=1, source_target_pairs={{0,2},{1,3},{2,0},{3,1},{4,6},{5,7},{6,4},{7,5},{8,10},{9,11},{10,... | collective-permute-start | bytes 165896 | tf_op jit(solution)/shard_map/ppermute | solution.py:286
  57.2 5.1 %collective-permute-start.7 = (bf16[72,384]{1,0:T(8,128)(2,1)S(1)}, bf16[72,384]{1,0:T(8,128)(2,1)S(1)}, u32[]{:S(2)}, u32[]{:S(2)}) collective-permute-start(bf16[72,384]{1,0:T(8,128)(2,1)S(1)} %update.3.a), channel_id=1, source_target_pairs={{0,1},{1,2},{2,3},{3,0},{4,5},{5,6},{6,7},{7,4},{8,9},{9,10},{10,1... | collective-permute-start | bytes 165896 | tf_op jit(solution)/shard_map/ppermute | solution.py:286
  80.8 13.9 %all-to-all-start.1 = ((f32[32,1,1152]{2,1,0:T(1,128)}), f32[32,1,1152]{2,1,0:T(1,128)S(1)}, u32[]{:S(2)}, u32[]{:S(2)}) async-start(f32[32,1,1152]{2,1,0:T(1,128)} %bitcast.25), calls=%async_computation.1 | async-start | bytes 294912 | tf_op jit(solution)/shard_map/while/body/all_to_all | solution.py:292
  98.8 5.1 %collective-permute-start.4 = (bf16[72,384]{1,0:T(8,128)(2,1)S(1)}, bf16[72,384]{1,0:T(8,128)(2,1)S(1)}, u32[]{:S(2)}, u32[]{:S(2)}) collective-permute-start(bf16[72,384]{1,0:T(8,128)(2,1)S(1)} %update.5.a), channel_id=1, source_target_pairs={{0,3},{1,0},{2,1},{3,2},{4,7},{5,4},{6,5},{7,6},{8,11},{9,8},{10,9... | collective-permute-start | bytes 165896 | tf_op jit(solution)/shard_map/while/body/ppermute | solution.py:286
  99.1 4.8 %collective-permute-start.3 = (bf16[72,384]{1,0:T(8,128)(2,1)S(1)}, bf16[72,384]{1,0:T(8,128)(2,1)S(1)}, u32[]{:S(2)}, u32[]{:S(2)}) collective-permute-start(bf16[72,384]{1,0:T(8,128)(2,1)S(1)} %update.5.a), channel_id=1, source_target_pairs={{0,2},{1,3},{2,0},{3,1},{4,6},{5,7},{6,4},{7,5},{8,10},{9,11},{10,... | collective-permute-start | bytes 165896 | tf_op jit(solution)/shard_map/while/body/ppermute | solution.py:286
  100.0 4.5 %collective-permute-start.2 = (bf16[72,384]{1,0:T(8,128)(2,1)S(1)}, bf16[72,384]{1,0:T(8,128)(2,1)S(1)}, u32[]{:S(2)}, u32[]{:S(2)}) collective-permute-start(bf16[72,384]{1,0:T(8,128)(2,1)S(1)} %update.5.a), channel_id=1, source_target_pairs={{0,1},{1,2},{2,3},{3,0},{4,5},{5,6},{6,7},{7,4},{8,9},{9,10},{10,1... | collective-permute-start | bytes 165896 | tf_op jit(solution)/shard_map/while/body/ppermute | solution.py:286
  122.8 13.9 %all-to-all-start.1 = ((f32[32,1,1152]{2,1,0:T(1,128)}), f32[32,1,1152]{2,1,0:T(1,128)S(1)}, u32[]{:S(2)}, u32[]{:S(2)}) async-start(f32[32,1,1152]{2,1,0:T(1,128)} %bitcast.25), calls=%async_computation.1 | async-start | bytes 294912 | tf_op jit(solution)/shard_map/while/body/all_to_all | solution.py:292
  140.8 6.2 %collective-permute-start.4 = (bf16[72,384]{1,0:T(8,128)(2,1)S(1)}, bf16[72,384]{1,0:T(8,128)(2,1)S(1)}, u32[]{:S(2)}, u32[]{:S(2)}) collective-permute-start(bf16[72,384]{1,0:T(8,128)(2,1)S(1)} %update.5.a), channel_id=1, source_target_pairs={{0,3},{1,0},{2,1},{3,2},{4,7},{5,4},{6,5},{7,6},{8,11},{9,8},{10,9... | collective-permute-start | bytes 165896 | tf_op jit(solution)/shard_map/while/body/ppermute | solution.py:286
  142.6 4.5 %collective-permute-start.3 = (bf16[72,384]{1,0:T(8,128)(2,1)S(1)}, bf16[72,384]{1,0:T(8,128)(2,1)S(1)}, u32[]{:S(2)}, u32[]{:S(2)}) collective-permute-start(bf16[72,384]{1,0:T(8,128)(2,1)S(1)} %update.5.a), channel_id=1, source_target_pairs={{0,2},{1,3},{2,0},{3,1},{4,6},{5,7},{6,4},{7,5},{8,10},{9,11},{10,... | collective-permute-start | bytes 165896 | tf_op jit(solution)/shard_map/while/body/ppermute | solution.py:286
  143.2 4.9 %collective-permute-start.2 = (bf16[72,384]{1,0:T(8,128)(2,1)S(1)}, bf16[72,384]{1,0:T(8,128)(2,1)S(1)}, u32[]{:S(2)}, u32[]{:S(2)}) collective-permute-start(bf16[72,384]{1,0:T(8,128)(2,1)S(1)} %update.5.a), channel_id=1, source_target_pairs={{0,1},{1,2},{2,3},{3,0},{4,5},{5,6},{6,7},{7,4},{8,9},{9,10},{10,1... | collective-permute-start | bytes 165896 | tf_op jit(solution)/shard_map/while/body/ppermute | solution.py:286
  166.3 13.9 %all-to-all-start.1 = ((f32[32,1,1152]{2,1,0:T(1,128)}), f32[32,1,1152]{2,1,0:T(1,128)S(1)}, u32[]{:S(2)}, u32[]{:S(2)}) async-start(f32[32,1,1152]{2,1,0:T(1,128)} %bitcast.25), calls=%async_computation.1 | async-start | bytes 294912 | tf_op jit(solution)/shard_map/while/body/all_to_all | solution.py:292
  184.3 5.1 %collective-permute-start.4 = (bf16[72,384]{1,0:T(8,128)(2,1)S(1)}, bf16[72,384]{1,0:T(8,128)(2,1)S(1)}, u32[]{:S(2)}, u32[]{:S(2)}) collective-permute-start(bf16[72,384]{1,0:T(8,128)(2,1)S(1)} %update.5.a), channel_id=1, source_target_pairs={{0,3},{1,0},{2,1},{3,2},{4,7},{5,4},{6,5},{7,6},{8,11},{9,8},{10,9... | collective-permute-start | bytes 165896 | tf_op jit(solution)/shard_map/while/body/ppermute | solution.py:286
  186.2 5.1 %collective-permute-start.2 = (bf16[72,384]{1,0:T(8,128)(2,1)S(1)}, bf16[72,384]{1,0:T(8,128)(2,1)S(1)}, u32[]{:S(2)}, u32[]{:S(2)}) collective-permute-start(bf16[72,384]{1,0:T(8,128)(2,1)S(1)} %update.5.a), channel_id=1, source_target_pairs={{0,1},{1,2},{2,3},{3,0},{4,5},{5,6},{6,7},{7,4},{8,9},{9,10},{10,1... | collective-permute-start | bytes 165896 | tf_op jit(solution)/shard_map/while/body/ppermute | solution.py:286
  209.1 13.9 %all-to-all-start.1 = ((f32[32,1,1152]{2,1,0:T(1,128)}), f32[32,1,1152]{2,1,0:T(1,128)S(1)}, u32[]{:S(2)}, u32[]{:S(2)}) async-start(f32[32,1,1152]{2,1,0:T(1,128)} %bitcast.25), calls=%async_computation.1 | async-start | bytes 294912 | tf_op jit(solution)/shard_map/while/body/all_to_all | solution.py:292
  227.2 5.3 %collective-permute-start.4 = (bf16[72,384]{1,0:T(8,128)(2,1)S(1)}, bf16[72,384]{1,0:T(8,128)(2,1)S(1)}, u32[]{:S(2)}, u32[]{:S(2)}) collective-permute-start(bf16[72,384]{1,0:T(8,128)(2,1)S(1)} %update.5.a), channel_id=1, source_target_pairs={{0,3},{1,0},{2,1},{3,2},{4,7},{5,4},{6,5},{7,6},{8,11},{9,8},{10,9... | collective-permute-start | bytes 165896 | tf_op jit(solution)/shard_map/while/body/ppermute | solution.py:286
  228.1 4.5 %collective-permute-start.3 = (bf16[72,384]{1,0:T(8,128)(2,1)S(1)}, bf16[72,384]{1,0:T(8,128)(2,1)S(1)}, u32[]{:S(2)}, u32[]{:S(2)}) collective-permute-start(bf16[72,384]{1,0:T(8,128)(2,1)S(1)} %update.5.a), channel_id=1, source_target_pairs={{0,2},{1,3},{2,0},{3,1},{4,6},{5,7},{6,4},{7,5},{8,10},{9,11},{10,... | collective-permute-start | bytes 165896 | tf_op jit(solution)/shard_map/while/body/ppermute | solution.py:286
  228.7 5.0 %collective-permute-start.2 = (bf16[72,384]{1,0:T(8,128)(2,1)S(1)}, bf16[72,384]{1,0:T(8,128)(2,1)S(1)}, u32[]{:S(2)}, u32[]{:S(2)}) collective-permute-start(bf16[72,384]{1,0:T(8,128)(2,1)S(1)} %update.5.a), channel_id=1, source_target_pairs={{0,1},{1,2},{2,3},{3,0},{4,5},{5,6},{6,7},{7,4},{8,9},{9,10},{10,1... | collective-permute-start | bytes 165896 | tf_op jit(solution)/shard_map/while/body/ppermute | solution.py:286
  251.9 13.9 %all-to-all-start.1 = ((f32[32,1,1152]{2,1,0:T(1,128)}), f32[32,1,1152]{2,1,0:T(1,128)S(1)}, u32[]{:S(2)}, u32[]{:S(2)}) async-start(f32[32,1,1152]{2,1,0:T(1,128)} %bitcast.25), calls=%async_computation.1 | async-start | bytes 294912 | tf_op jit(solution)/shard_map/while/body/all_to_all | solution.py:292
  269.9 5.5 %collective-permute-start.4 = (bf16[72,384]{1,0:T(8,128)(2,1)S(1)}, bf16[72,384]{1,0:T(8,128)(2,1)S(1)}, u32[]{:S(2)}, u32[]{:S(2)}) collective-permute-start(bf16[72,384]{1,0:T(8,128)(2,1)S(1)} %update.5.a), channel_id=1, source_target_pairs={{0,3},{1,0},{2,1},{3,2},{4,7},{5,4},{6,5},{7,6},{8,11},{9,8},{10,9... | collective-permute-start | bytes 165896 | tf_op jit(solution)/shard_map/while/body/ppermute | solution.py:286
  271.7 4.8 %collective-permute-start.2 = (bf16[72,384]{1,0:T(8,128)(2,1)S(1)}, bf16[72,384]{1,0:T(8,128)(2,1)S(1)}, u32[]{:S(2)}, u32[]{:S(2)}) collective-permute-start(bf16[72,384]{1,0:T(8,128)(2,1)S(1)} %update.5.a), channel_id=1, source_target_pairs={{0,1},{1,2},{2,3},{3,0},{4,5},{5,6},{6,7},{7,4},{8,9},{9,10},{10,1... | collective-permute-start | bytes 165896 | tf_op jit(solution)/shard_map/while/body/ppermute | solution.py:286
  311.9 5.2 %collective-permute-start.14 = (bf16[72,384]{1,0:T(8,128)(2,1)S(1)}, bf16[72,384]{1,0:T(8,128)(2,1)S(1)}, u32[]{:S(2)}, u32[]{:S(2)}) collective-permute-start(bf16[72,384]{1,0:T(8,128)(2,1)S(1)} %update.4.a), channel_id=1, source_target_pairs={{0,3},{1,0},{2,1},{3,2},{4,7},{5,4},{6,5},{7,6},{8,11},{9,8},{10,9... | collective-permute-start | bytes 165896 | tf_op jit(solution)/shard_map/ppermute | solution.py:286
  313.6 4.9 %collective-permute-start.12 = (bf16[72,384]{1,0:T(8,128)(2,1)S(1)}, bf16[72,384]{1,0:T(8,128)(2,1)S(1)}, u32[]{:S(2)}, u32[]{:S(2)}) collective-permute-start(bf16[72,384]{1,0:T(8,128)(2,1)S(1)} %update.4.a), channel_id=1, source_target_pairs={{0,1},{1,2},{2,3},{3,0},{4,5},{5,6},{6,7},{7,4},{8,9},{9,10},{10,1... | collective-permute-start | bytes 165896 | tf_op jit(solution)/shard_map/ppermute | solution.py:286
  (24 other events, 99.0 us)

commit v3 on v2

--- a/solution.py
+++ b/solution.py
@@ -69,18 +69,24 @@
     spread(both[:comps] + both[comps:] - shift, gram_of(stepped), first, keep_ref, send_ref)
 
 
-def first_kernel(core_ref, loadings_ref, picks_ref, pool_ref, keep_ref, send_ref, buffer_ref, sems):
+def first_kernel(place_ref, loadings_ref, picks_ref, pool_ref, keep_ref, send_ref, start_ref, names_ref, buffer_ref, sems):
     chunks, _, size = buffer_ref.shape
+    near = [
+        pltpu.make_async_copy(loadings_ref, start_ref, sems.at[chunks]),
+        pltpu.make_async_copy(picks_ref, names_ref, sems.at[chunks + 1]),
+    ]
     copies = [
         pltpu.make_async_copy(pool_ref.at[:, pl.ds(i * size, size)], buffer_ref.at[i], sems.at[i])
         for i in range(chunks)
     ]
-    for copy in copies:
+    for copy in near + copies:
         copy.start()
-    loadings = loadings_ref[...]
+    for copy in near:
+        copy.wait()
+    loadings = start_ref[...]
     comps = loadings.shape[0]
     pair = split_pair(loadings)
-    picks = picks_ref[...]
+    picks = names_ref[0:1, :] - place_ref[1]
     places = lax.broadcasted_iota(jnp.int32, (size, picks.shape[1]), 0)
     chosen = jnp.zeros((2 * comps, picks.shape[1]), f32)
     for i, copy in enumerate(copies):
@@ -89,7 +95,7 @@
         every = split_pair(both[:comps] + both[comps:])
         one_hot = jnp.where(places == picks - i * size, 1.0, 0.0).astype(bf16)
         chosen = chosen + lax.dot_general(every, one_hot, NN, preferred_element_type=f32)
-    spread(chosen[:comps] + chosen[comps:], gram_of(loadings), core_ref[0] == 0, keep_ref, send_ref)
+    spread(chosen[:comps] + chosen[comps:], gram_of(loadings), place_ref[0] == 0, keep_ref, send_ref)
 
 
 def add_kernel(a, b, out_ref):
@@ -137,12 +143,16 @@
 
 
 def make_last(batch):
-    def kernel(a, b, c, d, previous_ref, inverse_ref, gram_ref, stepped_ref):
+    def kernel(core_ref, a, b, c, d, previous_ref, inverse_ref, keep_ref, send_ref, stepped_ref):
         stepped = stepped_from((a, b, c, d), previous_ref[...], inverse_ref[...], batch)
         stepped_ref[...] = stepped
         gram = gram_of(stepped)
-        half = gram.shape[0] // 2
-        gram_ref[...] = jnp.concatenate([gram[:half], gram[half:]], axis=1)
+        quarter = gram.shape[0] // 4
+        top = jnp.concatenate([gram[:quarter], gram[quarter : 2 * quarter]], axis=1)
+        bottom = jnp.concatenate([gram[2 * quarter : 3 * quarter], gram[3 * quarter :]], axis=1)
+        first = core_ref[0] == 0
+        keep_ref[...] = jnp.where(first, top, bottom)
+        send_ref[...] = jnp.where(first, bottom, top)
 
     return kernel
 
@@ -244,11 +254,22 @@
     return kernel
 
 
+def copies_kernel(a, b, out_ref):
+    out_ref[...] = jnp.broadcast_to((a[...] + b[...])[None], out_ref.shape)
+
+
+def total_kernel(in_ref, out_ref):
+    out_ref[...] = jnp.sum(in_ref[...], axis=0)
+
+
 def make_finish(scale):
-    def kernel(in_ref, stepped_ref, out_ref):
+    def kernel(core_ref, mine_ref, other_ref, stepped_ref, out_ref):
         comps = stepped_ref.shape[0]
-        total = jnp.sum(in_ref[...], axis=0)
-        gram = jnp.concatenate([total[:, :comps], total[:, comps:]], axis=0)
+        total = by_core(core_ref[0] == 0, mine_ref[...], other_ref[...])
+        quarter = comps // 4
+        gram = jnp.concatenate(
+            [total[h : h + quarter, w : w + comps] for h in (0, quarter) for w in (0, comps)], axis=0
+        )
         out_ref[...] = scale * lax.dot_general(
             inverse_factor(gram), stepped_ref[...], NN, precision=HIGH, preferred_element_type=f32
         )
@@ -267,8 +288,9 @@
     batch = cells * cell_devices
     rows = cells // 128 + 1
     width = genes + 128 - genes % 128
-    core = (lax.axis_index("gene") % 2).astype(jnp.int32).reshape(1)
-    chosen = cell_picks - lax.axis_index("cell") * local_pool
+    first_cell = lax.axis_index("cell").astype(jnp.int32) * local_pool
+    core = jnp.stack([lax.axis_index("gene").astype(jnp.int32) % 2, first_cell])
+    chosen = cell_picks - first_cell
     pool_by_cell = pool_counts.T
     same_core = [[2 * chip + which for chip in range(chips)] for which in range(2)]
 
@@ -298,22 +320,27 @@
     row = jax.ShapeDtypeStruct((1, genes), f32)
     shared = jax.ShapeDtypeStruct((comps + 8, width), bf16)
 
-    tile = tile_of(chosen[0])
     chunk = local_pool // 8
     keep, send = vmem_call(
         first_kernel,
         (packed, packed),
-        2,
+        0,
         name="first",
-        pool=1,
-        scratch=[pltpu.VMEM((8, genes, chunk), bf16), pltpu.SemaphoreType.DMA((8,))],
-    )(core, loadings_init, chosen[:1], pool_counts)
-
-    def scores_of(keep, send):
+        pool=3,
+        scratch=[
+            pltpu.VMEM((comps, genes), f32),
+            pltpu.VMEM((steps, cells), jnp.int32),
+            pltpu.VMEM((8, genes, chunk), bf16),
+            pltpu.SemaphoreType.DMA((10,)),
+        ],
+    )(core, loadings_init, cell_picks, pool_counts)
+
+    def scores_of(keep, send, later):
         chip_sum = vmem_call(add_kernel, packed, 2, name="pair", core=False)(keep, swap_cores(send))
-        copies = vmem_call(make_sum(chips, rows), packed, 1, name="add_up", core=False)(exchange(chip_sum))
+        came, later = lax.optimization_barrier((exchange(chip_sum), later))
+        copies = vmem_call(make_sum(chips, rows), packed, 1, name="add_up", core=False)(came)
         mine = exchange(copies)
-        return mine, swap_cores(mine)
+        return mine, swap_cores(mine), later
 
     def change_of(mine, other, tile, mean, next_sums, own=None):
         change = vmem_call(make_update(half, rows, own), shared, 5, name="update")(
@@ -335,49 +362,34 @@
         following = step + 1
         picks = lax.dynamic_index_in_dim(chosen, following, keepdims=False)
         following, picks, send = lax.optimization_barrier((following, picks, send))
+        mine, other, picks = scores_of(keep, send, picks)
         next_tile = tile_of(picks)
-        mine, other = scores_of(keep, send)
         parts = change_of(mine, other, tile, mean, sums_of(next_tile))
         inverse = (factor_of(mine, other),)
         return (following, *advance(parts, stepped, inverse, next_tile), next_tile)
 
-    next_tile = tile_of(chosen[1])
-    mine, other = scores_of(keep, send)
+    mine, other, picks = scores_of(keep, send, chosen[:2])
+    tile, next_tile = jnp.split(tile_of(picks.reshape(-1)), 2)
     parts = change_of(mine, other, tile, sums_of(tile), sums_of(next_tile), cells)
     state = (*advance(parts, loadings_init, (), next_tile), next_tile)
     _, keep, send, stepped, mean, tile = lax.while_loop(
         lambda state: state[0] < steps - 1, one_step, (jnp.int32(1), *state)
     )
-    mine, other = scores_of(keep, send)
+    mine, other, _ = scores_of(keep, send, ())
     parts = change_of(mine, other, tile, mean, mean)
     inverse = factor_of(mine, other)
-    gram, stepped = vmem_call(
-        make_last(batch),
-        (jax.ShapeDtypeStruct((half, 2 * comps), f32), local),
-        len(parts) + 2,
-        name="last",
-        core=False,
-    )(*parts, stepped, inverse)
-    gram = gram + swap_cores(gram)
-    depth = 8
-    planes = chips // depth
-    gram = sum(
-        [gram]
-        + [
-            lax.ppermute(gram, "gene", [(i, (i + k * 2 * depth) % gene_devices) for i in range(gene_devices)])
-            for k in range(1, planes)
-        ]
-    )
-    columns = [
-        [(plane * depth + level) * 2 + which for level in range(depth)]
-        for plane in range(planes)
-        for which in range(2)
-    ]
-    grams = lax.all_to_all(
-        jnp.broadcast_to(gram[None], (depth, *gram.shape)), "gene", 0, 0, tiled=True, axis_index_groups=columns
-    )
+    few = jax.ShapeDtypeStruct((comps // 4, 2 * comps), f32)
+    many = jax.ShapeDtypeStruct((chips, comps // 4, 2 * comps), f32)
+    keep, send, stepped = vmem_call(make_last(batch), (few, few, local), len(parts) + 2, name="last")(
+        core, *parts, stepped, inverse
+    )
+    copies = vmem_call(copies_kernel, many, 2, name="copies", core=False)(keep, swap_cores(send))
+    came = lax.all_to_all(copies, "gene", 0, 0, tiled=True, axis_index_groups=same_core)
+    mine = vmem_call(total_kernel, few, 1, name="total", core=False)(came)
     scale = math.sqrt(genes * gene_devices)
-    return vmem_call(make_finish(scale), local, 2, name="finish", core=False, held=False)(grams, stepped)
+    return vmem_call(make_finish(scale), local, 3, name="finish", held=False)(
+        core, mine, swap_cores(mine), stepped
+    )
 
 
 def solution(mesh):

time: 343 us -> 352 us (1.026)
  Pallas kernels: 38.1 us -> 50.4 us
  waiting for transfers between devices: 47.8 us -> 38 us
  blocking collectives: 109 us -> 116 us
    pallas_call x36 -> x38, Pallas kernels: 38.1 us -> 50.4 us  [run(): return call(*args[:core], *near, *args[last:])]
    ppermute x21, starting transfers between devices: 17.7 us -> 27.1 us  [round_cells(): lax.ppermute(value, 'cell', [(i, (i + k) % cell_devices) for i in range(c...]
    ppermute x21, waiting for transfers between devices: 11.5 us -> 2.32 us  [round_cells(): lax.ppermute(value, 'cell', [(i, (i + k) % cell_devices) for i in range(c...]
    all_to_all x7, starting transfers between devices: 41.9 us -> 37.4 us  [exchange(): lax.all_to_all(pieces, 'gene', 0, 0, tiled=True, axis_index_groups=same_c...]
    ppermute x3 -> x0, waiting for transfers between devices: 4.09 us -> none  [shards(): lax.ppermute(gram, 'gene', [(i, (i + k * 2 * depth) % gene_devices) for i...]
    all_to_all x7, blocking collectives: 99 us -> 103 us  [exchange(): lax.all_to_all(pieces, 'gene', 0, 0, tiled=True, axis_index_groups=same_c...]
    gather x7 -> x6, local copies, waits for them, and re-layouts: 42.5 us -> 39.8 us  [tile_of(): return jnp.take(pool_by_cell, picks, axis=0, mode='clip')]
    ppermute x15 -> x16, starting transfers between devices: 33.7 us -> 34.5 us  [swap_cores(): lax.ppermute(value, 'gene', [(i, i ^ 1) for i in range(gene_devices)])]
  transfers between devices with their start and end apart: 46 -> 44, of which waited for: 38 -> 23; matrix products, arithmetic and copies ran while one was open for 14% -> 13% of each run, Pallas kernels for 5% -> 6%
where the time goes in v3:
time: 352 us; the launch traced here: 351 us
  blocking collectives  116 us (33%)
  starting transfers between devices  99 us (28%)
  Pallas kernels  50.4 us (14%)
  local copies, waits for them, and re-layouts  45.6 us (13%)
  waiting for transfers between devices  38 us (11%)
    all_to_all x7, blocking collectives, exchange(): lax.all_to_all(pieces, 'gene', 0, 0, tiled=True, axis_index_groups=same_c...  103 us
    pallas_call x38, Pallas kernels, run(): return call(*args[:core], *near, *args[last:])  50.4 us
    gather x6, local copies, waits for them, and re-layouts, tile_of(): return jnp.take(pool_by_cell, picks, axis=0, mode='clip')  39.8 us
    all_to_all x7, starting transfers between devices, exchange(): lax.all_to_all(pieces, 'gene', 0, 0, tiled=True, axis_index_groups=same_c...  37.4 us
    ppermute x16, starting transfers between devices, swap_cores(): lax.ppermute(value, 'gene', [(i, i ^ 1) for i in range(gene_devices)])  34.5 us
    ppermute x21, starting transfers between devices, round_cells(): lax.ppermute(value, 'cell', [(i, (i + k) % cell_devices) for i in range(c...  27.1 us
    all_to_all x7, waiting for transfers between devices, exchange(): lax.all_to_all(pieces, 'gene', 0, 0, tiled=True, axis_index_groups=same_c...  21.8 us
    ppermute x16, waiting for transfers between devices, swap_cores(): lax.ppermute(value, 'gene', [(i, i ^ 1) for i in range(gene_devices)])  13.9 us
  transfers between devices with their start and end apart: 44, of which 23 were waited for; matrix products, arithmetic and copies ran while one was open for 13% of the time, Pallas kernels for 6%

profile of v3, /device:TPU:1, one launch (start us, length us, event | category | flops | bytes accessed | tf_op | source)
XLA Modules:
  0.0 350.8 jit_solution(13519202136579619722)
XLA Ops:
  0.1 5.4 %first.1 = (f32[288,128]{1,0:T(8,128)S(1)}, f32[288,128]{1,0:T(8,128)S(1)}) custom-call(s32[2]{0:T(128)S(1)} %pad_add_fusion.place_ref.core_ref, f32[64,320]{1,0:T(8,128)} %previous_ref.1, s32[7,1024]{1,0:T(8,128)} %picks_ref.1, bf16[320,4096]{1,0:T(8,128)(2,1)} %pool_ref.1), custom_call_target="tpu_custom_call" | custom-call | tf_op jit(solution)/shard_map/first/pallas_call | solution.py:35
  10.5 9.3 %all-to-all-start.2 = ((f32[32,1,1152]{2,1,0:T(1,128)}), f32[32,1,1152]{2,1,0:T(1,128)S(1)}, u32[]{:S(2)}, u32[]{:S(2)}) async-start(f32[32,1,1152]{2,1,0:T(1,128)} %bitcast.7), calls=%async_computation.2 | async-start | bytes 294912 | tf_op jit(solution)/shard_map/all_to_all | solution.py:314
  22.7 6.3 %all-to-all-done.2 = f32[32,1,1152]{2,1,0:T(1,128)S(1)} async-done(((f32[32,1,1152]{2,1,0:T(1,128)}), f32[32,1,1152]{2,1,0:T(1,128)S(1)}, u32[]{:S(2)}, u32[]{:S(2)}) %all-to-all-start.2) | async-done | bytes 147488 | tf_op jit(solution)/shard_map/all_to_all | solution.py:314
  29.7 4.7 %all-to-all-start.3 = ((f32[32,1,1152]{2,1,0:T(1,128)}), f32[32,1,1152]{2,1,0:T(1,128)S(1)}, u32[]{:S(2)}, u32[]{:S(2)}) async-start(f32[32,1,1152]{2,1,0:T(1,128)} %bitcast.9), calls=%async_computation.3 | async-start | bytes 294912 | tf_op jit(solution)/shard_map/all_to_all | solution.py:314
  34.4 9.5 %gather_fusion.1 = bf16[2048,320]{1,0:T(8,128)(2,1)S(1)} fusion(bf16[4096,320]{1,0:T(8,128)(2,1)} %bitcast.43, s32[2048]{0:T(1024)S(1)} %bitcast_clamp_fusion), kind=kCustom, calls=%fused_computation.1 | custom fusion | bytes 2629632 | tf_op jit(solution)/shard_map/jit(_take)/gather | solution.py:298
  57.4 226.2 %while.20 = (s32[]{:T(128)}, f32[288,128]{1,0:T(8,128)S(1)}, f32[288,128]{1,0:T(8,128)S(1)}, f32[64,320]{1,0:T(8,128)S(1)}, f32[1,320]{1,0:T(1,128)S(1)}, /*inde...) while((s32[]{:T(128)}, f32[288,128]{1,0:T(8,128)S(1)}, ...), condition=%wide.region_4.5_spmd, body=%wide.region_2.4_spmd.sunk | while | flops 1000656064 | bytes 6045835 | solution.py:375
  60.0 18.5 %all_to_all.46 = f32[32,1,1152]{2,1,0:T(1,128)S(1)} all-to-all(f32[32,1,1152]{2,1,0:T(1,128)S(1)} %bitcast.32), channel_id=1, replica_groups={{0,8,16,24,32,40,48,56,64,72,80,88,96,104,112,120,128,136,144,152,160,1..., dimensions={0} | all-to-all | bytes 294912 | tf_op jit(solution)/shard_map/while/body/all_to_all | solution.py:314
  79.2 4.7 %all-to-all-start.1 = ((f32[32,1,1152]{2,1,0:T(1,128)}), f32[32,1,1152]{2,1,0:T(1,128)S(1)}, u32[]{:S(2)}, u32[]{:S(2)}) async-start(f32[32,1,1152]{2,1,0:T(1,128)} %bitcast.27), calls=%async_computation.1 | async-start | bytes 294912 | tf_op jit(solution)/shard_map/while/body/all_to_all | solution.py:314
  83.9 6.1 %gather_fusion = bf16[1024,320]{1,0:T(8,128)(2,1)S(1)} fusion(bf16[4096,320]{1,0:T(8,128)(2,1)} %get-tuple-element.285, s32[1024]{0:T(1024)S(1)} %broadcast_clamp_fusion.2), kind=kCustom, calls=%fused_computation.clone.1 | custom fusion | bytes 1314816 | tf_op jit(solution)/shard_map/while/body/jit(_take)/gather | solution.py:298
  108.8 14.2 %all_to_all.46 = f32[32,1,1152]{2,1,0:T(1,128)S(1)} all-to-all(f32[32,1,1152]{2,1,0:T(1,128)S(1)} %bitcast.32), channel_id=1, replica_groups={{0,8,16,24,32,40,48,56,64,72,80,88,96,104,112,120,128,136,144,152,160,1..., dimensions={0} | all-to-all | bytes 294912 | tf_op jit(solution)/shard_map/while/body/all_to_all | solution.py:314
  123.6 4.7 %all-to-all-start.1 = ((f32[32,1,1152]{2,1,0:T(1,128)}), f32[32,1,1152]{2,1,0:T(1,128)S(1)}, u32[]{:S(2)}, u32[]{:S(2)}) async-start(f32[32,1,1152]{2,1,0:T(1,128)} %bitcast.27), calls=%async_computation.1 | async-start | bytes 294912 | tf_op jit(solution)/shard_map/while/body/all_to_all | solution.py:314
  128.3 6.1 %gather_fusion = bf16[1024,320]{1,0:T(8,128)(2,1)S(1)} fusion(bf16[4096,320]{1,0:T(8,128)(2,1)} %get-tuple-element.285, s32[1024]{0:T(1024)S(1)} %broadcast_clamp_fusion.2), kind=kCustom, calls=%fused_computation.clone.1 | custom fusion | bytes 1314816 | tf_op jit(solution)/shard_map/while/body/jit(_take)/gather | solution.py:298
  153.0 14.2 %all_to_all.46 = f32[32,1,1152]{2,1,0:T(1,128)S(1)} all-to-all(f32[32,1,1152]{2,1,0:T(1,128)S(1)} %bitcast.32), channel_id=1, replica_groups={{0,8,16,24,32,40,48,56,64,72,80,88,96,104,112,120,128,136,144,152,160,1..., dimensions={0} | all-to-all | bytes 294912 | tf_op jit(solution)/shard_map/while/body/all_to_all | solution.py:314
  167.8 4.7 %all-to-all-start.1 = ((f32[32,1,1152]{2,1,0:T(1,128)}), f32[32,1,1152]{2,1,0:T(1,128)S(1)}, u32[]{:S(2)}, u32[]{:S(2)}) async-start(f32[32,1,1152]{2,1,0:T(1,128)} %bitcast.27), calls=%async_computation.1 | async-start | bytes 294912 | tf_op jit(solution)/shard_map/while/body/all_to_all | solution.py:314
  172.6 6.1 %gather_fusion = bf16[1024,320]{1,0:T(8,128)(2,1)S(1)} fusion(bf16[4096,320]{1,0:T(8,128)(2,1)} %get-tuple-element.285, s32[1024]{0:T(1024)S(1)} %broadcast_clamp_fusion.2), kind=kCustom, calls=%fused_computation.clone.1 | custom fusion | bytes 1314816 | tf_op jit(solution)/shard_map/while/body/jit(_take)/gather | solution.py:298
  197.4 14.2 %all_to_all.46 = f32[32,1,1152]{2,1,0:T(1,128)S(1)} all-to-all(f32[32,1,1152]{2,1,0:T(1,128)S(1)} %bitcast.32), channel_id=1, replica_groups={{0,8,16,24,32,40,48,56,64,72,80,88,96,104,112,120,128,136,144,152,160,1..., dimensions={0} | all-to-all | bytes 294912 | tf_op jit(solution)/shard_map/while/body/all_to_all | solution.py:314
  212.2 4.7 %all-to-all-start.1 = ((f32[32,1,1152]{2,1,0:T(1,128)}), f32[32,1,1152]{2,1,0:T(1,128)S(1)}, u32[]{:S(2)}, u32[]{:S(2)}) async-start(f32[32,1,1152]{2,1,0:T(1,128)} %bitcast.27), calls=%async_computation.1 | async-start | bytes 294912 | tf_op jit(solution)/shard_map/while/body/all_to_all | solution.py:314
  216.9 6.1 %gather_fusion = bf16[1024,320]{1,0:T(8,128)(2,1)S(1)} fusion(bf16[4096,320]{1,0:T(8,128)(2,1)} %get-tuple-element.285, s32[1024]{0:T(1024)S(1)} %broadcast_clamp_fusion.2), kind=kCustom, calls=%fused_computation.clone.1 | custom fusion | bytes 1314816 | tf_op jit(solution)/shard_map/while/body/jit(_take)/gather | solution.py:298
  241.6 14.2 %all_to_all.46 = f32[32,1,1152]{2,1,0:T(1,128)S(1)} all-to-all(f32[32,1,1152]{2,1,0:T(1,128)S(1)} %bitcast.32), channel_id=1, replica_groups={{0,8,16,24,32,40,48,56,64,72,80,88,96,104,112,120,128,136,144,152,160,1..., dimensions={0} | all-to-all | bytes 294912 | tf_op jit(solution)/shard_map/while/body/all_to_all | solution.py:314
  256.5 4.7 %all-to-all-start.1 = ((f32[32,1,1152]{2,1,0:T(1,128)}), f32[32,1,1152]{2,1,0:T(1,128)S(1)}, u32[]{:S(2)}, u32[]{:S(2)}) async-start(f32[32,1,1152]{2,1,0:T(1,128)} %bitcast.27), calls=%async_computation.1 | async-start | bytes 294912 | tf_op jit(solution)/shard_map/while/body/all_to_all | solution.py:314
  261.2 6.1 %gather_fusion = bf16[1024,320]{1,0:T(8,128)(2,1)S(1)} fusion(bf16[4096,320]{1,0:T(8,128)(2,1)} %get-tuple-element.285, s32[1024]{0:T(1024)S(1)} %broadcast_clamp_fusion.2), kind=kCustom, calls=%fused_computation.clone.1 | custom fusion | bytes 1314816 | tf_op jit(solution)/shard_map/while/body/jit(_take)/gather | solution.py:298
  286.0 14.2 %all_to_all.43 = f32[32,1,1152]{2,1,0:T(1,128)S(1)} all-to-all(f32[32,1,1152]{2,1,0:T(1,128)S(1)} %bitcast.39), channel_id=1, replica_groups={{0,8,16,24,32,40,48,56,64,72,80,88,96,104,112,120,128,136,144,152,160,1..., dimensions={0} | all-to-all | bytes 294912 | tf_op jit(solution)/shard_map/all_to_all | solution.py:314
  300.2 13.7 %all_to_all.44 = f32[32,1,1152]{2,1,0:T(1,128)S(1)} all-to-all(f32[32,1,1152]{2,1,0:T(1,128)S(1)} %bitcast.42), channel_id=1, replica_groups={{0,8,16,24,32,40,48,56,64,72,80,88,96,104,112,120,128,136,144,152,160,1..., dimensions={0} | all-to-all | bytes 294912 | tf_op jit(solution)/shard_map/all_to_all | solution.py:314
  328.8 12.9 %all_to_all.45.in_ref = f32[32,16,128]{2,1,0:T(8,128)S(1)} all-to-all(f32[32,16,128]{2,1,0:T(8,128)S(1)} %copies.1), channel_id=1, replica_groups={{0,8,16,24,32,40,48,56,64,72,80,88,96,104,112,120,128,136,144,152,160,1..., dimensions={0} | all-to-all | bytes 524288 | tf_op jit(solution)/shard_map/all_to_all | solution.py:387
  (164 shorter events, 145.2 us)
Async XLA Ops:
  10.5 18.5 %all-to-all-start.2 = ((f32[32,1,1152]{2,1,0:T(1,128)}), f32[32,1,1152]{2,1,0:T(1,128)S(1)}, u32[]{:S(2)}, u32[]{:S(2)}) async-start(f32[32,1,1152]{2,1,0:T(1,128)} %bitcast.7), calls=%async_computation.2 | async-start | bytes 294912 | tf_op jit(solution)/shard_map/all_to_all | solution.py:314
  29.7 14.5 %all-to-all-start.3 = ((f32[32,1,1152]{2,1,0:T(1,128)}), f32[32,1,1152]{2,1,0:T(1,128)S(1)}, u32[]{:S(2)}, u32[]{:S(2)}) async-start(f32[32,1,1152]{2,1,0:T(1,128)} %bitcast.9), calls=%async_computation.3 | async-start | bytes 294912 | tf_op jit(solution)/shard_map/all_to_all | solution.py:314
  49.0 5.1 %collective-permute-start.7 = (bf16[72,384]{1,0:T(8,128)(2,1)S(1)}, bf16[72,384]{1,0:T(8,128)(2,1)S(1)}, u32[]{:S(2)}, u32[]{:S(2)}) collective-permute-start(bf16[72,384]{1,0:T(8,128)(2,1)S(1)} %update.3.a), channel_id=1, source_target_pairs={{0,1},{1,2},{2,3},{3,0},{4,5},{5,6},{6,7},{7,4},{8,9},{9,10},{10,1... | collective-permute-start | bytes 165896 | tf_op jit(solution)/shard_map/ppermute | solution.py:308
  50.3 5.7 %collective-permute-start.8 = (bf16[72,384]{1,0:T(8,128)(2,1)S(1)}, bf16[72,384]{1,0:T(8,128)(2,1)S(1)}, u32[]{:S(2)}, u32[]{:S(2)}) collective-permute-start(bf16[72,384]{1,0:T(8,128)(2,1)S(1)} %update.3.a), channel_id=1, source_target_pairs={{0,2},{1,3},{2,0},{3,1},{4,6},{5,7},{6,4},{7,5},{8,10},{9,11},{10,... | collective-permute-start | bytes 165896 | tf_op jit(solution)/shard_map/ppermute | solution.py:308
  79.2 13.9 %all-to-all-start.1 = ((f32[32,1,1152]{2,1,0:T(1,128)}), f32[32,1,1152]{2,1,0:T(1,128)S(1)}, u32[]{:S(2)}, u32[]{:S(2)}) async-start(f32[32,1,1152]{2,1,0:T(1,128)} %bitcast.27), calls=%async_computation.1 | async-start | bytes 294912 | tf_op jit(solution)/shard_map/while/body/all_to_all | solution.py:314
  97.8 7.3 %collective-permute-start.2 = (bf16[72,384]{1,0:T(8,128)(2,1)S(1)}, bf16[72,384]{1,0:T(8,128)(2,1)S(1)}, u32[]{:S(2)}, u32[]{:S(2)}) collective-permute-start(bf16[72,384]{1,0:T(8,128)(2,1)S(1)} %update.5.a), channel_id=1, source_target_pairs={{0,1},{1,2},{2,3},{3,0},{4,5},{5,6},{6,7},{7,4},{8,9},{9,10},{10,1... | collective-permute-start | bytes 165896 | tf_op jit(solution)/shard_map/while/body/ppermute | solution.py:308
  98.2 6.9 %collective-permute-start.3 = (bf16[72,384]{1,0:T(8,128)(2,1)S(1)}, bf16[72,384]{1,0:T(8,128)(2,1)S(1)}, u32[]{:S(2)}, u32[]{:S(2)}) collective-permute-start(bf16[72,384]{1,0:T(8,128)(2,1)S(1)} %update.5.a), channel_id=1, source_target_pairs={{0,2},{1,3},{2,0},{3,1},{4,6},{5,7},{6,4},{7,5},{8,10},{9,11},{10,... | collective-permute-start | bytes 165896 | tf_op jit(solution)/shard_map/while/body/ppermute | solution.py:308
  123.6 13.9 %all-to-all-start.1 = ((f32[32,1,1152]{2,1,0:T(1,128)}), f32[32,1,1152]{2,1,0:T(1,128)S(1)}, u32[]{:S(2)}, u32[]{:S(2)}) async-start(f32[32,1,1152]{2,1,0:T(1,128)} %bitcast.27), calls=%async_computation.1 | async-start | bytes 294912 | tf_op jit(solution)/shard_map/while/body/all_to_all | solution.py:314
  142.2 7.5 %collective-permute-start.2 = (bf16[72,384]{1,0:T(8,128)(2,1)S(1)}, bf16[72,384]{1,0:T(8,128)(2,1)S(1)}, u32[]{:S(2)}, u32[]{:S(2)}) collective-permute-start(bf16[72,384]{1,0:T(8,128)(2,1)S(1)} %update.5.a), channel_id=1, source_target_pairs={{0,1},{1,2},{2,3},{3,0},{4,5},{5,6},{6,7},{7,4},{8,9},{9,10},{10,1... | collective-permute-start | bytes 165896 | tf_op jit(solution)/shard_map/while/body/ppermute | solution.py:308
  143.5 6.2 %collective-permute-start.3 = (bf16[72,384]{1,0:T(8,128)(2,1)S(1)}, bf16[72,384]{1,0:T(8,128)(2,1)S(1)}, u32[]{:S(2)}, u32[]{:S(2)}) collective-permute-start(bf16[72,384]{1,0:T(8,128)(2,1)S(1)} %update.5.a), channel_id=1, source_target_pairs={{0,2},{1,3},{2,0},{3,1},{4,6},{5,7},{6,4},{7,5},{8,10},{9,11},{10,... | collective-permute-start | bytes 165896 | tf_op jit(solution)/shard_map/while/body/ppermute | solution.py:308
  144.8 4.9 %collective-permute-start.4 = (bf16[72,384]{1,0:T(8,128)(2,1)S(1)}, bf16[72,384]{1,0:T(8,128)(2,1)S(1)}, u32[]{:S(2)}, u32[]{:S(2)}) collective-permute-start(bf16[72,384]{1,0:T(8,128)(2,1)S(1)} %update.5.a), channel_id=1, source_target_pairs={{0,3},{1,0},{2,1},{3,2},{4,7},{5,4},{6,5},{7,6},{8,11},{9,8},{10,9... | collective-permute-start | bytes 165896 | tf_op jit(solution)/shard_map/while/body/ppermute | solution.py:308
  167.8 13.9 %all-to-all-start.1 = ((f32[32,1,1152]{2,1,0:T(1,128)}), f32[32,1,1152]{2,1,0:T(1,128)S(1)}, u32[]{:S(2)}, u32[]{:S(2)}) async-start(f32[32,1,1152]{2,1,0:T(1,128)} %bitcast.27), calls=%async_computation.1 | async-start | bytes 294912 | tf_op jit(solution)/shard_map/while/body/all_to_all | solution.py:314
  186.4 7.4 %collective-permute-start.2 = (bf16[72,384]{1,0:T(8,128)(2,1)S(1)}, bf16[72,384]{1,0:T(8,128)(2,1)S(1)}, u32[]{:S(2)}, u32[]{:S(2)}) collective-permute-start(bf16[72,384]{1,0:T(8,128)(2,1)S(1)} %update.5.a), channel_id=1, source_target_pairs={{0,1},{1,2},{2,3},{3,0},{4,5},{5,6},{6,7},{7,4},{8,9},{9,10},{10,1... | collective-permute-start | bytes 165896 | tf_op jit(solution)/shard_map/while/body/ppermute | solution.py:308
  187.0 6.8 %collective-permute-start.3 = (bf16[72,384]{1,0:T(8,128)(2,1)S(1)}, bf16[72,384]{1,0:T(8,128)(2,1)S(1)}, u32[]{:S(2)}, u32[]{:S(2)}) collective-permute-start(bf16[72,384]{1,0:T(8,128)(2,1)S(1)} %update.5.a), channel_id=1, source_target_pairs={{0,2},{1,3},{2,0},{3,1},{4,6},{5,7},{6,4},{7,5},{8,10},{9,11},{10,... | collective-permute-start | bytes 165896 | tf_op jit(solution)/shard_map/while/body/ppermute | solution.py:308
  189.1 4.6 %collective-permute-start.4 = (bf16[72,384]{1,0:T(8,128)(2,1)S(1)}, bf16[72,384]{1,0:T(8,128)(2,1)S(1)}, u32[]{:S(2)}, u32[]{:S(2)}) collective-permute-start(bf16[72,384]{1,0:T(8,128)(2,1)S(1)} %update.5.a), channel_id=1, source_target_pairs={{0,3},{1,0},{2,1},{3,2},{4,7},{5,4},{6,5},{7,6},{8,11},{9,8},{10,9... | collective-permute-start | bytes 165896 | tf_op jit(solution)/shard_map/while/body/ppermute | solution.py:308
  212.2 13.9 %all-to-all-start.1 = ((f32[32,1,1152]{2,1,0:T(1,128)}), f32[32,1,1152]{2,1,0:T(1,128)S(1)}, u32[]{:S(2)}, u32[]{:S(2)}) async-start(f32[32,1,1152]{2,1,0:T(1,128)} %bitcast.27), calls=%async_computation.1 | async-start | bytes 294912 | tf_op jit(solution)/shard_map/while/body/all_to_all | solution.py:314
  230.8 7.2 %collective-permute-start.2 = (bf16[72,384]{1,0:T(8,128)(2,1)S(1)}, bf16[72,384]{1,0:T(8,128)(2,1)S(1)}, u32[]{:S(2)}, u32[]{:S(2)}) collective-permute-start(bf16[72,384]{1,0:T(8,128)(2,1)S(1)} %update.5.a), channel_id=1, source_target_pairs={{0,1},{1,2},{2,3},{3,0},{4,5},{5,6},{6,7},{7,4},{8,9},{9,10},{10,1... | collective-permute-start | bytes 165896 | tf_op jit(solution)/shard_map/while/body/ppermute | solution.py:308
  231.4 6.7 %collective-permute-start.3 = (bf16[72,384]{1,0:T(8,128)(2,1)S(1)}, bf16[72,384]{1,0:T(8,128)(2,1)S(1)}, u32[]{:S(2)}, u32[]{:S(2)}) collective-permute-start(bf16[72,384]{1,0:T(8,128)(2,1)S(1)} %update.5.a), channel_id=1, source_target_pairs={{0,2},{1,3},{2,0},{3,1},{4,6},{5,7},{6,4},{7,5},{8,10},{9,11},{10,... | collective-permute-start | bytes 165896 | tf_op jit(solution)/shard_map/while/body/ppermute | solution.py:308
  256.5 13.9 %all-to-all-start.1 = ((f32[32,1,1152]{2,1,0:T(1,128)}), f32[32,1,1152]{2,1,0:T(1,128)S(1)}, u32[]{:S(2)}, u32[]{:S(2)}) async-start(f32[32,1,1152]{2,1,0:T(1,128)} %bitcast.27), calls=%async_computation.1 | async-start | bytes 294912 | tf_op jit(solution)/shard_map/while/body/all_to_all | solution.py:314
  275.0 7.4 %collective-permute-start.2 = (bf16[72,384]{1,0:T(8,128)(2,1)S(1)}, bf16[72,384]{1,0:T(8,128)(2,1)S(1)}, u32[]{:S(2)}, u32[]{:S(2)}) collective-permute-start(bf16[72,384]{1,0:T(8,128)(2,1)S(1)} %update.5.a), channel_id=1, source_target_pairs={{0,1},{1,2},{2,3},{3,0},{4,5},{5,6},{6,7},{7,4},{8,9},{9,10},{10,1... | collective-permute-start | bytes 165896 | tf_op jit(solution)/shard_map/while/body/ppermute | solution.py:308
  275.7 6.7 %collective-permute-start.3 = (bf16[72,384]{1,0:T(8,128)(2,1)S(1)}, bf16[72,384]{1,0:T(8,128)(2,1)S(1)}, u32[]{:S(2)}, u32[]{:S(2)}) collective-permute-start(bf16[72,384]{1,0:T(8,128)(2,1)S(1)} %update.5.a), channel_id=1, source_target_pairs={{0,2},{1,3},{2,0},{3,1},{4,6},{5,7},{6,4},{7,5},{8,10},{9,11},{10,... | collective-permute-start | bytes 165896 | tf_op jit(solution)/shard_map/while/body/ppermute | solution.py:308
  318.4 7.1 %collective-permute-start.12 = (bf16[72,384]{1,0:T(8,128)(2,1)S(1)}, bf16[72,384]{1,0:T(8,128)(2,1)S(1)}, u32[]{:S(2)}, u32[]{:S(2)}) collective-permute-start(bf16[72,384]{1,0:T(8,128)(2,1)S(1)} %update.4.a), channel_id=1, source_target_pairs={{0,1},{1,2},{2,3},{3,0},{4,5},{5,6},{6,7},{7,4},{8,9},{9,10},{10,1... | collective-permute-start | bytes 165896 | tf_op jit(solution)/shard_map/ppermute | solution.py:308
  319.1 6.5 %collective-permute-start.13 = (bf16[72,384]{1,0:T(8,128)(2,1)S(1)}, bf16[72,384]{1,0:T(8,128)(2,1)S(1)}, u32[]{:S(2)}, u32[]{:S(2)}) collective-permute-start(bf16[72,384]{1,0:T(8,128)(2,1)S(1)} %update.4.a), channel_id=1, source_target_pairs={{0,2},{1,3},{2,0},{3,1},{4,6},{5,7},{6,4},{7,5},{8,10},{9,11},{10,... | collective-permute-start | bytes 165896 | tf_op jit(solution)/shard_map/ppermute | solution.py:308
  341.8 4.6 %collective-permute-start.16 = (f32[16,128]{1,0:T(8,128)S(1)}, f32[16,128]{1,0:T(8,128)S(1)}, u32[]{:S(2)}, u32[]{:S(2)}) collective-permute-start(f32[16,128]{1,0:T(8,128)S(1)} %total.1.mine_ref), channel_id=1, source_target_pairs={{0,4},{4,0},{8,12},{12,8},{16,20},{20,16},{24,28},{28,24},{32,36},... | collective-permute-start | bytes 24584 | tf_op jit(solution)/shard_map/ppermute | solution.py:304
  (24 other events, 101.8 us)

commit v4 on v3

--- a/solution.py
+++ b/solution.py
@@ -69,7 +69,7 @@
     spread(both[:comps] + both[comps:] - shift, gram_of(stepped), first, keep_ref, send_ref)
 
 
-def first_kernel(place_ref, loadings_ref, picks_ref, pool_ref, keep_ref, send_ref, start_ref, names_ref, buffer_ref, sems):
+def first_kernel(core_ref, cell_ref, loadings_ref, picks_ref, pool_ref, keep_ref, send_ref, start_ref, names_ref, buffer_ref, sems):
     chunks, _, size = buffer_ref.shape
     near = [
         pltpu.make_async_copy(loadings_ref, start_ref, sems.at[chunks]),
@@ -86,7 +86,7 @@
     loadings = start_ref[...]
     comps = loadings.shape[0]
     pair = split_pair(loadings)
-    picks = names_ref[0:1, :] - place_ref[1]
+    picks = names_ref[0:1, :] - cell_ref[0]
     places = lax.broadcasted_iota(jnp.int32, (size, picks.shape[1]), 0)
     chosen = jnp.zeros((2 * comps, picks.shape[1]), f32)
     for i, copy in enumerate(copies):
@@ -95,7 +95,7 @@
         every = split_pair(both[:comps] + both[comps:])
         one_hot = jnp.where(places == picks - i * size, 1.0, 0.0).astype(bf16)
         chosen = chosen + lax.dot_general(every, one_hot, NN, preferred_element_type=f32)
-    spread(chosen[:comps] + chosen[comps:], gram_of(loadings), place_ref[0] == 0, keep_ref, send_ref)
+    spread(chosen[:comps] + chosen[comps:], gram_of(loadings), core_ref[0] == 0, keep_ref, send_ref)
 
 
 def add_kernel(a, b, out_ref):
@@ -289,7 +289,7 @@
     rows = cells // 128 + 1
     width = genes + 128 - genes % 128
     first_cell = lax.axis_index("cell").astype(jnp.int32) * local_pool
-    core = jnp.stack([lax.axis_index("gene").astype(jnp.int32) % 2, first_cell])
+    core = (lax.axis_index("gene") % 2).astype(jnp.int32).reshape(1)
     chosen = cell_picks - first_cell
     pool_by_cell = pool_counts.T
     same_core = [[2 * chip + which for chip in range(chips)] for which in range(2)]
@@ -326,6 +326,7 @@
         (packed, packed),
         0,
         name="first",
+        core=2,
         pool=3,
         scratch=[
             pltpu.VMEM((comps, genes), f32),
@@ -333,7 +334,7 @@
             pltpu.VMEM((8, genes, chunk), bf16),
             pltpu.SemaphoreType.DMA((10,)),
         ],
-    )(core, loadings_init, cell_picks, pool_counts)
+    )(core, first_cell.reshape(1), loadings_init, cell_picks, pool_counts)
 
     def scores_of(keep, send, later):
         chip_sum = vmem_call(add_kernel, packed, 2, name="pair", core=False)(keep, swap_cores(send))

time: 352 us -> 341 us (0.969)
  Pallas kernels: 50.4 us -> 38.4 us
    pallas_call x38, Pallas kernels: 50.4 us -> 38.4 us  [run(): return call(*args[:core], *near, *args[last:])]
  transfers between devices with their start and end apart: 44 -> 44, of which waited for: 23 -> 27; matrix products, arithmetic and copies ran while one was open for 13% -> 13% of each run, Pallas kernels for 6% -> 5%
where the time goes in v4:
time: 341 us; the launch traced here: 340 us
  blocking collectives  116 us (34%)
  starting transfers between devices  99.4 us (29%)
  local copies, waits for them, and re-layouts  45.6 us (13%)
  waiting for transfers between devices  38.9 us (11%)
  Pallas kernels  38.4 us (11%)
    all_to_all x7, blocking collectives, exchange(): lax.all_to_all(pieces, 'gene', 0, 0, tiled=True, axis_index_groups=same_c...  103 us
    gather x6, local copies, waits for them, and re-layouts, tile_of(): return jnp.take(pool_by_cell, picks, axis=0, mode='clip')  39.8 us
    pallas_call x38, Pallas kernels, run(): return call(*args[:core], *near, *args[last:])  38.4 us
    all_to_all x7, starting transfers between devices, exchange(): lax.all_to_all(pieces, 'gene', 0, 0, tiled=True, axis_index_groups=same_c...  37.4 us
    ppermute x16, starting transfers between devices, swap_cores(): lax.ppermute(value, 'gene', [(i, i ^ 1) for i in range(gene_devices)])  35.8 us
    ppermute x21, starting transfers between devices, round_cells(): lax.ppermute(value, 'cell', [(i, (i + k) % cell_devices) for i in range(c...  26.3 us
    all_to_all x7, waiting for transfers between devices, exchange(): lax.all_to_all(pieces, 'gene', 0, 0, tiled=True, axis_index_groups=same_c...  21.8 us
    ppermute x16, waiting for transfers between devices, swap_cores(): lax.ppermute(value, 'gene', [(i, i ^ 1) for i in range(gene_devices)])  13.9 us
  transfers between devices with their start and end apart: 44, of which 27 were waited for; matrix products, arithmetic and copies ran while one was open for 13% of the time, Pallas kernels for 5%

profile of v4, /device:TPU:1, one launch (start us, length us, event | category | flops | bytes accessed | tf_op | source)
XLA Modules:
  0.0 340.1 jit_solution(2635262927624222054)
XLA Ops:
  0.0 4.8 %first.1 = (f32[288,128]{1,0:T(8,128)S(1)}, f32[288,128]{1,0:T(8,128)S(1)}) custom-call(s32[1]{0:T(128)} %bitcast.5.core_ref, s32[1]{0:T(128)} %bitcast.6.cell_ref, f32[64,320]{1,0:T(8,128)} %previous_ref.1, s32[7,1024]{1,0:T(8,128)} %picks_ref.1, bf16[320,4096]{1,0:T(8,128)(2,1)} %pool_ref.1), custom_call_target="tpu_custom_call" | custom-call | tf_op jit(solution)/shard_map/first/pallas_call | solution.py:35
  9.8 9.3 %all-to-all-start.2 = ((f32[32,1,1152]{2,1,0:T(1,128)}), f32[32,1,1152]{2,1,0:T(1,128)S(1)}, u32[]{:S(2)}, u32[]{:S(2)}) async-start(f32[32,1,1152]{2,1,0:T(1,128)} %bitcast.7), calls=%async_computation.2 | async-start | bytes 294912 | tf_op jit(solution)/shard_map/all_to_all | solution.py:314
  22.0 6.3 %all-to-all-done.2 = f32[32,1,1152]{2,1,0:T(1,128)S(1)} async-done(((f32[32,1,1152]{2,1,0:T(1,128)}), f32[32,1,1152]{2,1,0:T(1,128)S(1)}, u32[]{:S(2)}, u32[]{:S(2)}) %all-to-all-start.2) | async-done | bytes 147488 | tf_op jit(solution)/shard_map/all_to_all | solution.py:314
  29.0 4.7 %all-to-all-start.3 = ((f32[32,1,1152]{2,1,0:T(1,128)}), f32[32,1,1152]{2,1,0:T(1,128)S(1)}, u32[]{:S(2)}, u32[]{:S(2)}) async-start(f32[32,1,1152]{2,1,0:T(1,128)} %bitcast.9), calls=%async_computation.3 | async-start | bytes 294912 | tf_op jit(solution)/shard_map/all_to_all | solution.py:314
  33.7 9.5 %gather_fusion.1 = bf16[2048,320]{1,0:T(8,128)(2,1)S(1)} fusion(bf16[4096,320]{1,0:T(8,128)(2,1)} %bitcast.43, s32[2048]{0:T(1024)S(1)} %bitcast_clamp_fusion), kind=kCustom, calls=%fused_computation.1 | custom fusion | bytes 2629632 | tf_op jit(solution)/shard_map/jit(_take)/gather | solution.py:298
  55.6 219.0 %while.20 = (s32[]{:T(128)}, f32[288,128]{1,0:T(8,128)S(1)}, f32[288,128]{1,0:T(8,128)S(1)}, f32[64,320]{1,0:T(8,128)S(1)}, f32[1,320]{1,0:T(1,128)S(1)}, /*inde...) while((s32[]{:T(128)}, f32[288,128]{1,0:T(8,128)S(1)}, ...), condition=%wide.region_4.5_spmd, body=%wide.region_2.4_spmd.sunk | while | flops 1000656064 | bytes 6045835 | solution.py:376
  58.2 18.5 %all_to_all.46 = f32[32,1,1152]{2,1,0:T(1,128)S(1)} all-to-all(f32[32,1,1152]{2,1,0:T(1,128)S(1)} %bitcast.32), channel_id=1, replica_groups={{0,8,16,24,32,40,48,56,64,72,80,88,96,104,112,120,128,136,144,152,160,1..., dimensions={0} | all-to-all | bytes 294912 | tf_op jit(solution)/shard_map/while/body/all_to_all | solution.py:314
  77.4 4.7 %all-to-all-start.1 = ((f32[32,1,1152]{2,1,0:T(1,128)}), f32[32,1,1152]{2,1,0:T(1,128)S(1)}, u32[]{:S(2)}, u32[]{:S(2)}) async-start(f32[32,1,1152]{2,1,0:T(1,128)} %bitcast.27), calls=%async_computation.1 | async-start | bytes 294912 | tf_op jit(solution)/shard_map/while/body/all_to_all | solution.py:314
  82.1 6.1 %gather_fusion = bf16[1024,320]{1,0:T(8,128)(2,1)S(1)} fusion(bf16[4096,320]{1,0:T(8,128)(2,1)} %get-tuple-element.285, s32[1024]{0:T(1024)S(1)} %broadcast_clamp_fusion.2), kind=kCustom, calls=%fused_computation.clone.1 | custom fusion | bytes 1314816 | tf_op jit(solution)/shard_map/while/body/jit(_take)/gather | solution.py:298
  105.9 14.2 %all_to_all.46 = f32[32,1,1152]{2,1,0:T(1,128)S(1)} all-to-all(f32[32,1,1152]{2,1,0:T(1,128)S(1)} %bitcast.32), channel_id=1, replica_groups={{0,8,16,24,32,40,48,56,64,72,80,88,96,104,112,120,128,136,144,152,160,1..., dimensions={0} | all-to-all | bytes 294912 | tf_op jit(solution)/shard_map/while/body/all_to_all | solution.py:314
  120.7 4.7 %all-to-all-start.1 = ((f32[32,1,1152]{2,1,0:T(1,128)}), f32[32,1,1152]{2,1,0:T(1,128)S(1)}, u32[]{:S(2)}, u32[]{:S(2)}) async-start(f32[32,1,1152]{2,1,0:T(1,128)} %bitcast.27), calls=%async_computation.1 | async-start | bytes 294912 | tf_op jit(solution)/shard_map/while/body/all_to_all | solution.py:314
  125.4 6.1 %gather_fusion = bf16[1024,320]{1,0:T(8,128)(2,1)S(1)} fusion(bf16[4096,320]{1,0:T(8,128)(2,1)} %get-tuple-element.285, s32[1024]{0:T(1024)S(1)} %broadcast_clamp_fusion.2), kind=kCustom, calls=%fused_computation.clone.1 | custom fusion | bytes 1314816 | tf_op jit(solution)/shard_map/while/body/jit(_take)/gather | solution.py:298
  148.3 14.2 %all_to_all.46 = f32[32,1,1152]{2,1,0:T(1,128)S(1)} all-to-all(f32[32,1,1152]{2,1,0:T(1,128)S(1)} %bitcast.32), channel_id=1, replica_groups={{0,8,16,24,32,40,48,56,64,72,80,88,96,104,112,120,128,136,144,152,160,1..., dimensions={0} | all-to-all | bytes 294912 | tf_op jit(solution)/shard_map/while/body/all_to_all | solution.py:314
  163.2 4.7 %all-to-all-start.1 = ((f32[32,1,1152]{2,1,0:T(1,128)}), f32[32,1,1152]{2,1,0:T(1,128)S(1)}, u32[]{:S(2)}, u32[]{:S(2)}) async-start(f32[32,1,1152]{2,1,0:T(1,128)} %bitcast.27), calls=%async_computation.1 | async-start | bytes 294912 | tf_op jit(solution)/shard_map/while/body/all_to_all | solution.py:314
  167.9 6.1 %gather_fusion = bf16[1024,320]{1,0:T(8,128)(2,1)S(1)} fusion(bf16[4096,320]{1,0:T(8,128)(2,1)} %get-tuple-element.285, s32[1024]{0:T(1024)S(1)} %broadcast_clamp_fusion.2), kind=kCustom, calls=%fused_computation.clone.1 | custom fusion | bytes 1314816 | tf_op jit(solution)/shard_map/while/body/jit(_take)/gather | solution.py:298
  191.5 14.2 %all_to_all.46 = f32[32,1,1152]{2,1,0:T(1,128)S(1)} all-to-all(f32[32,1,1152]{2,1,0:T(1,128)S(1)} %bitcast.32), channel_id=1, replica_groups={{0,8,16,24,32,40,48,56,64,72,80,88,96,104,112,120,128,136,144,152,160,1..., dimensions={0} | all-to-all | bytes 294912 | tf_op jit(solution)/shard_map/while/body/all_to_all | solution.py:314
  206.3 4.7 %all-to-all-start.1 = ((f32[32,1,1152]{2,1,0:T(1,128)}), f32[32,1,1152]{2,1,0:T(1,128)S(1)}, u32[]{:S(2)}, u32[]{:S(2)}) async-start(f32[32,1,1152]{2,1,0:T(1,128)} %bitcast.27), calls=%async_computation.1 | async-start | bytes 294912 | tf_op jit(solution)/shard_map/while/body/all_to_all | solution.py:314
  211.0 6.1 %gather_fusion = bf16[1024,320]{1,0:T(8,128)(2,1)S(1)} fusion(bf16[4096,320]{1,0:T(8,128)(2,1)} %get-tuple-element.285, s32[1024]{0:T(1024)S(1)} %broadcast_clamp_fusion.2), kind=kCustom, calls=%fused_computation.clone.1 | custom fusion | bytes 1314816 | tf_op jit(solution)/shard_map/while/body/jit(_take)/gather | solution.py:298
  234.2 14.2 %all_to_all.46 = f32[32,1,1152]{2,1,0:T(1,128)S(1)} all-to-all(f32[32,1,1152]{2,1,0:T(1,128)S(1)} %bitcast.32), channel_id=1, replica_groups={{0,8,16,24,32,40,48,56,64,72,80,88,96,104,112,120,128,136,144,152,160,1..., dimensions={0} | all-to-all | bytes 294912 | tf_op jit(solution)/shard_map/while/body/all_to_all | solution.py:314
  249.1 4.7 %all-to-all-start.1 = ((f32[32,1,1152]{2,1,0:T(1,128)}), f32[32,1,1152]{2,1,0:T(1,128)S(1)}, u32[]{:S(2)}, u32[]{:S(2)}) async-start(f32[32,1,1152]{2,1,0:T(1,128)} %bitcast.27), calls=%async_computation.1 | async-start | bytes 294912 | tf_op jit(solution)/shard_map/while/body/all_to_all | solution.py:314
  253.8 6.1 %gather_fusion = bf16[1024,320]{1,0:T(8,128)(2,1)S(1)} fusion(bf16[4096,320]{1,0:T(8,128)(2,1)} %get-tuple-element.285, s32[1024]{0:T(1024)S(1)} %broadcast_clamp_fusion.2), kind=kCustom, calls=%fused_computation.clone.1 | custom fusion | bytes 1314816 | tf_op jit(solution)/shard_map/while/body/jit(_take)/gather | solution.py:298
  277.2 14.2 %all_to_all.43 = f32[32,1,1152]{2,1,0:T(1,128)S(1)} all-to-all(f32[32,1,1152]{2,1,0:T(1,128)S(1)} %bitcast.39), channel_id=1, replica_groups={{0,8,16,24,32,40,48,56,64,72,80,88,96,104,112,120,128,136,144,152,160,1..., dimensions={0} | all-to-all | bytes 294912 | tf_op jit(solution)/shard_map/all_to_all | solution.py:314
  291.3 13.7 %all_to_all.44 = f32[32,1,1152]{2,1,0:T(1,128)S(1)} all-to-all(f32[32,1,1152]{2,1,0:T(1,128)S(1)} %bitcast.42), channel_id=1, replica_groups={{0,8,16,24,32,40,48,56,64,72,80,88,96,104,112,120,128,136,144,152,160,1..., dimensions={0} | all-to-all | bytes 294912 | tf_op jit(solution)/shard_map/all_to_all | solution.py:314
  318.6 12.9 %all_to_all.45.in_ref = f32[32,16,128]{2,1,0:T(8,128)S(1)} all-to-all(f32[32,16,128]{2,1,0:T(8,128)S(1)} %copies.1), channel_id=1, replica_groups={{0,8,16,24,32,40,48,56,64,72,80,88,96,104,112,120,128,136,144,152,160,1..., dimensions={0} | all-to-all | bytes 524288 | tf_op jit(solution)/shard_map/all_to_all | solution.py:388
  (163 shorter events, 135.1 us)
Async XLA Ops:
  4.8 4.3 %collective-permute-start.5 = (f32[288,128]{1,0:T(8,128)S(1)}, f32[288,128]{1,0:T(8,128)S(1)}, u32[]{:S(2)}, u32[]{:S(2)}) collective-permute-start(f32[288,128]{1,0:T(8,128)S(1)} %get-tuple-element.144), channel_id=1, source_target_pairs={{0,4},{4,0},{8,12},{12,8},{16,20},{20,16},{24,28},{28,24},{32,36},... | collective-permute-start | bytes 442376 | tf_op jit(solution)/shard_map/ppermute | solution.py:304
  9.8 18.5 %all-to-all-start.2 = ((f32[32,1,1152]{2,1,0:T(1,128)}), f32[32,1,1152]{2,1,0:T(1,128)S(1)}, u32[]{:S(2)}, u32[]{:S(2)}) async-start(f32[32,1,1152]{2,1,0:T(1,128)} %bitcast.7), calls=%async_computation.2 | async-start | bytes 294912 | tf_op jit(solution)/shard_map/all_to_all | solution.py:314
  29.0 14.5 %all-to-all-start.3 = ((f32[32,1,1152]{2,1,0:T(1,128)}), f32[32,1,1152]{2,1,0:T(1,128)S(1)}, u32[]{:S(2)}, u32[]{:S(2)}) async-start(f32[32,1,1152]{2,1,0:T(1,128)} %bitcast.9), calls=%async_computation.3 | async-start | bytes 294912 | tf_op jit(solution)/shard_map/all_to_all | solution.py:314
  47.7 5.1 %collective-permute-start.7 = (bf16[72,384]{1,0:T(8,128)(2,1)S(1)}, bf16[72,384]{1,0:T(8,128)(2,1)S(1)}, u32[]{:S(2)}, u32[]{:S(2)}) collective-permute-start(bf16[72,384]{1,0:T(8,128)(2,1)S(1)} %update.3.a), channel_id=1, source_target_pairs={{0,1},{1,2},{2,3},{3,0},{4,5},{5,6},{6,7},{7,4},{8,9},{9,10},{10,1... | collective-permute-start | bytes 165896 | tf_op jit(solution)/shard_map/ppermute | solution.py:308
  49.1 5.7 %collective-permute-start.8 = (bf16[72,384]{1,0:T(8,128)(2,1)S(1)}, bf16[72,384]{1,0:T(8,128)(2,1)S(1)}, u32[]{:S(2)}, u32[]{:S(2)}) collective-permute-start(bf16[72,384]{1,0:T(8,128)(2,1)S(1)} %update.3.a), channel_id=1, source_target_pairs={{0,2},{1,3},{2,0},{3,1},{4,6},{5,7},{6,4},{7,5},{8,10},{9,11},{10,... | collective-permute-start | bytes 165896 | tf_op jit(solution)/shard_map/ppermute | solution.py:308
  77.4 13.9 %all-to-all-start.1 = ((f32[32,1,1152]{2,1,0:T(1,128)}), f32[32,1,1152]{2,1,0:T(1,128)S(1)}, u32[]{:S(2)}, u32[]{:S(2)}) async-start(f32[32,1,1152]{2,1,0:T(1,128)} %bitcast.27), calls=%async_computation.1 | async-start | bytes 294912 | tf_op jit(solution)/shard_map/while/body/all_to_all | solution.py:314
  95.4 6.8 %collective-permute-start.2 = (bf16[72,384]{1,0:T(8,128)(2,1)S(1)}, bf16[72,384]{1,0:T(8,128)(2,1)S(1)}, u32[]{:S(2)}, u32[]{:S(2)}) collective-permute-start(bf16[72,384]{1,0:T(8,128)(2,1)S(1)} %update.5.a), channel_id=1, source_target_pairs={{0,1},{1,2},{2,3},{3,0},{4,5},{5,6},{6,7},{7,4},{8,9},{9,10},{10,1... | collective-permute-start | bytes 165896 | tf_op jit(solution)/shard_map/while/body/ppermute | solution.py:308
  95.8 6.4 %collective-permute-start.3 = (bf16[72,384]{1,0:T(8,128)(2,1)S(1)}, bf16[72,384]{1,0:T(8,128)(2,1)S(1)}, u32[]{:S(2)}, u32[]{:S(2)}) collective-permute-start(bf16[72,384]{1,0:T(8,128)(2,1)S(1)} %update.5.a), channel_id=1, source_target_pairs={{0,2},{1,3},{2,0},{3,1},{4,6},{5,7},{6,4},{7,5},{8,10},{9,11},{10,... | collective-permute-start | bytes 165896 | tf_op jit(solution)/shard_map/while/body/ppermute | solution.py:308
  120.7 13.9 %all-to-all-start.1 = ((f32[32,1,1152]{2,1,0:T(1,128)}), f32[32,1,1152]{2,1,0:T(1,128)S(1)}, u32[]{:S(2)}, u32[]{:S(2)}) async-start(f32[32,1,1152]{2,1,0:T(1,128)} %bitcast.27), calls=%async_computation.1 | async-start | bytes 294912 | tf_op jit(solution)/shard_map/while/body/all_to_all | solution.py:314
  138.7 6.5 %collective-permute-start.2 = (bf16[72,384]{1,0:T(8,128)(2,1)S(1)}, bf16[72,384]{1,0:T(8,128)(2,1)S(1)}, u32[]{:S(2)}, u32[]{:S(2)}) collective-permute-start(bf16[72,384]{1,0:T(8,128)(2,1)S(1)} %update.5.a), channel_id=1, source_target_pairs={{0,1},{1,2},{2,3},{3,0},{4,5},{5,6},{6,7},{7,4},{8,9},{9,10},{10,1... | collective-permute-start | bytes 165896 | tf_op jit(solution)/shard_map/while/body/ppermute | solution.py:308
  139.5 5.7 %collective-permute-start.3 = (bf16[72,384]{1,0:T(8,128)(2,1)S(1)}, bf16[72,384]{1,0:T(8,128)(2,1)S(1)}, u32[]{:S(2)}, u32[]{:S(2)}) collective-permute-start(bf16[72,384]{1,0:T(8,128)(2,1)S(1)} %update.5.a), channel_id=1, source_target_pairs={{0,2},{1,3},{2,0},{3,1},{4,6},{5,7},{6,4},{7,5},{8,10},{9,11},{10,... | collective-permute-start | bytes 165896 | tf_op jit(solution)/shard_map/while/body/ppermute | solution.py:308
  141.3 3.9 %collective-permute-start.4 = (bf16[72,384]{1,0:T(8,128)(2,1)S(1)}, bf16[72,384]{1,0:T(8,128)(2,1)S(1)}, u32[]{:S(2)}, u32[]{:S(2)}) collective-permute-start(bf16[72,384]{1,0:T(8,128)(2,1)S(1)} %update.5.a), channel_id=1, source_target_pairs={{0,3},{1,0},{2,1},{3,2},{4,7},{5,4},{6,5},{7,6},{8,11},{9,8},{10,9... | collective-permute-start | bytes 165896 | tf_op jit(solution)/shard_map/while/body/ppermute | solution.py:308
  163.2 13.9 %all-to-all-start.1 = ((f32[32,1,1152]{2,1,0:T(1,128)}), f32[32,1,1152]{2,1,0:T(1,128)S(1)}, u32[]{:S(2)}, u32[]{:S(2)}) async-start(f32[32,1,1152]{2,1,0:T(1,128)} %bitcast.27), calls=%async_computation.1 | async-start | bytes 294912 | tf_op jit(solution)/shard_map/while/body/all_to_all | solution.py:314
  181.2 7.0 %collective-permute-start.2 = (bf16[72,384]{1,0:T(8,128)(2,1)S(1)}, bf16[72,384]{1,0:T(8,128)(2,1)S(1)}, u32[]{:S(2)}, u32[]{:S(2)}) collective-permute-start(bf16[72,384]{1,0:T(8,128)(2,1)S(1)} %update.5.a), channel_id=1, source_target_pairs={{0,1},{1,2},{2,3},{3,0},{4,5},{5,6},{6,7},{7,4},{8,9},{9,10},{10,1... | collective-permute-start | bytes 165896 | tf_op jit(solution)/shard_map/while/body/ppermute | solution.py:308
  181.9 6.2 %collective-permute-start.3 = (bf16[72,384]{1,0:T(8,128)(2,1)S(1)}, bf16[72,384]{1,0:T(8,128)(2,1)S(1)}, u32[]{:S(2)}, u32[]{:S(2)}) collective-permute-start(bf16[72,384]{1,0:T(8,128)(2,1)S(1)} %update.5.a), channel_id=1, source_target_pairs={{0,2},{1,3},{2,0},{3,1},{4,6},{5,7},{6,4},{7,5},{8,10},{9,11},{10,... | collective-permute-start | bytes 165896 | tf_op jit(solution)/shard_map/while/body/ppermute | solution.py:308
  206.3 13.9 %all-to-all-start.1 = ((f32[32,1,1152]{2,1,0:T(1,128)}), f32[32,1,1152]{2,1,0:T(1,128)S(1)}, u32[]{:S(2)}, u32[]{:S(2)}) async-start(f32[32,1,1152]{2,1,0:T(1,128)} %bitcast.27), calls=%async_computation.1 | async-start | bytes 294912 | tf_op jit(solution)/shard_map/while/body/all_to_all | solution.py:314
  224.3 6.5 %collective-permute-start.2 = (bf16[72,384]{1,0:T(8,128)(2,1)S(1)}, bf16[72,384]{1,0:T(8,128)(2,1)S(1)}, u32[]{:S(2)}, u32[]{:S(2)}) collective-permute-start(bf16[72,384]{1,0:T(8,128)(2,1)S(1)} %update.5.a), channel_id=1, source_target_pairs={{0,1},{1,2},{2,3},{3,0},{4,5},{5,6},{6,7},{7,4},{8,9},{9,10},{10,1... | collective-permute-start | bytes 165896 | tf_op jit(solution)/shard_map/while/body/ppermute | solution.py:308
  225.2 5.7 %collective-permute-start.3 = (bf16[72,384]{1,0:T(8,128)(2,1)S(1)}, bf16[72,384]{1,0:T(8,128)(2,1)S(1)}, u32[]{:S(2)}, u32[]{:S(2)}) collective-permute-start(bf16[72,384]{1,0:T(8,128)(2,1)S(1)} %update.5.a), channel_id=1, source_target_pairs={{0,2},{1,3},{2,0},{3,1},{4,6},{5,7},{6,4},{7,5},{8,10},{9,11},{10,... | collective-permute-start | bytes 165896 | tf_op jit(solution)/shard_map/while/body/ppermute | solution.py:308
  249.1 13.9 %all-to-all-start.1 = ((f32[32,1,1152]{2,1,0:T(1,128)}), f32[32,1,1152]{2,1,0:T(1,128)S(1)}, u32[]{:S(2)}, u32[]{:S(2)}) async-start(f32[32,1,1152]{2,1,0:T(1,128)} %bitcast.27), calls=%async_computation.1 | async-start | bytes 294912 | tf_op jit(solution)/shard_map/while/body/all_to_all | solution.py:314
  267.1 6.7 %collective-permute-start.2 = (bf16[72,384]{1,0:T(8,128)(2,1)S(1)}, bf16[72,384]{1,0:T(8,128)(2,1)S(1)}, u32[]{:S(2)}, u32[]{:S(2)}) collective-permute-start(bf16[72,384]{1,0:T(8,128)(2,1)S(1)} %update.5.a), channel_id=1, source_target_pairs={{0,1},{1,2},{2,3},{3,0},{4,5},{5,6},{6,7},{7,4},{8,9},{9,10},{10,1... | collective-permute-start | bytes 165896 | tf_op jit(solution)/shard_map/while/body/ppermute | solution.py:308
  267.9 5.9 %collective-permute-start.3 = (bf16[72,384]{1,0:T(8,128)(2,1)S(1)}, bf16[72,384]{1,0:T(8,128)(2,1)S(1)}, u32[]{:S(2)}, u32[]{:S(2)}) collective-permute-start(bf16[72,384]{1,0:T(8,128)(2,1)S(1)} %update.5.a), channel_id=1, source_target_pairs={{0,2},{1,3},{2,0},{3,1},{4,6},{5,7},{6,4},{7,5},{8,10},{9,11},{10,... | collective-permute-start | bytes 165896 | tf_op jit(solution)/shard_map/while/body/ppermute | solution.py:308
  309.1 6.4 %collective-permute-start.12 = (bf16[72,384]{1,0:T(8,128)(2,1)S(1)}, bf16[72,384]{1,0:T(8,128)(2,1)S(1)}, u32[]{:S(2)}, u32[]{:S(2)}) collective-permute-start(bf16[72,384]{1,0:T(8,128)(2,1)S(1)} %update.4.a), channel_id=1, source_target_pairs={{0,1},{1,2},{2,3},{3,0},{4,5},{5,6},{6,7},{7,4},{8,9},{9,10},{10,1... | collective-permute-start | bytes 165896 | tf_op jit(solution)/shard_map/ppermute | solution.py:308
  309.9 5.6 %collective-permute-start.13 = (bf16[72,384]{1,0:T(8,128)(2,1)S(1)}, bf16[72,384]{1,0:T(8,128)(2,1)S(1)}, u32[]{:S(2)}, u32[]{:S(2)}) collective-permute-start(bf16[72,384]{1,0:T(8,128)(2,1)S(1)} %update.4.a), channel_id=1, source_target_pairs={{0,2},{1,3},{2,0},{3,1},{4,6},{5,7},{6,4},{7,5},{8,10},{9,11},{10,... | collective-permute-start | bytes 165896 | tf_op jit(solution)/shard_map/ppermute | solution.py:308
  331.6 4.6 %collective-permute-start.16 = (f32[16,128]{1,0:T(8,128)S(1)}, f32[16,128]{1,0:T(8,128)S(1)}, u32[]{:S(2)}, u32[]{:S(2)}) collective-permute-start(f32[16,128]{1,0:T(8,128)S(1)} %total.1.mine_ref), channel_id=1, source_target_pairs={{0,4},{4,0},{8,12},{12,8},{16,20},{20,16},{24,28},{28,24},{32,36},... | collective-permute-start | bytes 24584 | tf_op jit(solution)/shard_map/ppermute | solution.py:304
  (24 other events, 98.5 us)

commit v5 on v4

--- a/solution.py
+++ b/solution.py
@@ -128,7 +128,11 @@
 def make_middle(batch, normalised):
     def kernel(core_ref, a, b, c, d, previous_ref, *refs):
         inverse = refs[0][...] if normalised else None
-        tile_ref, keep_ref, send_ref, stepped_ref, mean_ref = refs[-5:]
+        if normalised:
+            tile_ref, keep_ref, send_ref, stepped_ref, mean_ref = refs[1:]
+        else:
+            tiles_ref, keep_ref, send_ref, stepped_ref, mean_ref, tile_ref = refs
+            tile_ref[...] = tiles_ref[tile_ref.shape[0] :, :]
         comps, genes = previous_ref.shape
         parts = (a, b, c, d)
         left = 0.0 if normalised else between_groups(parts, comps, genes, batch)
@@ -142,17 +146,33 @@
     return kernel
 
 
+def lay_out(block):
+    return jnp.concatenate([block[h : h + 8] for h in range(0, 32, 8)], axis=1)
+
+
+def gather_up(rows):
+    return jnp.concatenate([rows[:, w : w + 32] for w in range(0, 128, 32)], axis=0)
+
+
 def make_last(batch):
     def kernel(core_ref, a, b, c, d, previous_ref, inverse_ref, keep_ref, send_ref, stepped_ref):
         stepped = stepped_from((a, b, c, d), previous_ref[...], inverse_ref[...], batch)
         stepped_ref[...] = stepped
         gram = gram_of(stepped)
-        quarter = gram.shape[0] // 4
-        top = jnp.concatenate([gram[:quarter], gram[quarter : 2 * quarter]], axis=1)
-        bottom = jnp.concatenate([gram[2 * quarter : 3 * quarter], gram[3 * quarter :]], axis=1)
+        half = gram.shape[0] // 2
+        rows = lax.broadcasted_iota(jnp.int32, (half, half), 0)
+        columns = lax.broadcasted_iota(jnp.int32, (half, half), 1)
+        upper, lower = gram[:half, :half], gram[half:, half:]
+        corner = lay_out(gram[half:, :half])
+        triangles = lay_out(jnp.where(rows >= columns, upper, lower))
+        diagonal = jnp.sum(jnp.where(rows == columns, lower, 0.0), axis=0, keepdims=True)
+        diagonal = jnp.concatenate([diagonal, jnp.zeros((1, 128 - half), f32)], axis=1)
         first = core_ref[0] == 0
-        keep_ref[...] = jnp.where(first, top, bottom)
-        send_ref[...] = jnp.where(first, bottom, top)
+        nothing = jnp.zeros((1, 128), f32)
+        keep_ref[:8, :] = jnp.where(first, corner, triangles)
+        keep_ref[8:9, :] = jnp.where(first, nothing, diagonal)
+        send_ref[:8, :] = jnp.where(first, triangles, corner)
+        send_ref[8:9, :] = jnp.where(first, diagonal, nothing)
 
     return kernel
 
@@ -180,7 +200,8 @@
             for j in range(rows - 1)
         ]
         scores = jnp.concatenate(chunks, axis=1)
-        both = lax.dot_general(split_pair(scores), tile_ref[...], NN, preferred_element_type=f32)
+        tile = tile_ref[: scores.shape[1], :]
+        both = lax.dot_general(split_pair(scores), tile, NN, preferred_element_type=f32)
         totals = jnp.sum(scores, axis=1, keepdims=True)
         mean = mean_ref[...] * (1.0 / cells) if cells else mean_ref[...]
         raw = both[:comps] + both[comps:] - totals * mean
@@ -255,20 +276,44 @@
 
 
 def copies_kernel(a, b, out_ref):
-    out_ref[...] = jnp.broadcast_to((a[...] + b[...])[None], out_ref.shape)
+    rows = a.shape[0]
+    count = out_ref.shape[0] // rows
+    total = a[...] + b[...]
+    for j in range(rows):
+        out_ref[pl.ds(j, count, stride=rows), :] = jnp.broadcast_to(total[j : j + 1], (count, 128))
 
 
 def total_kernel(in_ref, out_ref):
-    out_ref[...] = jnp.sum(in_ref[...], axis=0)
+    rows = out_ref.shape[0]
+    count = in_ref.shape[0] // rows
+    for j in range(rows):
+        out_ref[j : j + 1, :] = jnp.sum(in_ref[pl.ds(j, count, stride=rows), :], axis=0, keepdims=True)
 
 
 def make_finish(scale):
     def kernel(core_ref, mine_ref, other_ref, stepped_ref, out_ref):
-        comps = stepped_ref.shape[0]
-        total = by_core(core_ref[0] == 0, mine_ref[...], other_ref[...])
-        quarter = comps // 4
+        first = core_ref[0] == 0
+        corner = gather_up(jnp.where(first, mine_ref[:8, :], other_ref[:8, :]))
+        triangles = gather_up(jnp.where(first, other_ref[:8, :], mine_ref[:8, :]))
+        half = corner.shape[0]
+        diagonal = jnp.where(first, other_ref[8:9, :half], mine_ref[8:9, :half])
+        rows = lax.broadcasted_iota(jnp.int32, (half, half), 0)
+        columns = lax.broadcasted_iota(jnp.int32, (half, half), 1)
+        eye = jnp.where(rows == columns, 1.0, 0.0).astype(f32)
+
+        def turned(block):
+            return lax.dot_general(block, eye, (((0,), (0,)), ((), ())), precision=HIGH, preferred_element_type=f32)
+
+        across = turned(triangles)
+        upper = jnp.where(rows >= columns, triangles, across)
+        lower = jnp.where(rows < columns, triangles, across)
+        lower = jnp.where(rows == columns, jnp.broadcast_to(diagonal, (half, half)), lower)
         gram = jnp.concatenate(
-            [total[h : h + quarter, w : w + comps] for h in (0, quarter) for w in (0, comps)], axis=0
+            [
+                jnp.concatenate([upper, turned(corner)], axis=1),
+                jnp.concatenate([corner, lower], axis=1),
+            ],
+            axis=0,
         )
         out_ref[...] = scale * lax.dot_general(
             inverse_factor(gram), stepped_ref[...], NN, precision=HIGH, preferred_element_type=f32
@@ -353,10 +398,10 @@
         return vmem_call(make_factor(half, rows), square, 2, flops=10**9, name="factor")(core, mine, other)
 
     def advance(parts, stepped, inverse, next_tile):
-        inputs = [*parts, stepped, *inverse, next_tile]
-        return vmem_call(
-            make_middle(batch, bool(inverse)), (packed, packed, local, row), len(inputs), name="middle"
-        )(core, *inputs)
+        inputs = [*parts, stepped, inverse, next_tile]
+        return vmem_call(make_middle(batch, True), (packed, packed, local, row), len(inputs), name="middle")(
+            core, *inputs
+        )
 
     def one_step(state):
         step, keep, send, stepped, mean, tile = state
@@ -366,27 +411,32 @@
         mine, other, picks = scores_of(keep, send, picks)
         next_tile = tile_of(picks)
         parts = change_of(mine, other, tile, mean, sums_of(next_tile))
-        inverse = (factor_of(mine, other),)
+        inverse = factor_of(mine, other)
         return (following, *advance(parts, stepped, inverse, next_tile), next_tile)
 
     mine, other, picks = scores_of(keep, send, chosen[:2])
-    tile, next_tile = jnp.split(tile_of(picks.reshape(-1)), 2)
-    parts = change_of(mine, other, tile, sums_of(tile), sums_of(next_tile), cells)
-    state = (*advance(parts, loadings_init, (), next_tile), next_tile)
+    tiles = tile_of(picks.reshape(-1))
+    both_sums = jnp.sum(tiles.reshape(2, cells, genes), axis=1, dtype=f32)
+    parts = change_of(mine, other, tiles, both_sums[:1], both_sums[1:], cells)
+    state = vmem_call(
+        make_middle(batch, False),
+        (packed, packed, local, row, jax.ShapeDtypeStruct((cells, genes), bf16)),
+        len(parts) + 2,
+        name="middle",
+    )(core, *parts, loadings_init, tiles)
     _, keep, send, stepped, mean, tile = lax.while_loop(
         lambda state: state[0] < steps - 1, one_step, (jnp.int32(1), *state)
     )
     mine, other, _ = scores_of(keep, send, ())
     parts = change_of(mine, other, tile, mean, mean)
     inverse = factor_of(mine, other)
-    few = jax.ShapeDtypeStruct((comps // 4, 2 * comps), f32)
-    many = jax.ShapeDtypeStruct((chips, comps // 4, 2 * comps), f32)
+    few = jax.ShapeDtypeStruct((9, 128), f32)
+    many = jax.ShapeDtypeStruct((9 * chips, 128), f32)
     keep, send, stepped = vmem_call(make_last(batch), (few, few, local), len(parts) + 2, name="last")(
         core, *parts, stepped, inverse
     )
     copies = vmem_call(copies_kernel, many, 2, name="copies", core=False)(keep, swap_cores(send))
-    came = lax.all_to_all(copies, "gene", 0, 0, tiled=True, axis_index_groups=same_core)
-    mine = vmem_call(total_kernel, few, 1, name="total", core=False)(came)
+    mine = vmem_call(total_kernel, few, 1, name="total", core=False)(exchange(copies))
     scale = math.sqrt(genes * gene_devices)
     return vmem_call(make_finish(scale), local, 3, name="finish", held=False)(
         core, mine, swap_cores(mine), stepped

time: 341 us -> 344 us (level)
  local copies, waits for them, and re-layouts: 45.6 us -> 49.9 us
    all_to_all x1 -> x0, blocking collectives: 12.9 us -> none  [shards(): lax.all_to_all(copies, 'gene', 0, 0, tiled=True, axis_index_groups=same_c...]
    all_to_all x7 -> x8, blocking collectives: 103 us -> 115 us  [exchange(): lax.all_to_all(pieces, 'gene', 0, 0, tiled=True, axis_index_groups=same_c...]
    while x10 -> x20, local copies, waits for them, and re-layouts: 0.44 us -> 4.5 us
  transfers between devices with their start and end apart: 44 -> 44, of which waited for: 27 -> 24; matrix products, arithmetic and copies ran while one was open for 13% -> 14% of each run, Pallas kernels for 5% -> 5%
where the time goes in v5:
time: 344 us; the launch traced here: 343 us
  blocking collectives  115 us (33%)
  starting transfers between devices  98.5 us (29%)
  local copies, waits for them, and re-layouts  49.9 us (15%)
  Pallas kernels  38.9 us (11%)
  waiting for transfers between devices  38.6 us (11%)
    all_to_all x8, blocking collectives, exchange(): lax.all_to_all(pieces, 'gene', 0, 0, tiled=True, axis_index_groups=same_c...  115 us
    gather x6, local copies, waits for them, and re-layouts, tile_of(): return jnp.take(pool_by_cell, picks, axis=0, mode='clip')  40.2 us
    pallas_call x38, Pallas kernels, run(): return call(*args[:core], *near, *args[last:])  38.9 us
    all_to_all x7, starting transfers between devices, exchange(): lax.all_to_all(pieces, 'gene', 0, 0, tiled=True, axis_index_groups=same_c...  37.4 us
    ppermute x16, starting transfers between devices, swap_cores(): lax.ppermute(value, 'gene', [(i, i ^ 1) for i in range(gene_devices)])  33.9 us
    ppermute x21, starting transfers between devices, round_cells(): lax.ppermute(value, 'cell', [(i, (i + k) % cell_devices) for i in range(c...  27.2 us
    all_to_all x7, waiting for transfers between devices, exchange(): lax.all_to_all(pieces, 'gene', 0, 0, tiled=True, axis_index_groups=same_c...  21.4 us
    ppermute x16, waiting for transfers between devices, swap_cores(): lax.ppermute(value, 'gene', [(i, i ^ 1) for i in range(gene_devices)])  14.9 us
  transfers between devices with their start and end apart: 44, of which 24 were waited for; matrix products, arithmetic and copies ran while one was open for 14% of the time, Pallas kernels for 5%

profile of v5, /device:TPU:1, one launch (start us, length us, event | category | flops | bytes accessed | tf_op | source)
XLA Modules:
  0.0 343.2 jit_solution(4758723334026707912)
XLA Ops:
  0.0 4.8 %first.1 = (f32[288,128]{1,0:T(8,128)S(1)}, f32[288,128]{1,0:T(8,128)S(1)}) custom-call(s32[1]{0:T(128)} %bitcast.5.core_ref, s32[1]{0:T(128)} %bitcast.6.cell_ref, f32[64,320]{1,0:T(8,128)} %previous_ref.1, s32[7,1024]{1,0:T(8,128)} %picks_ref.1, bf16[320,4096]{1,0:T(8,128)(2,1)} %pool_ref.1), custom_call_target="tpu_custom_call" | custom-call | tf_op jit(solution)/shard_map/first/pallas_call | solution.py:35
  9.8 9.3 %all-to-all-start.2 = ((f32[32,1,1152]{2,1,0:T(1,128)}), f32[32,1,1152]{2,1,0:T(1,128)S(1)}, u32[]{:S(2)}, u32[]{:S(2)}) async-start(f32[32,1,1152]{2,1,0:T(1,128)} %bitcast.7), calls=%async_computation.2 | async-start | bytes 294912 | tf_op jit(solution)/shard_map/all_to_all | solution.py:359
  22.0 6.4 %all-to-all-done.2 = f32[32,1,1152]{2,1,0:T(1,128)S(1)} async-done(((f32[32,1,1152]{2,1,0:T(1,128)}), f32[32,1,1152]{2,1,0:T(1,128)S(1)}, u32[]{:S(2)}, u32[]{:S(2)}) %all-to-all-start.2) | async-done | bytes 147488 | tf_op jit(solution)/shard_map/all_to_all | solution.py:359
  29.0 4.7 %all-to-all-start.3 = ((f32[32,1,1152]{2,1,0:T(1,128)}), f32[32,1,1152]{2,1,0:T(1,128)S(1)}, u32[]{:S(2)}, u32[]{:S(2)}) async-start(f32[32,1,1152]{2,1,0:T(1,128)} %bitcast.9), calls=%async_computation.3 | async-start | bytes 294912 | tf_op jit(solution)/shard_map/all_to_all | solution.py:359
  33.7 9.5 %gather_fusion.1 = bf16[2048,320]{1,0:T(8,128)(2,1)S(1)} fusion(bf16[4096,320]{1,0:T(8,128)(2,1)} %bitcast.50, s32[2048]{0:T(1024)S(1)} %bitcast_clamp_fusion), kind=kCustom, calls=%fused_computation.1 | custom fusion | bytes 2629632 | tf_op jit(solution)/shard_map/jit(_take)/gather | solution.py:343
  57.2 222.0 %while.20 = (s32[]{:T(128)}, f32[288,128]{1,0:T(8,128)S(1)}, f32[288,128]{1,0:T(8,128)S(1)}, f32[64,320]{1,0:T(8,128)S(1)}, f32[1,320]{1,0:T(1,128)S(1)}, /*inde...) while((s32[]{:T(128)}, f32[288,128]{1,0:T(8,128)S(1)}, ...), condition=%wide.region_3.4_spmd, body=%wide.region_1.3_spmd.sunk | while | flops 1000656064 | bytes 8667303 | solution.py:427
  60.1 17.9 %all_to_all.46 = f32[32,1,1152]{2,1,0:T(1,128)S(1)} all-to-all(f32[32,1,1152]{2,1,0:T(1,128)S(1)} %bitcast.37), channel_id=1, replica_groups={{0,8,16,24,32,40,48,56,64,72,80,88,96,104,112,120,128,136,144,152,160,1..., dimensions={0} | all-to-all | bytes 294912 | tf_op jit(solution)/shard_map/while/body/all_to_all | solution.py:359
  78.7 4.7 %all-to-all-start.1 = ((f32[32,1,1152]{2,1,0:T(1,128)}), f32[32,1,1152]{2,1,0:T(1,128)S(1)}, u32[]{:S(2)}, u32[]{:S(2)}) async-start(f32[32,1,1152]{2,1,0:T(1,128)} %bitcast.32), calls=%async_computation.1 | async-start | bytes 294912 | tf_op jit(solution)/shard_map/while/body/all_to_all | solution.py:359
  83.4 6.1 %gather_fusion = bf16[1024,320]{1,0:T(8,128)(2,1)S(1)} fusion(bf16[4096,320]{1,0:T(8,128)(2,1)} %get-tuple-element.285, s32[1024]{0:T(1024)S(1)} %broadcast_clamp_fusion.2), kind=kCustom, calls=%fused_computation.clone.1 | custom fusion | bytes 1314816 | tf_op jit(solution)/shard_map/while/body/jit(_take)/gather | solution.py:343
  107.2 14.3 %all_to_all.46 = f32[32,1,1152]{2,1,0:T(1,128)S(1)} all-to-all(f32[32,1,1152]{2,1,0:T(1,128)S(1)} %bitcast.37), channel_id=1, replica_groups={{0,8,16,24,32,40,48,56,64,72,80,88,96,104,112,120,128,136,144,152,160,1..., dimensions={0} | all-to-all | bytes 294912 | tf_op jit(solution)/shard_map/while/body/all_to_all | solution.py:359
  122.1 4.7 %all-to-all-start.1 = ((f32[32,1,1152]{2,1,0:T(1,128)}), f32[32,1,1152]{2,1,0:T(1,128)S(1)}, u32[]{:S(2)}, u32[]{:S(2)}) async-start(f32[32,1,1152]{2,1,0:T(1,128)} %bitcast.32), calls=%async_computation.1 | async-start | bytes 294912 | tf_op jit(solution)/shard_map/while/body/all_to_all | solution.py:359
  126.9 6.1 %gather_fusion = bf16[1024,320]{1,0:T(8,128)(2,1)S(1)} fusion(bf16[4096,320]{1,0:T(8,128)(2,1)} %get-tuple-element.285, s32[1024]{0:T(1024)S(1)} %broadcast_clamp_fusion.2), kind=kCustom, calls=%fused_computation.clone.1 | custom fusion | bytes 1314816 | tf_op jit(solution)/shard_map/while/body/jit(_take)/gather | solution.py:343
  151.0 14.3 %all_to_all.46 = f32[32,1,1152]{2,1,0:T(1,128)S(1)} all-to-all(f32[32,1,1152]{2,1,0:T(1,128)S(1)} %bitcast.37), channel_id=1, replica_groups={{0,8,16,24,32,40,48,56,64,72,80,88,96,104,112,120,128,136,144,152,160,1..., dimensions={0} | all-to-all | bytes 294912 | tf_op jit(solution)/shard_map/while/body/all_to_all | solution.py:359
  165.9 4.7 %all-to-all-start.1 = ((f32[32,1,1152]{2,1,0:T(1,128)}), f32[32,1,1152]{2,1,0:T(1,128)S(1)}, u32[]{:S(2)}, u32[]{:S(2)}) async-start(f32[32,1,1152]{2,1,0:T(1,128)} %bitcast.32), calls=%async_computation.1 | async-start | bytes 294912 | tf_op jit(solution)/shard_map/while/body/all_to_all | solution.py:359
  170.6 6.1 %gather_fusion = bf16[1024,320]{1,0:T(8,128)(2,1)S(1)} fusion(bf16[4096,320]{1,0:T(8,128)(2,1)} %get-tuple-element.285, s32[1024]{0:T(1024)S(1)} %broadcast_clamp_fusion.2), kind=kCustom, calls=%fused_computation.clone.1 | custom fusion | bytes 1314816 | tf_op jit(solution)/shard_map/while/body/jit(_take)/gather | solution.py:343
  194.4 14.3 %all_to_all.46 = f32[32,1,1152]{2,1,0:T(1,128)S(1)} all-to-all(f32[32,1,1152]{2,1,0:T(1,128)S(1)} %bitcast.37), channel_id=1, replica_groups={{0,8,16,24,32,40,48,56,64,72,80,88,96,104,112,120,128,136,144,152,160,1..., dimensions={0} | all-to-all | bytes 294912 | tf_op jit(solution)/shard_map/while/body/all_to_all | solution.py:359
  209.3 4.7 %all-to-all-start.1 = ((f32[32,1,1152]{2,1,0:T(1,128)}), f32[32,1,1152]{2,1,0:T(1,128)S(1)}, u32[]{:S(2)}, u32[]{:S(2)}) async-start(f32[32,1,1152]{2,1,0:T(1,128)} %bitcast.32), calls=%async_computation.1 | async-start | bytes 294912 | tf_op jit(solution)/shard_map/while/body/all_to_all | solution.py:359
  214.0 6.1 %gather_fusion = bf16[1024,320]{1,0:T(8,128)(2,1)S(1)} fusion(bf16[4096,320]{1,0:T(8,128)(2,1)} %get-tuple-element.285, s32[1024]{0:T(1024)S(1)} %broadcast_clamp_fusion.2), kind=kCustom, calls=%fused_computation.clone.1 | custom fusion | bytes 1314816 | tf_op jit(solution)/shard_map/while/body/jit(_take)/gather | solution.py:343
  238.1 14.3 %all_to_all.46 = f32[32,1,1152]{2,1,0:T(1,128)S(1)} all-to-all(f32[32,1,1152]{2,1,0:T(1,128)S(1)} %bitcast.37), channel_id=1, replica_groups={{0,8,16,24,32,40,48,56,64,72,80,88,96,104,112,120,128,136,144,152,160,1..., dimensions={0} | all-to-all | bytes 294912 | tf_op jit(solution)/shard_map/while/body/all_to_all | solution.py:359
  253.1 4.7 %all-to-all-start.1 = ((f32[32,1,1152]{2,1,0:T(1,128)}), f32[32,1,1152]{2,1,0:T(1,128)S(1)}, u32[]{:S(2)}, u32[]{:S(2)}) async-start(f32[32,1,1152]{2,1,0:T(1,128)} %bitcast.32), calls=%async_computation.1 | async-start | bytes 294912 | tf_op jit(solution)/shard_map/while/body/all_to_all | solution.py:359
  257.8 6.1 %gather_fusion = bf16[1024,320]{1,0:T(8,128)(2,1)S(1)} fusion(bf16[4096,320]{1,0:T(8,128)(2,1)} %get-tuple-element.285, s32[1024]{0:T(1024)S(1)} %broadcast_clamp_fusion.2), kind=kCustom, calls=%fused_computation.clone.1 | custom fusion | bytes 1314816 | tf_op jit(solution)/shard_map/while/body/jit(_take)/gather | solution.py:343
  281.5 14.3 %all_to_all.43 = f32[32,1,1152]{2,1,0:T(1,128)S(1)} all-to-all(f32[32,1,1152]{2,1,0:T(1,128)S(1)} %bitcast.42), channel_id=1, replica_groups={{0,8,16,24,32,40,48,56,64,72,80,88,96,104,112,120,128,136,144,152,160,1..., dimensions={0} | all-to-all | bytes 294912 | tf_op jit(solution)/shard_map/all_to_all | solution.py:359
  295.8 13.7 %all_to_all.44 = f32[32,1,1152]{2,1,0:T(1,128)S(1)} all-to-all(f32[32,1,1152]{2,1,0:T(1,128)S(1)} %bitcast.46), channel_id=1, replica_groups={{0,8,16,24,32,40,48,56,64,72,80,88,96,104,112,120,128,136,144,152,160,1..., dimensions={0} | all-to-all | bytes 294912 | tf_op jit(solution)/shard_map/all_to_all | solution.py:359
  323.2 12.5 %all_to_all.45 = f32[32,1,1152]{2,1,0:T(1,128)S(1)} all-to-all(f32[32,1,1152]{2,1,0:T(1,128)S(1)} %bitcast.44), channel_id=1, replica_groups={{0,8,16,24,32,40,48,56,64,72,80,88,96,104,112,120,128,136,144,152,160,1..., dimensions={0} | all-to-all | bytes 294912 | tf_op jit(solution)/shard_map/all_to_all | solution.py:359
  (177 shorter events, 138.4 us)
Async XLA Ops:
  9.8 18.5 %all-to-all-start.2 = ((f32[32,1,1152]{2,1,0:T(1,128)}), f32[32,1,1152]{2,1,0:T(1,128)S(1)}, u32[]{:S(2)}, u32[]{:S(2)}) async-start(f32[32,1,1152]{2,1,0:T(1,128)} %bitcast.7), calls=%async_computation.2 | async-start | bytes 294912 | tf_op jit(solution)/shard_map/all_to_all | solution.py:359
  29.0 14.5 %all-to-all-start.3 = ((f32[32,1,1152]{2,1,0:T(1,128)}), f32[32,1,1152]{2,1,0:T(1,128)S(1)}, u32[]{:S(2)}, u32[]{:S(2)}) async-start(f32[32,1,1152]{2,1,0:T(1,128)} %bitcast.9), calls=%async_computation.3 | async-start | bytes 294912 | tf_op jit(solution)/shard_map/all_to_all | solution.py:359
  47.0 5.1 %collective-permute-start.7 = (bf16[72,384]{1,0:T(8,128)(2,1)S(1)}, bf16[72,384]{1,0:T(8,128)(2,1)S(1)}, u32[]{:S(2)}, u32[]{:S(2)}) collective-permute-start(bf16[72,384]{1,0:T(8,128)(2,1)S(1)} %update.3.a), channel_id=1, source_target_pairs={{0,1},{1,2},{2,3},{3,0},{4,5},{5,6},{6,7},{7,4},{8,9},{9,10},{10,1... | collective-permute-start | bytes 165896 | tf_op jit(solution)/shard_map/ppermute | solution.py:353
  48.4 5.1 %collective-permute-start.8 = (bf16[72,384]{1,0:T(8,128)(2,1)S(1)}, bf16[72,384]{1,0:T(8,128)(2,1)S(1)}, u32[]{:S(2)}, u32[]{:S(2)}) collective-permute-start(bf16[72,384]{1,0:T(8,128)(2,1)S(1)} %update.3.a), channel_id=1, source_target_pairs={{0,2},{1,3},{2,0},{3,1},{4,6},{5,7},{6,4},{7,5},{8,10},{9,11},{10,... | collective-permute-start | bytes 165896 | tf_op jit(solution)/shard_map/ppermute | solution.py:353
  78.7 13.9 %all-to-all-start.1 = ((f32[32,1,1152]{2,1,0:T(1,128)}), f32[32,1,1152]{2,1,0:T(1,128)S(1)}, u32[]{:S(2)}, u32[]{:S(2)}) async-start(f32[32,1,1152]{2,1,0:T(1,128)} %bitcast.32), calls=%async_computation.1 | async-start | bytes 294912 | tf_op jit(solution)/shard_map/while/body/all_to_all | solution.py:359
  96.7 7.5 %collective-permute-start.2 = (bf16[72,384]{1,0:T(8,128)(2,1)S(1)}, bf16[72,384]{1,0:T(8,128)(2,1)S(1)}, u32[]{:S(2)}, u32[]{:S(2)}) collective-permute-start(bf16[72,384]{1,0:T(8,128)(2,1)S(1)} %update.5.a), channel_id=1, source_target_pairs={{0,1},{1,2},{2,3},{3,0},{4,5},{5,6},{6,7},{7,4},{8,9},{9,10},{10,1... | collective-permute-start | bytes 165896 | tf_op jit(solution)/shard_map/while/body/ppermute | solution.py:353
  96.8 7.4 %collective-permute-start.3 = (bf16[72,384]{1,0:T(8,128)(2,1)S(1)}, bf16[72,384]{1,0:T(8,128)(2,1)S(1)}, u32[]{:S(2)}, u32[]{:S(2)}) collective-permute-start(bf16[72,384]{1,0:T(8,128)(2,1)S(1)} %update.5.a), channel_id=1, source_target_pairs={{0,2},{1,3},{2,0},{3,1},{4,6},{5,7},{6,4},{7,5},{8,10},{9,11},{10,... | collective-permute-start | bytes 165896 | tf_op jit(solution)/shard_map/while/body/ppermute | solution.py:353
  122.1 13.9 %all-to-all-start.1 = ((f32[32,1,1152]{2,1,0:T(1,128)}), f32[32,1,1152]{2,1,0:T(1,128)S(1)}, u32[]{:S(2)}, u32[]{:S(2)}) async-start(f32[32,1,1152]{2,1,0:T(1,128)} %bitcast.32), calls=%async_computation.1 | async-start | bytes 294912 | tf_op jit(solution)/shard_map/while/body/all_to_all | solution.py:359
  140.2 8.0 %collective-permute-start.2 = (bf16[72,384]{1,0:T(8,128)(2,1)S(1)}, bf16[72,384]{1,0:T(8,128)(2,1)S(1)}, u32[]{:S(2)}, u32[]{:S(2)}) collective-permute-start(bf16[72,384]{1,0:T(8,128)(2,1)S(1)} %update.5.a), channel_id=1, source_target_pairs={{0,1},{1,2},{2,3},{3,0},{4,5},{5,6},{6,7},{7,4},{8,9},{9,10},{10,1... | collective-permute-start | bytes 165896 | tf_op jit(solution)/shard_map/while/body/ppermute | solution.py:353
  141.8 6.4 %collective-permute-start.3 = (bf16[72,384]{1,0:T(8,128)(2,1)S(1)}, bf16[72,384]{1,0:T(8,128)(2,1)S(1)}, u32[]{:S(2)}, u32[]{:S(2)}) collective-permute-start(bf16[72,384]{1,0:T(8,128)(2,1)S(1)} %update.5.a), channel_id=1, source_target_pairs={{0,2},{1,3},{2,0},{3,1},{4,6},{5,7},{6,4},{7,5},{8,10},{9,11},{10,... | collective-permute-start | bytes 165896 | tf_op jit(solution)/shard_map/while/body/ppermute | solution.py:353
  142.5 5.7 %collective-permute-start.4 = (bf16[72,384]{1,0:T(8,128)(2,1)S(1)}, bf16[72,384]{1,0:T(8,128)(2,1)S(1)}, u32[]{:S(2)}, u32[]{:S(2)}) collective-permute-start(bf16[72,384]{1,0:T(8,128)(2,1)S(1)} %update.5.a), channel_id=1, source_target_pairs={{0,3},{1,0},{2,1},{3,2},{4,7},{5,4},{6,5},{7,6},{8,11},{9,8},{10,9... | collective-permute-start | bytes 165896 | tf_op jit(solution)/shard_map/while/body/ppermute | solution.py:353
  165.9 13.9 %all-to-all-start.1 = ((f32[32,1,1152]{2,1,0:T(1,128)}), f32[32,1,1152]{2,1,0:T(1,128)S(1)}, u32[]{:S(2)}, u32[]{:S(2)}) async-start(f32[32,1,1152]{2,1,0:T(1,128)} %bitcast.32), calls=%async_computation.1 | async-start | bytes 294912 | tf_op jit(solution)/shard_map/while/body/all_to_all | solution.py:359
  183.9 7.4 %collective-permute-start.2 = (bf16[72,384]{1,0:T(8,128)(2,1)S(1)}, bf16[72,384]{1,0:T(8,128)(2,1)S(1)}, u32[]{:S(2)}, u32[]{:S(2)}) collective-permute-start(bf16[72,384]{1,0:T(8,128)(2,1)S(1)} %update.5.a), channel_id=1, source_target_pairs={{0,1},{1,2},{2,3},{3,0},{4,5},{5,6},{6,7},{7,4},{8,9},{9,10},{10,1... | collective-permute-start | bytes 165896 | tf_op jit(solution)/shard_map/while/body/ppermute | solution.py:353
  184.0 7.3 %collective-permute-start.3 = (bf16[72,384]{1,0:T(8,128)(2,1)S(1)}, bf16[72,384]{1,0:T(8,128)(2,1)S(1)}, u32[]{:S(2)}, u32[]{:S(2)}) collective-permute-start(bf16[72,384]{1,0:T(8,128)(2,1)S(1)} %update.5.a), channel_id=1, source_target_pairs={{0,2},{1,3},{2,0},{3,1},{4,6},{5,7},{6,4},{7,5},{8,10},{9,11},{10,... | collective-permute-start | bytes 165896 | tf_op jit(solution)/shard_map/while/body/ppermute | solution.py:353
  209.3 13.9 %all-to-all-start.1 = ((f32[32,1,1152]{2,1,0:T(1,128)}), f32[32,1,1152]{2,1,0:T(1,128)S(1)}, u32[]{:S(2)}, u32[]{:S(2)}) async-start(f32[32,1,1152]{2,1,0:T(1,128)} %bitcast.32), calls=%async_computation.1 | async-start | bytes 294912 | tf_op jit(solution)/shard_map/while/body/all_to_all | solution.py:359
  227.4 7.7 %collective-permute-start.2 = (bf16[72,384]{1,0:T(8,128)(2,1)S(1)}, bf16[72,384]{1,0:T(8,128)(2,1)S(1)}, u32[]{:S(2)}, u32[]{:S(2)}) collective-permute-start(bf16[72,384]{1,0:T(8,128)(2,1)S(1)} %update.5.a), channel_id=1, source_target_pairs={{0,1},{1,2},{2,3},{3,0},{4,5},{5,6},{6,7},{7,4},{8,9},{9,10},{10,1... | collective-permute-start | bytes 165896 | tf_op jit(solution)/shard_map/while/body/ppermute | solution.py:353
  227.9 7.2 %collective-permute-start.3 = (bf16[72,384]{1,0:T(8,128)(2,1)S(1)}, bf16[72,384]{1,0:T(8,128)(2,1)S(1)}, u32[]{:S(2)}, u32[]{:S(2)}) collective-permute-start(bf16[72,384]{1,0:T(8,128)(2,1)S(1)} %update.5.a), channel_id=1, source_target_pairs={{0,2},{1,3},{2,0},{3,1},{4,6},{5,7},{6,4},{7,5},{8,10},{9,11},{10,... | collective-permute-start | bytes 165896 | tf_op jit(solution)/shard_map/while/body/ppermute | solution.py:353
  229.8 5.3 %collective-permute-start.4 = (bf16[72,384]{1,0:T(8,128)(2,1)S(1)}, bf16[72,384]{1,0:T(8,128)(2,1)S(1)}, u32[]{:S(2)}, u32[]{:S(2)}) collective-permute-start(bf16[72,384]{1,0:T(8,128)(2,1)S(1)} %update.5.a), channel_id=1, source_target_pairs={{0,3},{1,0},{2,1},{3,2},{4,7},{5,4},{6,5},{7,6},{8,11},{9,8},{10,9... | collective-permute-start | bytes 165896 | tf_op jit(solution)/shard_map/while/body/ppermute | solution.py:353
  253.1 13.9 %all-to-all-start.1 = ((f32[32,1,1152]{2,1,0:T(1,128)}), f32[32,1,1152]{2,1,0:T(1,128)S(1)}, u32[]{:S(2)}, u32[]{:S(2)}) async-start(f32[32,1,1152]{2,1,0:T(1,128)} %bitcast.32), calls=%async_computation.1 | async-start | bytes 294912 | tf_op jit(solution)/shard_map/while/body/all_to_all | solution.py:359
  271.1 7.4 %collective-permute-start.2 = (bf16[72,384]{1,0:T(8,128)(2,1)S(1)}, bf16[72,384]{1,0:T(8,128)(2,1)S(1)}, u32[]{:S(2)}, u32[]{:S(2)}) collective-permute-start(bf16[72,384]{1,0:T(8,128)(2,1)S(1)} %update.5.a), channel_id=1, source_target_pairs={{0,1},{1,2},{2,3},{3,0},{4,5},{5,6},{6,7},{7,4},{8,9},{9,10},{10,1... | collective-permute-start | bytes 165896 | tf_op jit(solution)/shard_map/while/body/ppermute | solution.py:353
  271.3 7.2 %collective-permute-start.3 = (bf16[72,384]{1,0:T(8,128)(2,1)S(1)}, bf16[72,384]{1,0:T(8,128)(2,1)S(1)}, u32[]{:S(2)}, u32[]{:S(2)}) collective-permute-start(bf16[72,384]{1,0:T(8,128)(2,1)S(1)} %update.5.a), channel_id=1, source_target_pairs={{0,2},{1,3},{2,0},{3,1},{4,6},{5,7},{6,4},{7,5},{8,10},{9,11},{10,... | collective-permute-start | bytes 165896 | tf_op jit(solution)/shard_map/while/body/ppermute | solution.py:353
  273.5 5.0 %collective-permute-start.4 = (bf16[72,384]{1,0:T(8,128)(2,1)S(1)}, bf16[72,384]{1,0:T(8,128)(2,1)S(1)}, u32[]{:S(2)}, u32[]{:S(2)}) collective-permute-start(bf16[72,384]{1,0:T(8,128)(2,1)S(1)} %update.5.a), channel_id=1, source_target_pairs={{0,3},{1,0},{2,1},{3,2},{4,7},{5,4},{6,5},{7,6},{8,11},{9,8},{10,9... | collective-permute-start | bytes 165896 | tf_op jit(solution)/shard_map/while/body/ppermute | solution.py:353
  313.6 6.9 %collective-permute-start.12 = (bf16[72,384]{1,0:T(8,128)(2,1)S(1)}, bf16[72,384]{1,0:T(8,128)(2,1)S(1)}, u32[]{:S(2)}, u32[]{:S(2)}) collective-permute-start(bf16[72,384]{1,0:T(8,128)(2,1)S(1)} %update.4.a), channel_id=1, source_target_pairs={{0,1},{1,2},{2,3},{3,0},{4,5},{5,6},{6,7},{7,4},{8,9},{9,10},{10,1... | collective-permute-start | bytes 165896 | tf_op jit(solution)/shard_map/ppermute | solution.py:353
  314.1 6.4 %collective-permute-start.13 = (bf16[72,384]{1,0:T(8,128)(2,1)S(1)}, bf16[72,384]{1,0:T(8,128)(2,1)S(1)}, u32[]{:S(2)}, u32[]{:S(2)}) collective-permute-start(bf16[72,384]{1,0:T(8,128)(2,1)S(1)} %update.4.a), channel_id=1, source_target_pairs={{0,2},{1,3},{2,0},{3,1},{4,6},{5,7},{6,4},{7,5},{8,10},{9,11},{10,... | collective-permute-start | bytes 165896 | tf_op jit(solution)/shard_map/ppermute | solution.py:353
  (32 other events, 204.5 us)

commit v6 on v5

--- a/solution.py
+++ b/solution.py
@@ -128,11 +128,7 @@
 def make_middle(batch, normalised):
     def kernel(core_ref, a, b, c, d, previous_ref, *refs):
         inverse = refs[0][...] if normalised else None
-        if normalised:
-            tile_ref, keep_ref, send_ref, stepped_ref, mean_ref = refs[1:]
-        else:
-            tiles_ref, keep_ref, send_ref, stepped_ref, mean_ref, tile_ref = refs
-            tile_ref[...] = tiles_ref[tile_ref.shape[0] :, :]
+        tile_ref, keep_ref, send_ref, stepped_ref, mean_ref = refs[-5:]
         comps, genes = previous_ref.shape
         parts = (a, b, c, d)
         left = 0.0 if normalised else between_groups(parts, comps, genes, batch)
@@ -200,8 +196,7 @@
             for j in range(rows - 1)
         ]
         scores = jnp.concatenate(chunks, axis=1)
-        tile = tile_ref[: scores.shape[1], :]
-        both = lax.dot_general(split_pair(scores), tile, NN, preferred_element_type=f32)
+        both = lax.dot_general(split_pair(scores), tile_ref[...], NN, preferred_element_type=f32)
         totals = jnp.sum(scores, axis=1, keepdims=True)
         mean = mean_ref[...] * (1.0 / cells) if cells else mean_ref[...]
         raw = both[:comps] + both[comps:] - totals * mean
@@ -398,10 +393,10 @@
         return vmem_call(make_factor(half, rows), square, 2, flops=10**9, name="factor")(core, mine, other)
 
     def advance(parts, stepped, inverse, next_tile):
-        inputs = [*parts, stepped, inverse, next_tile]
-        return vmem_call(make_middle(batch, True), (packed, packed, local, row), len(inputs), name="middle")(
-            core, *inputs
-        )
+        inputs = [*parts, stepped, *inverse, next_tile]
+        return vmem_call(
+            make_middle(batch, bool(inverse)), (packed, packed, local, row), len(inputs), name="middle"
+        )(core, *inputs)
 
     def one_step(state):
         step, keep, send, stepped, mean, tile = state
@@ -411,19 +406,13 @@
         mine, other, picks = scores_of(keep, send, picks)
         next_tile = tile_of(picks)
         parts = change_of(mine, other, tile, mean, sums_of(next_tile))
-        inverse = factor_of(mine, other)
+        inverse = (factor_of(mine, other),)
         return (following, *advance(parts, stepped, inverse, next_tile), next_tile)
 
     mine, other, picks = scores_of(keep, send, chosen[:2])
-    tiles = tile_of(picks.reshape(-1))
-    both_sums = jnp.sum(tiles.reshape(2, cells, genes), axis=1, dtype=f32)
-    parts = change_of(mine, other, tiles, both_sums[:1], both_sums[1:], cells)
-    state = vmem_call(
-        make_middle(batch, False),
-        (packed, packed, local, row, jax.ShapeDtypeStruct((cells, genes), bf16)),
-        len(parts) + 2,
-        name="middle",
-    )(core, *parts, loadings_init, tiles)
+    tile, next_tile = jnp.split(tile_of(picks.reshape(-1)), 2)
+    parts = change_of(mine, other, tile, sums_of(tile), sums_of(next_tile), cells)
+    state = (*advance(parts, loadings_init, (), next_tile), next_tile)
     _, keep, send, stepped, mean, tile = lax.while_loop(
         lambda state: state[0] < steps - 1, one_step, (jnp.int32(1), *state)
     )

time: 344 us -> 340 us (0.988)
  local copies, waits for them, and re-layouts: 49.9 us -> 45.6 us
    while x20 -> x10, local copies, waits for them, and re-layouts: 4.5 us -> 0.44 us
  transfers between devices with their start and end apart: 44 -> 44, of which waited for: 24 -> 27; matrix products, arithmetic and copies ran while one was open for 14% -> 14% of each run, Pallas kernels for 5% -> 5%
where the time goes in v6:
time: 340 us; the launch traced here: 339 us
  blocking collectives  116 us (34%)
  starting transfers between devices  98.1 us (29%)
  local copies, waits for them, and re-layouts  45.6 us (13%)
  Pallas kernels  38.9 us (11%)
  waiting for transfers between devices  38.9 us (11%)
    all_to_all x8, blocking collectives, exchange(): lax.all_to_all(pieces, 'gene', 0, 0, tiled=True, axis_index_groups=same_c...  116 us
    gather x6, local copies, waits for them, and re-layouts, tile_of(): return jnp.take(pool_by_cell, picks, axis=0, mode='clip')  39.8 us
    pallas_call x38, Pallas kernels, run(): return call(*args[:core], *near, *args[last:])  38.9 us
    all_to_all x7, starting transfers between devices, exchange(): lax.all_to_all(pieces, 'gene', 0, 0, tiled=True, axis_index_groups=same_c...  37.4 us
    ppermute x16, starting transfers between devices, swap_cores(): lax.ppermute(value, 'gene', [(i, i ^ 1) for i in range(gene_devices)])  34.4 us
    ppermute x21, starting transfers between devices, round_cells(): lax.ppermute(value, 'cell', [(i, (i + k) % cell_devices) for i in range(c...  26.3 us
    all_to_all x7, waiting for transfers between devices, exchange(): lax.all_to_all(pieces, 'gene', 0, 0, tiled=True, axis_index_groups=same_c...  21.8 us
    ppermute x16, waiting for transfers between devices, swap_cores(): lax.ppermute(value, 'gene', [(i, i ^ 1) for i in range(gene_devices)])  13.9 us
  transfers between devices with their start and end apart: 44, of which 27 were waited for; matrix products, arithmetic and copies ran while one was open for 14% of the time, Pallas kernels for 5%

profile of v6, /device:TPU:1, one launch (start us, length us, event | category | flops | bytes accessed | tf_op | source)
XLA Modules:
  0.0 338.7 jit_solution(2600448936595286282)
XLA Ops:
  0.0 4.8 %first.1 = (f32[288,128]{1,0:T(8,128)S(1)}, f32[288,128]{1,0:T(8,128)S(1)}) custom-call(s32[1]{0:T(128)} %bitcast.5.core_ref, s32[1]{0:T(128)} %bitcast.6.cell_ref, f32[64,320]{1,0:T(8,128)} %previous_ref.1, s32[7,1024]{1,0:T(8,128)} %picks_ref.1, bf16[320,4096]{1,0:T(8,128)(2,1)} %pool_ref.1), custom_call_target="tpu_custom_call" | custom-call | tf_op jit(solution)/shard_map/first/pallas_call | solution.py:35
  9.8 9.3 %all-to-all-start.2 = ((f32[32,1,1152]{2,1,0:T(1,128)}), f32[32,1,1152]{2,1,0:T(1,128)S(1)}, u32[]{:S(2)}, u32[]{:S(2)}) async-start(f32[32,1,1152]{2,1,0:T(1,128)} %bitcast.7), calls=%async_computation.2 | async-start | bytes 294912 | tf_op jit(solution)/shard_map/all_to_all | solution.py:354
  22.0 6.3 %all-to-all-done.2 = f32[32,1,1152]{2,1,0:T(1,128)S(1)} async-done(((f32[32,1,1152]{2,1,0:T(1,128)}), f32[32,1,1152]{2,1,0:T(1,128)S(1)}, u32[]{:S(2)}, u32[]{:S(2)}) %all-to-all-start.2) | async-done | bytes 147488 | tf_op jit(solution)/shard_map/all_to_all | solution.py:354
  29.0 4.7 %all-to-all-start.3 = ((f32[32,1,1152]{2,1,0:T(1,128)}), f32[32,1,1152]{2,1,0:T(1,128)S(1)}, u32[]{:S(2)}, u32[]{:S(2)}) async-start(f32[32,1,1152]{2,1,0:T(1,128)} %bitcast.9), calls=%async_computation.3 | async-start | bytes 294912 | tf_op jit(solution)/shard_map/all_to_all | solution.py:354
  33.7 9.5 %gather_fusion.1 = bf16[2048,320]{1,0:T(8,128)(2,1)S(1)} fusion(bf16[4096,320]{1,0:T(8,128)(2,1)} %bitcast.47, s32[2048]{0:T(1024)S(1)} %bitcast_clamp_fusion), kind=kCustom, calls=%fused_computation.1 | custom fusion | bytes 2629632 | tf_op jit(solution)/shard_map/jit(_take)/gather | solution.py:338
  55.6 219.0 %while.20 = (s32[]{:T(128)}, f32[288,128]{1,0:T(8,128)S(1)}, f32[288,128]{1,0:T(8,128)S(1)}, f32[64,320]{1,0:T(8,128)S(1)}, f32[1,320]{1,0:T(1,128)S(1)}, /*inde...) while((s32[]{:T(128)}, f32[288,128]{1,0:T(8,128)S(1)}, ...), condition=%wide.region_4.5_spmd, body=%wide.region_2.4_spmd.sunk | while | flops 1000656064 | bytes 6045835 | solution.py:416
  58.2 18.5 %all_to_all.46 = f32[32,1,1152]{2,1,0:T(1,128)S(1)} all-to-all(f32[32,1,1152]{2,1,0:T(1,128)S(1)} %bitcast.34), channel_id=1, replica_groups={{0,8,16,24,32,40,48,56,64,72,80,88,96,104,112,120,128,136,144,152,160,1..., dimensions={0} | all-to-all | bytes 294912 | tf_op jit(solution)/shard_map/while/body/all_to_all | solution.py:354
  77.4 4.7 %all-to-all-start.1 = ((f32[32,1,1152]{2,1,0:T(1,128)}), f32[32,1,1152]{2,1,0:T(1,128)S(1)}, u32[]{:S(2)}, u32[]{:S(2)}) async-start(f32[32,1,1152]{2,1,0:T(1,128)} %bitcast.29), calls=%async_computation.1 | async-start | bytes 294912 | tf_op jit(solution)/shard_map/while/body/all_to_all | solution.py:354
  82.1 6.1 %gather_fusion = bf16[1024,320]{1,0:T(8,128)(2,1)S(1)} fusion(bf16[4096,320]{1,0:T(8,128)(2,1)} %get-tuple-element.285, s32[1024]{0:T(1024)S(1)} %broadcast_clamp_fusion.2), kind=kCustom, calls=%fused_computation.clone.1 | custom fusion | bytes 1314816 | tf_op jit(solution)/shard_map/while/body/jit(_take)/gather | solution.py:338
  105.9 14.2 %all_to_all.46 = f32[32,1,1152]{2,1,0:T(1,128)S(1)} all-to-all(f32[32,1,1152]{2,1,0:T(1,128)S(1)} %bitcast.34), channel_id=1, replica_groups={{0,8,16,24,32,40,48,56,64,72,80,88,96,104,112,120,128,136,144,152,160,1..., dimensions={0} | all-to-all | bytes 294912 | tf_op jit(solution)/shard_map/while/body/all_to_all | solution.py:354
  120.7 4.7 %all-to-all-start.1 = ((f32[32,1,1152]{2,1,0:T(1,128)}), f32[32,1,1152]{2,1,0:T(1,128)S(1)}, u32[]{:S(2)}, u32[]{:S(2)}) async-start(f32[32,1,1152]{2,1,0:T(1,128)} %bitcast.29), calls=%async_computation.1 | async-start | bytes 294912 | tf_op jit(solution)/shard_map/while/body/all_to_all | solution.py:354
  125.4 6.1 %gather_fusion = bf16[1024,320]{1,0:T(8,128)(2,1)S(1)} fusion(bf16[4096,320]{1,0:T(8,128)(2,1)} %get-tuple-element.285, s32[1024]{0:T(1024)S(1)} %broadcast_clamp_fusion.2), kind=kCustom, calls=%fused_computation.clone.1 | custom fusion | bytes 1314816 | tf_op jit(solution)/shard_map/while/body/jit(_take)/gather | solution.py:338
  148.3 14.2 %all_to_all.46 = f32[32,1,1152]{2,1,0:T(1,128)S(1)} all-to-all(f32[32,1,1152]{2,1,0:T(1,128)S(1)} %bitcast.34), channel_id=1, replica_groups={{0,8,16,24,32,40,48,56,64,72,80,88,96,104,112,120,128,136,144,152,160,1..., dimensions={0} | all-to-all | bytes 294912 | tf_op jit(solution)/shard_map/while/body/all_to_all | solution.py:354
  163.2 4.7 %all-to-all-start.1 = ((f32[32,1,1152]{2,1,0:T(1,128)}), f32[32,1,1152]{2,1,0:T(1,128)S(1)}, u32[]{:S(2)}, u32[]{:S(2)}) async-start(f32[32,1,1152]{2,1,0:T(1,128)} %bitcast.29), calls=%async_computation.1 | async-start | bytes 294912 | tf_op jit(solution)/shard_map/while/body/all_to_all | solution.py:354
  167.9 6.1 %gather_fusion = bf16[1024,320]{1,0:T(8,128)(2,1)S(1)} fusion(bf16[4096,320]{1,0:T(8,128)(2,1)} %get-tuple-element.285, s32[1024]{0:T(1024)S(1)} %broadcast_clamp_fusion.2), kind=kCustom, calls=%fused_computation.clone.1 | custom fusion | bytes 1314816 | tf_op jit(solution)/shard_map/while/body/jit(_take)/gather | solution.py:338
  191.5 14.2 %all_to_all.46 = f32[32,1,1152]{2,1,0:T(1,128)S(1)} all-to-all(f32[32,1,1152]{2,1,0:T(1,128)S(1)} %bitcast.34), channel_id=1, replica_groups={{0,8,16,24,32,40,48,56,64,72,80,88,96,104,112,120,128,136,144,152,160,1..., dimensions={0} | all-to-all | bytes 294912 | tf_op jit(solution)/shard_map/while/body/all_to_all | solution.py:354
  206.3 4.7 %all-to-all-start.1 = ((f32[32,1,1152]{2,1,0:T(1,128)}), f32[32,1,1152]{2,1,0:T(1,128)S(1)}, u32[]{:S(2)}, u32[]{:S(2)}) async-start(f32[32,1,1152]{2,1,0:T(1,128)} %bitcast.29), calls=%async_computation.1 | async-start | bytes 294912 | tf_op jit(solution)/shard_map/while/body/all_to_all | solution.py:354
  211.0 6.1 %gather_fusion = bf16[1024,320]{1,0:T(8,128)(2,1)S(1)} fusion(bf16[4096,320]{1,0:T(8,128)(2,1)} %get-tuple-element.285, s32[1024]{0:T(1024)S(1)} %broadcast_clamp_fusion.2), kind=kCustom, calls=%fused_computation.clone.1 | custom fusion | bytes 1314816 | tf_op jit(solution)/shard_map/while/body/jit(_take)/gather | solution.py:338
  234.2 14.2 %all_to_all.46 = f32[32,1,1152]{2,1,0:T(1,128)S(1)} all-to-all(f32[32,1,1152]{2,1,0:T(1,128)S(1)} %bitcast.34), channel_id=1, replica_groups={{0,8,16,24,32,40,48,56,64,72,80,88,96,104,112,120,128,136,144,152,160,1..., dimensions={0} | all-to-all | bytes 294912 | tf_op jit(solution)/shard_map/while/body/all_to_all | solution.py:354
  249.1 4.7 %all-to-all-start.1 = ((f32[32,1,1152]{2,1,0:T(1,128)}), f32[32,1,1152]{2,1,0:T(1,128)S(1)}, u32[]{:S(2)}, u32[]{:S(2)}) async-start(f32[32,1,1152]{2,1,0:T(1,128)} %bitcast.29), calls=%async_computation.1 | async-start | bytes 294912 | tf_op jit(solution)/shard_map/while/body/all_to_all | solution.py:354
  253.8 6.1 %gather_fusion = bf16[1024,320]{1,0:T(8,128)(2,1)S(1)} fusion(bf16[4096,320]{1,0:T(8,128)(2,1)} %get-tuple-element.285, s32[1024]{0:T(1024)S(1)} %broadcast_clamp_fusion.2), kind=kCustom, calls=%fused_computation.clone.1 | custom fusion | bytes 1314816 | tf_op jit(solution)/shard_map/while/body/jit(_take)/gather | solution.py:338
  277.2 14.2 %all_to_all.43 = f32[32,1,1152]{2,1,0:T(1,128)S(1)} all-to-all(f32[32,1,1152]{2,1,0:T(1,128)S(1)} %bitcast.41), channel_id=1, replica_groups={{0,8,16,24,32,40,48,56,64,72,80,88,96,104,112,120,128,136,144,152,160,1..., dimensions={0} | all-to-all | bytes 294912 | tf_op jit(solution)/shard_map/all_to_all | solution.py:354
  291.3 13.7 %all_to_all.44 = f32[32,1,1152]{2,1,0:T(1,128)S(1)} all-to-all(f32[32,1,1152]{2,1,0:T(1,128)S(1)} %bitcast.45), channel_id=1, replica_groups={{0,8,16,24,32,40,48,56,64,72,80,88,96,104,112,120,128,136,144,152,160,1..., dimensions={0} | all-to-all | bytes 294912 | tf_op jit(solution)/shard_map/all_to_all | solution.py:354
  318.7 12.5 %all_to_all.45 = f32[32,1,1152]{2,1,0:T(1,128)S(1)} all-to-all(f32[32,1,1152]{2,1,0:T(1,128)S(1)} %bitcast.43), channel_id=1, replica_groups={{0,8,16,24,32,40,48,56,64,72,80,88,96,104,112,120,128,136,144,152,160,1..., dimensions={0} | all-to-all | bytes 294912 | tf_op jit(solution)/shard_map/all_to_all | solution.py:354
  (163 shorter events, 134.2 us)
Async XLA Ops:
  4.8 4.3 %collective-permute-start.5 = (f32[288,128]{1,0:T(8,128)S(1)}, f32[288,128]{1,0:T(8,128)S(1)}, u32[]{:S(2)}, u32[]{:S(2)}) collective-permute-start(f32[288,128]{1,0:T(8,128)S(1)} %get-tuple-element.144), channel_id=1, source_target_pairs={{0,4},{4,0},{8,12},{12,8},{16,20},{20,16},{24,28},{28,24},{32,36},... | collective-permute-start | bytes 442376 | tf_op jit(solution)/shard_map/ppermute | solution.py:344
  9.8 18.5 %all-to-all-start.2 = ((f32[32,1,1152]{2,1,0:T(1,128)}), f32[32,1,1152]{2,1,0:T(1,128)S(1)}, u32[]{:S(2)}, u32[]{:S(2)}) async-start(f32[32,1,1152]{2,1,0:T(1,128)} %bitcast.7), calls=%async_computation.2 | async-start | bytes 294912 | tf_op jit(solution)/shard_map/all_to_all | solution.py:354
  29.0 14.5 %all-to-all-start.3 = ((f32[32,1,1152]{2,1,0:T(1,128)}), f32[32,1,1152]{2,1,0:T(1,128)S(1)}, u32[]{:S(2)}, u32[]{:S(2)}) async-start(f32[32,1,1152]{2,1,0:T(1,128)} %bitcast.9), calls=%async_computation.3 | async-start | bytes 294912 | tf_op jit(solution)/shard_map/all_to_all | solution.py:354
  47.7 5.1 %collective-permute-start.7 = (bf16[72,384]{1,0:T(8,128)(2,1)S(1)}, bf16[72,384]{1,0:T(8,128)(2,1)S(1)}, u32[]{:S(2)}, u32[]{:S(2)}) collective-permute-start(bf16[72,384]{1,0:T(8,128)(2,1)S(1)} %update.3.a), channel_id=1, source_target_pairs={{0,1},{1,2},{2,3},{3,0},{4,5},{5,6},{6,7},{7,4},{8,9},{9,10},{10,1... | collective-permute-start | bytes 165896 | tf_op jit(solution)/shard_map/ppermute | solution.py:348
  49.1 5.7 %collective-permute-start.8 = (bf16[72,384]{1,0:T(8,128)(2,1)S(1)}, bf16[72,384]{1,0:T(8,128)(2,1)S(1)}, u32[]{:S(2)}, u32[]{:S(2)}) collective-permute-start(bf16[72,384]{1,0:T(8,128)(2,1)S(1)} %update.3.a), channel_id=1, source_target_pairs={{0,2},{1,3},{2,0},{3,1},{4,6},{5,7},{6,4},{7,5},{8,10},{9,11},{10,... | collective-permute-start | bytes 165896 | tf_op jit(solution)/shard_map/ppermute | solution.py:348
  77.4 13.9 %all-to-all-start.1 = ((f32[32,1,1152]{2,1,0:T(1,128)}), f32[32,1,1152]{2,1,0:T(1,128)S(1)}, u32[]{:S(2)}, u32[]{:S(2)}) async-start(f32[32,1,1152]{2,1,0:T(1,128)} %bitcast.29), calls=%async_computation.1 | async-start | bytes 294912 | tf_op jit(solution)/shard_map/while/body/all_to_all | solution.py:354
  95.4 6.8 %collective-permute-start.2 = (bf16[72,384]{1,0:T(8,128)(2,1)S(1)}, bf16[72,384]{1,0:T(8,128)(2,1)S(1)}, u32[]{:S(2)}, u32[]{:S(2)}) collective-permute-start(bf16[72,384]{1,0:T(8,128)(2,1)S(1)} %update.5.a), channel_id=1, source_target_pairs={{0,1},{1,2},{2,3},{3,0},{4,5},{5,6},{6,7},{7,4},{8,9},{9,10},{10,1... | collective-permute-start | bytes 165896 | tf_op jit(solution)/shard_map/while/body/ppermute | solution.py:348
  95.8 6.4 %collective-permute-start.3 = (bf16[72,384]{1,0:T(8,128)(2,1)S(1)}, bf16[72,384]{1,0:T(8,128)(2,1)S(1)}, u32[]{:S(2)}, u32[]{:S(2)}) collective-permute-start(bf16[72,384]{1,0:T(8,128)(2,1)S(1)} %update.5.a), channel_id=1, source_target_pairs={{0,2},{1,3},{2,0},{3,1},{4,6},{5,7},{6,4},{7,5},{8,10},{9,11},{10,... | collective-permute-start | bytes 165896 | tf_op jit(solution)/shard_map/while/body/ppermute | solution.py:348
  120.7 13.9 %all-to-all-start.1 = ((f32[32,1,1152]{2,1,0:T(1,128)}), f32[32,1,1152]{2,1,0:T(1,128)S(1)}, u32[]{:S(2)}, u32[]{:S(2)}) async-start(f32[32,1,1152]{2,1,0:T(1,128)} %bitcast.29), calls=%async_computation.1 | async-start | bytes 294912 | tf_op jit(solution)/shard_map/while/body/all_to_all | solution.py:354
  138.7 6.5 %collective-permute-start.2 = (bf16[72,384]{1,0:T(8,128)(2,1)S(1)}, bf16[72,384]{1,0:T(8,128)(2,1)S(1)}, u32[]{:S(2)}, u32[]{:S(2)}) collective-permute-start(bf16[72,384]{1,0:T(8,128)(2,1)S(1)} %update.5.a), channel_id=1, source_target_pairs={{0,1},{1,2},{2,3},{3,0},{4,5},{5,6},{6,7},{7,4},{8,9},{9,10},{10,1... | collective-permute-start | bytes 165896 | tf_op jit(solution)/shard_map/while/body/ppermute | solution.py:348
  139.5 5.7 %collective-permute-start.3 = (bf16[72,384]{1,0:T(8,128)(2,1)S(1)}, bf16[72,384]{1,0:T(8,128)(2,1)S(1)}, u32[]{:S(2)}, u32[]{:S(2)}) collective-permute-start(bf16[72,384]{1,0:T(8,128)(2,1)S(1)} %update.5.a), channel_id=1, source_target_pairs={{0,2},{1,3},{2,0},{3,1},{4,6},{5,7},{6,4},{7,5},{8,10},{9,11},{10,... | collective-permute-start | bytes 165896 | tf_op jit(solution)/shard_map/while/body/ppermute | solution.py:348
  141.3 3.9 %collective-permute-start.4 = (bf16[72,384]{1,0:T(8,128)(2,1)S(1)}, bf16[72,384]{1,0:T(8,128)(2,1)S(1)}, u32[]{:S(2)}, u32[]{:S(2)}) collective-permute-start(bf16[72,384]{1,0:T(8,128)(2,1)S(1)} %update.5.a), channel_id=1, source_target_pairs={{0,3},{1,0},{2,1},{3,2},{4,7},{5,4},{6,5},{7,6},{8,11},{9,8},{10,9... | collective-permute-start | bytes 165896 | tf_op jit(solution)/shard_map/while/body/ppermute | solution.py:348
  163.2 13.9 %all-to-all-start.1 = ((f32[32,1,1152]{2,1,0:T(1,128)}), f32[32,1,1152]{2,1,0:T(1,128)S(1)}, u32[]{:S(2)}, u32[]{:S(2)}) async-start(f32[32,1,1152]{2,1,0:T(1,128)} %bitcast.29), calls=%async_computation.1 | async-start | bytes 294912 | tf_op jit(solution)/shard_map/while/body/all_to_all | solution.py:354
  177.0 3.8 %collective-permute-start.1 = (f32[288,128]{1,0:T(8,128)S(1)}, f32[288,128]{1,0:T(8,128)S(1)}, u32[]{:S(2)}, u32[]{:S(2)}) collective-permute-start(f32[288,128]{1,0:T(8,128)S(1)} %bitcast.31), channel_id=1, source_target_pairs={{0,4},{4,0},{8,12},{12,8},{16,20},{20,16},{24,28},{28,24},{32,36},... | collective-permute-start | bytes 442376 | tf_op jit(solution)/shard_map/while/body/ppermute | solution.py:344
  181.2 7.0 %collective-permute-start.2 = (bf16[72,384]{1,0:T(8,128)(2,1)S(1)}, bf16[72,384]{1,0:T(8,128)(2,1)S(1)}, u32[]{:S(2)}, u32[]{:S(2)}) collective-permute-start(bf16[72,384]{1,0:T(8,128)(2,1)S(1)} %update.5.a), channel_id=1, source_target_pairs={{0,1},{1,2},{2,3},{3,0},{4,5},{5,6},{6,7},{7,4},{8,9},{9,10},{10,1... | collective-permute-start | bytes 165896 | tf_op jit(solution)/shard_map/while/body/ppermute | solution.py:348
  181.9 6.2 %collective-permute-start.3 = (bf16[72,384]{1,0:T(8,128)(2,1)S(1)}, bf16[72,384]{1,0:T(8,128)(2,1)S(1)}, u32[]{:S(2)}, u32[]{:S(2)}) collective-permute-start(bf16[72,384]{1,0:T(8,128)(2,1)S(1)} %update.5.a), channel_id=1, source_target_pairs={{0,2},{1,3},{2,0},{3,1},{4,6},{5,7},{6,4},{7,5},{8,10},{9,11},{10,... | collective-permute-start | bytes 165896 | tf_op jit(solution)/shard_map/while/body/ppermute | solution.py:348
  206.3 13.9 %all-to-all-start.1 = ((f32[32,1,1152]{2,1,0:T(1,128)}), f32[32,1,1152]{2,1,0:T(1,128)S(1)}, u32[]{:S(2)}, u32[]{:S(2)}) async-start(f32[32,1,1152]{2,1,0:T(1,128)} %bitcast.29), calls=%async_computation.1 | async-start | bytes 294912 | tf_op jit(solution)/shard_map/while/body/all_to_all | solution.py:354
  224.3 6.5 %collective-permute-start.2 = (bf16[72,384]{1,0:T(8,128)(2,1)S(1)}, bf16[72,384]{1,0:T(8,128)(2,1)S(1)}, u32[]{:S(2)}, u32[]{:S(2)}) collective-permute-start(bf16[72,384]{1,0:T(8,128)(2,1)S(1)} %update.5.a), channel_id=1, source_target_pairs={{0,1},{1,2},{2,3},{3,0},{4,5},{5,6},{6,7},{7,4},{8,9},{9,10},{10,1... | collective-permute-start | bytes 165896 | tf_op jit(solution)/shard_map/while/body/ppermute | solution.py:348
  225.2 5.7 %collective-permute-start.3 = (bf16[72,384]{1,0:T(8,128)(2,1)S(1)}, bf16[72,384]{1,0:T(8,128)(2,1)S(1)}, u32[]{:S(2)}, u32[]{:S(2)}) collective-permute-start(bf16[72,384]{1,0:T(8,128)(2,1)S(1)} %update.5.a), channel_id=1, source_target_pairs={{0,2},{1,3},{2,0},{3,1},{4,6},{5,7},{6,4},{7,5},{8,10},{9,11},{10,... | collective-permute-start | bytes 165896 | tf_op jit(solution)/shard_map/while/body/ppermute | solution.py:348
  249.1 13.9 %all-to-all-start.1 = ((f32[32,1,1152]{2,1,0:T(1,128)}), f32[32,1,1152]{2,1,0:T(1,128)S(1)}, u32[]{:S(2)}, u32[]{:S(2)}) async-start(f32[32,1,1152]{2,1,0:T(1,128)} %bitcast.29), calls=%async_computation.1 | async-start | bytes 294912 | tf_op jit(solution)/shard_map/while/body/all_to_all | solution.py:354
  267.1 6.7 %collective-permute-start.2 = (bf16[72,384]{1,0:T(8,128)(2,1)S(1)}, bf16[72,384]{1,0:T(8,128)(2,1)S(1)}, u32[]{:S(2)}, u32[]{:S(2)}) collective-permute-start(bf16[72,384]{1,0:T(8,128)(2,1)S(1)} %update.5.a), channel_id=1, source_target_pairs={{0,1},{1,2},{2,3},{3,0},{4,5},{5,6},{6,7},{7,4},{8,9},{9,10},{10,1... | collective-permute-start | bytes 165896 | tf_op jit(solution)/shard_map/while/body/ppermute | solution.py:348
  267.9 5.9 %collective-permute-start.3 = (bf16[72,384]{1,0:T(8,128)(2,1)S(1)}, bf16[72,384]{1,0:T(8,128)(2,1)S(1)}, u32[]{:S(2)}, u32[]{:S(2)}) collective-permute-start(bf16[72,384]{1,0:T(8,128)(2,1)S(1)} %update.5.a), channel_id=1, source_target_pairs={{0,2},{1,3},{2,0},{3,1},{4,6},{5,7},{6,4},{7,5},{8,10},{9,11},{10,... | collective-permute-start | bytes 165896 | tf_op jit(solution)/shard_map/while/body/ppermute | solution.py:348
  309.1 6.4 %collective-permute-start.12 = (bf16[72,384]{1,0:T(8,128)(2,1)S(1)}, bf16[72,384]{1,0:T(8,128)(2,1)S(1)}, u32[]{:S(2)}, u32[]{:S(2)}) collective-permute-start(bf16[72,384]{1,0:T(8,128)(2,1)S(1)} %update.4.a), channel_id=1, source_target_pairs={{0,1},{1,2},{2,3},{3,0},{4,5},{5,6},{6,7},{7,4},{8,9},{9,10},{10,1... | collective-permute-start | bytes 165896 | tf_op jit(solution)/shard_map/ppermute | solution.py:348
  309.9 5.6 %collective-permute-start.13 = (bf16[72,384]{1,0:T(8,128)(2,1)S(1)}, bf16[72,384]{1,0:T(8,128)(2,1)S(1)}, u32[]{:S(2)}, u32[]{:S(2)}) collective-permute-start(bf16[72,384]{1,0:T(8,128)(2,1)S(1)} %update.4.a), channel_id=1, source_target_pairs={{0,2},{1,3},{2,0},{3,1},{4,6},{5,7},{6,4},{7,5},{8,10},{9,11},{10,... | collective-permute-start | bytes 165896 | tf_op jit(solution)/shard_map/ppermute | solution.py:348
  (24 other events, 97.9 us)

commit v7 on v6

--- a/solution.py
+++ b/solution.py
@@ -346,7 +346,7 @@
     def round_cells(value):
         return [value] + [
             lax.ppermute(value, "cell", [(i, (i + k) % cell_devices) for i in range(cell_devices)])
-            for k in range(1, cell_devices)
+            for k in (1, 3, 2)
         ]
 
     def exchange(value):

time: 340 us -> 347 us (1.021)
  waiting for transfers between devices: 38.9 us -> 46.6 us
    ppermute x21, waiting for transfers between devices: 3.19 us -> 10.9 us  [round_cells(): lax.ppermute(value, 'cell', [(i, (i + k) % cell_devices) for i in range(c...]
    ppermute x21, starting transfers between devices: 26.3 us -> 21.4 us  [round_cells(): lax.ppermute(value, 'cell', [(i, (i + k) % cell_devices) for i in range(c...]
    ppermute x16, starting transfers between devices: 34.4 us -> 38.6 us  [swap_cores(): lax.ppermute(value, 'gene', [(i, i ^ 1) for i in range(gene_devices)])]
  transfers between devices with their start and end apart: 44 -> 44, of which waited for: 27 -> 29; matrix products, arithmetic and copies ran while one was open for 14% -> 13% of each run, Pallas kernels for 5% -> 5%
where the time goes in v7:
time: 347 us; the launch traced here: 346 us
  blocking collectives  116 us (33%)
  starting transfers between devices  97.4 us (28%)
  waiting for transfers between devices  46.6 us (13%)
  local copies, waits for them, and re-layouts  45.6 us (13%)
  Pallas kernels  38.9 us (11%)
    all_to_all x8, blocking collectives, exchange(): lax.all_to_all(pieces, 'gene', 0, 0, tiled=True, axis_index_groups=same_c...  116 us
    gather x6, local copies, waits for them, and re-layouts, tile_of(): return jnp.take(pool_by_cell, picks, axis=0, mode='clip')  39.8 us
    pallas_call x38, Pallas kernels, run(): return call(*args[:core], *near, *args[last:])  38.9 us
    ppermute x16, starting transfers between devices, swap_cores(): lax.ppermute(value, 'gene', [(i, i ^ 1) for i in range(gene_devices)])  38.6 us
    all_to_all x7, starting transfers between devices, exchange(): lax.all_to_all(pieces, 'gene', 0, 0, tiled=True, axis_index_groups=same_c...  37.4 us
    all_to_all x7, waiting for transfers between devices, exchange(): lax.all_to_all(pieces, 'gene', 0, 0, tiled=True, axis_index_groups=same_c...  21.8 us
    ppermute x21, starting transfers between devices, round_cells(): lax.ppermute(value, 'cell', [(i, (i + k) % cell_devices) for i in range(c...  21.4 us
    ppermute x16, waiting for transfers between devices, swap_cores(): lax.ppermute(value, 'gene', [(i, i ^ 1) for i in range(gene_devices)])  13.8 us
  transfers between devices with their start and end apart: 44, of which 29 were waited for; matrix products, arithmetic and copies ran while one was open for 13% of the time, Pallas kernels for 5%

profile of v7, /device:TPU:1, one launch (start us, length us, event | category | flops | bytes accessed | tf_op | source)
XLA Modules:
  0.0 345.8 jit_solution(9383317857017640723)
XLA Ops:
  0.0 4.8 %first.1 = (f32[288,128]{1,0:T(8,128)S(1)}, f32[288,128]{1,0:T(8,128)S(1)}) custom-call(s32[1]{0:T(128)} %bitcast.5.core_ref, s32[1]{0:T(128)} %bitcast.6.cell_ref, f32[64,320]{1,0:T(8,128)} %previous_ref.1, s32[7,1024]{1,0:T(8,128)} %picks_ref.1, bf16[320,4096]{1,0:T(8,128)(2,1)} %pool_ref.1), custom_call_target="tpu_custom_call" | custom-call | tf_op jit(solution)/shard_map/first/pallas_call | solution.py:35
  9.8 9.3 %all-to-all-start.2 = ((f32[32,1,1152]{2,1,0:T(1,128)}), f32[32,1,1152]{2,1,0:T(1,128)S(1)}, u32[]{:S(2)}, u32[]{:S(2)}) async-start(f32[32,1,1152]{2,1,0:T(1,128)} %bitcast.7), calls=%async_computation.2 | async-start | bytes 294912 | tf_op jit(solution)/shard_map/all_to_all | solution.py:354
  22.0 6.3 %all-to-all-done.2 = f32[32,1,1152]{2,1,0:T(1,128)S(1)} async-done(((f32[32,1,1152]{2,1,0:T(1,128)}), f32[32,1,1152]{2,1,0:T(1,128)S(1)}, u32[]{:S(2)}, u32[]{:S(2)}) %all-to-all-start.2) | async-done | bytes 147488 | tf_op jit(solution)/shard_map/all_to_all | solution.py:354
  29.0 4.7 %all-to-all-start.3 = ((f32[32,1,1152]{2,1,0:T(1,128)}), f32[32,1,1152]{2,1,0:T(1,128)S(1)}, u32[]{:S(2)}, u32[]{:S(2)}) async-start(f32[32,1,1152]{2,1,0:T(1,128)} %bitcast.9), calls=%async_computation.3 | async-start | bytes 294912 | tf_op jit(solution)/shard_map/all_to_all | solution.py:354
  33.7 9.5 %gather_fusion.1 = bf16[2048,320]{1,0:T(8,128)(2,1)S(1)} fusion(bf16[4096,320]{1,0:T(8,128)(2,1)} %bitcast.47, s32[2048]{0:T(1024)S(1)} %bitcast_clamp_fusion), kind=kCustom, calls=%fused_computation.1 | custom fusion | bytes 2629632 | tf_op jit(solution)/shard_map/jit(_take)/gather | solution.py:338
  55.7 224.1 %while.20 = (s32[]{:T(128)}, f32[288,128]{1,0:T(8,128)S(1)}, f32[288,128]{1,0:T(8,128)S(1)}, f32[64,320]{1,0:T(8,128)S(1)}, f32[1,320]{1,0:T(1,128)S(1)}, /*inde...) while((s32[]{:T(128)}, f32[288,128]{1,0:T(8,128)S(1)}, ...), condition=%wide.region_4.5_spmd, body=%wide.region_2.4_spmd.sunk | while | flops 1000656064 | bytes 6045835 | solution.py:416
  58.5 18.5 %all_to_all.46 = f32[32,1,1152]{2,1,0:T(1,128)S(1)} all-to-all(f32[32,1,1152]{2,1,0:T(1,128)S(1)} %bitcast.34), channel_id=1, replica_groups={{0,8,16,24,32,40,48,56,64,72,80,88,96,104,112,120,128,136,144,152,160,1..., dimensions={0} | all-to-all | bytes 294912 | tf_op jit(solution)/shard_map/while/body/all_to_all | solution.py:354
  77.7 4.7 %all-to-all-start.1 = ((f32[32,1,1152]{2,1,0:T(1,128)}), f32[32,1,1152]{2,1,0:T(1,128)S(1)}, u32[]{:S(2)}, u32[]{:S(2)}) async-start(f32[32,1,1152]{2,1,0:T(1,128)} %bitcast.29), calls=%async_computation.1 | async-start | bytes 294912 | tf_op jit(solution)/shard_map/while/body/all_to_all | solution.py:354
  82.4 6.1 %gather_fusion = bf16[1024,320]{1,0:T(8,128)(2,1)S(1)} fusion(bf16[4096,320]{1,0:T(8,128)(2,1)} %get-tuple-element.285, s32[1024]{0:T(1024)S(1)} %broadcast_clamp_fusion.2), kind=kCustom, calls=%fused_computation.clone.1 | custom fusion | bytes 1314816 | tf_op jit(solution)/shard_map/while/body/jit(_take)/gather | solution.py:338
  106.9 14.2 %all_to_all.46 = f32[32,1,1152]{2,1,0:T(1,128)S(1)} all-to-all(f32[32,1,1152]{2,1,0:T(1,128)S(1)} %bitcast.34), channel_id=1, replica_groups={{0,8,16,24,32,40,48,56,64,72,80,88,96,104,112,120,128,136,144,152,160,1..., dimensions={0} | all-to-all | bytes 294912 | tf_op jit(solution)/shard_map/while/body/all_to_all | solution.py:354
  121.7 4.7 %all-to-all-start.1 = ((f32[32,1,1152]{2,1,0:T(1,128)}), f32[32,1,1152]{2,1,0:T(1,128)S(1)}, u32[]{:S(2)}, u32[]{:S(2)}) async-start(f32[32,1,1152]{2,1,0:T(1,128)} %bitcast.29), calls=%async_computation.1 | async-start | bytes 294912 | tf_op jit(solution)/shard_map/while/body/all_to_all | solution.py:354
  126.4 6.1 %gather_fusion = bf16[1024,320]{1,0:T(8,128)(2,1)S(1)} fusion(bf16[4096,320]{1,0:T(8,128)(2,1)} %get-tuple-element.285, s32[1024]{0:T(1024)S(1)} %broadcast_clamp_fusion.2), kind=kCustom, calls=%fused_computation.clone.1 | custom fusion | bytes 1314816 | tf_op jit(solution)/shard_map/while/body/jit(_take)/gather | solution.py:338
  150.9 14.2 %all_to_all.46 = f32[32,1,1152]{2,1,0:T(1,128)S(1)} all-to-all(f32[32,1,1152]{2,1,0:T(1,128)S(1)} %bitcast.34), channel_id=1, replica_groups={{0,8,16,24,32,40,48,56,64,72,80,88,96,104,112,120,128,136,144,152,160,1..., dimensions={0} | all-to-all | bytes 294912 | tf_op jit(solution)/shard_map/while/body/all_to_all | solution.py:354
  165.8 4.7 %all-to-all-start.1 = ((f32[32,1,1152]{2,1,0:T(1,128)}), f32[32,1,1152]{2,1,0:T(1,128)S(1)}, u32[]{:S(2)}, u32[]{:S(2)}) async-start(f32[32,1,1152]{2,1,0:T(1,128)} %bitcast.29), calls=%async_computation.1 | async-start | bytes 294912 | tf_op jit(solution)/shard_map/while/body/all_to_all | solution.py:354
  170.5 6.1 %gather_fusion = bf16[1024,320]{1,0:T(8,128)(2,1)S(1)} fusion(bf16[4096,320]{1,0:T(8,128)(2,1)} %get-tuple-element.285, s32[1024]{0:T(1024)S(1)} %broadcast_clamp_fusion.2), kind=kCustom, calls=%fused_computation.clone.1 | custom fusion | bytes 1314816 | tf_op jit(solution)/shard_map/while/body/jit(_take)/gather | solution.py:338
  195.0 14.2 %all_to_all.46 = f32[32,1,1152]{2,1,0:T(1,128)S(1)} all-to-all(f32[32,1,1152]{2,1,0:T(1,128)S(1)} %bitcast.34), channel_id=1, replica_groups={{0,8,16,24,32,40,48,56,64,72,80,88,96,104,112,120,128,136,144,152,160,1..., dimensions={0} | all-to-all | bytes 294912 | tf_op jit(solution)/shard_map/while/body/all_to_all | solution.py:354
  209.8 4.7 %all-to-all-start.1 = ((f32[32,1,1152]{2,1,0:T(1,128)}), f32[32,1,1152]{2,1,0:T(1,128)S(1)}, u32[]{:S(2)}, u32[]{:S(2)}) async-start(f32[32,1,1152]{2,1,0:T(1,128)} %bitcast.29), calls=%async_computation.1 | async-start | bytes 294912 | tf_op jit(solution)/shard_map/while/body/all_to_all | solution.py:354
  214.5 6.1 %gather_fusion = bf16[1024,320]{1,0:T(8,128)(2,1)S(1)} fusion(bf16[4096,320]{1,0:T(8,128)(2,1)} %get-tuple-element.285, s32[1024]{0:T(1024)S(1)} %broadcast_clamp_fusion.2), kind=kCustom, calls=%fused_computation.clone.1 | custom fusion | bytes 1314816 | tf_op jit(solution)/shard_map/while/body/jit(_take)/gather | solution.py:338
  239.0 14.2 %all_to_all.46 = f32[32,1,1152]{2,1,0:T(1,128)S(1)} all-to-all(f32[32,1,1152]{2,1,0:T(1,128)S(1)} %bitcast.34), channel_id=1, replica_groups={{0,8,16,24,32,40,48,56,64,72,80,88,96,104,112,120,128,136,144,152,160,1..., dimensions={0} | all-to-all | bytes 294912 | tf_op jit(solution)/shard_map/while/body/all_to_all | solution.py:354
  253.9 4.7 %all-to-all-start.1 = ((f32[32,1,1152]{2,1,0:T(1,128)}), f32[32,1,1152]{2,1,0:T(1,128)S(1)}, u32[]{:S(2)}, u32[]{:S(2)}) async-start(f32[32,1,1152]{2,1,0:T(1,128)} %bitcast.29), calls=%async_computation.1 | async-start | bytes 294912 | tf_op jit(solution)/shard_map/while/body/all_to_all | solution.py:354
  258.6 6.1 %gather_fusion = bf16[1024,320]{1,0:T(8,128)(2,1)S(1)} fusion(bf16[4096,320]{1,0:T(8,128)(2,1)} %get-tuple-element.285, s32[1024]{0:T(1024)S(1)} %broadcast_clamp_fusion.2), kind=kCustom, calls=%fused_computation.clone.1 | custom fusion | bytes 1314816 | tf_op jit(solution)/shard_map/while/body/jit(_take)/gather | solution.py:338
  283.0 14.2 %all_to_all.43 = f32[32,1,1152]{2,1,0:T(1,128)S(1)} all-to-all(f32[32,1,1152]{2,1,0:T(1,128)S(1)} %bitcast.41), channel_id=1, replica_groups={{0,8,16,24,32,40,48,56,64,72,80,88,96,104,112,120,128,136,144,152,160,1..., dimensions={0} | all-to-all | bytes 294912 | tf_op jit(solution)/shard_map/all_to_all | solution.py:354
  297.2 13.7 %all_to_all.44 = f32[32,1,1152]{2,1,0:T(1,128)S(1)} all-to-all(f32[32,1,1152]{2,1,0:T(1,128)S(1)} %bitcast.45), channel_id=1, replica_groups={{0,8,16,24,32,40,48,56,64,72,80,88,96,104,112,120,128,136,144,152,160,1..., dimensions={0} | all-to-all | bytes 294912 | tf_op jit(solution)/shard_map/all_to_all | solution.py:354
  325.9 12.5 %all_to_all.45 = f32[32,1,1152]{2,1,0:T(1,128)S(1)} all-to-all(f32[32,1,1152]{2,1,0:T(1,128)S(1)} %bitcast.43), channel_id=1, replica_groups={{0,8,16,24,32,40,48,56,64,72,80,88,96,104,112,120,128,136,144,152,160,1..., dimensions={0} | all-to-all | bytes 294912 | tf_op jit(solution)/shard_map/all_to_all | solution.py:354
  (163 shorter events, 141.3 us)
Async XLA Ops:
  9.8 18.5 %all-to-all-start.2 = ((f32[32,1,1152]{2,1,0:T(1,128)}), f32[32,1,1152]{2,1,0:T(1,128)S(1)}, u32[]{:S(2)}, u32[]{:S(2)}) async-start(f32[32,1,1152]{2,1,0:T(1,128)} %bitcast.7), calls=%async_computation.2 | async-start | bytes 294912 | tf_op jit(solution)/shard_map/all_to_all | solution.py:354
  29.0 14.5 %all-to-all-start.3 = ((f32[32,1,1152]{2,1,0:T(1,128)}), f32[32,1,1152]{2,1,0:T(1,128)S(1)}, u32[]{:S(2)}, u32[]{:S(2)}) async-start(f32[32,1,1152]{2,1,0:T(1,128)} %bitcast.9), calls=%async_computation.3 | async-start | bytes 294912 | tf_op jit(solution)/shard_map/all_to_all | solution.py:354
  47.7 4.8 %collective-permute-start.7 = (bf16[72,384]{1,0:T(8,128)(2,1)S(1)}, bf16[72,384]{1,0:T(8,128)(2,1)S(1)}, u32[]{:S(2)}, u32[]{:S(2)}) collective-permute-start(bf16[72,384]{1,0:T(8,128)(2,1)S(1)} %update.3.a), channel_id=1, source_target_pairs={{0,1},{1,2},{2,3},{3,0},{4,5},{5,6},{6,7},{7,4},{8,9},{9,10},{10,1... | collective-permute-start | bytes 165896 | tf_op jit(solution)/shard_map/ppermute | solution.py:348
  50.6 4.5 %collective-permute-start.9 = (bf16[72,384]{1,0:T(8,128)(2,1)S(1)}, bf16[72,384]{1,0:T(8,128)(2,1)S(1)}, u32[]{:S(2)}, u32[]{:S(2)}) collective-permute-start(bf16[72,384]{1,0:T(8,128)(2,1)S(1)} %update.3.a), channel_id=1, source_target_pairs={{0,2},{1,3},{2,0},{3,1},{4,6},{5,7},{6,4},{7,5},{8,10},{9,11},{10,... | collective-permute-start | bytes 165896 | tf_op jit(solution)/shard_map/ppermute | solution.py:348
  77.7 13.9 %all-to-all-start.1 = ((f32[32,1,1152]{2,1,0:T(1,128)}), f32[32,1,1152]{2,1,0:T(1,128)S(1)}, u32[]{:S(2)}, u32[]{:S(2)}) async-start(f32[32,1,1152]{2,1,0:T(1,128)} %bitcast.29), calls=%async_computation.1 | async-start | bytes 294912 | tf_op jit(solution)/shard_map/while/body/all_to_all | solution.py:354
  95.7 6.4 %collective-permute-start.2 = (bf16[72,384]{1,0:T(8,128)(2,1)S(1)}, bf16[72,384]{1,0:T(8,128)(2,1)S(1)}, u32[]{:S(2)}, u32[]{:S(2)}) collective-permute-start(bf16[72,384]{1,0:T(8,128)(2,1)S(1)} %update.5.a), channel_id=1, source_target_pairs={{0,1},{1,2},{2,3},{3,0},{4,5},{5,6},{6,7},{7,4},{8,9},{9,10},{10,1... | collective-permute-start | bytes 165896 | tf_op jit(solution)/shard_map/while/body/ppermute | solution.py:348
  95.9 6.2 %collective-permute-start.3 = (bf16[72,384]{1,0:T(8,128)(2,1)S(1)}, bf16[72,384]{1,0:T(8,128)(2,1)S(1)}, u32[]{:S(2)}, u32[]{:S(2)}) collective-permute-start(bf16[72,384]{1,0:T(8,128)(2,1)S(1)} %update.5.a), channel_id=1, source_target_pairs={{0,3},{1,0},{2,1},{3,2},{4,7},{5,4},{6,5},{7,6},{8,11},{9,8},{10,9... | collective-permute-start | bytes 165896 | tf_op jit(solution)/shard_map/while/body/ppermute | solution.py:348
  98.4 4.5 %collective-permute-start.4 = (bf16[72,384]{1,0:T(8,128)(2,1)S(1)}, bf16[72,384]{1,0:T(8,128)(2,1)S(1)}, u32[]{:S(2)}, u32[]{:S(2)}) collective-permute-start(bf16[72,384]{1,0:T(8,128)(2,1)S(1)} %update.5.a), channel_id=1, source_target_pairs={{0,2},{1,3},{2,0},{3,1},{4,6},{5,7},{6,4},{7,5},{8,10},{9,11},{10,... | collective-permute-start | bytes 165896 | tf_op jit(solution)/shard_map/while/body/ppermute | solution.py:348
  121.7 13.9 %all-to-all-start.1 = ((f32[32,1,1152]{2,1,0:T(1,128)}), f32[32,1,1152]{2,1,0:T(1,128)S(1)}, u32[]{:S(2)}, u32[]{:S(2)}) async-start(f32[32,1,1152]{2,1,0:T(1,128)} %bitcast.29), calls=%async_computation.1 | async-start | bytes 294912 | tf_op jit(solution)/shard_map/while/body/all_to_all | solution.py:354
  139.7 5.9 %collective-permute-start.2 = (bf16[72,384]{1,0:T(8,128)(2,1)S(1)}, bf16[72,384]{1,0:T(8,128)(2,1)S(1)}, u32[]{:S(2)}, u32[]{:S(2)}) collective-permute-start(bf16[72,384]{1,0:T(8,128)(2,1)S(1)} %update.5.a), channel_id=1, source_target_pairs={{0,1},{1,2},{2,3},{3,0},{4,5},{5,6},{6,7},{7,4},{8,9},{9,10},{10,1... | collective-permute-start | bytes 165896 | tf_op jit(solution)/shard_map/while/body/ppermute | solution.py:348
  139.8 5.8 %collective-permute-start.3 = (bf16[72,384]{1,0:T(8,128)(2,1)S(1)}, bf16[72,384]{1,0:T(8,128)(2,1)S(1)}, u32[]{:S(2)}, u32[]{:S(2)}) collective-permute-start(bf16[72,384]{1,0:T(8,128)(2,1)S(1)} %update.5.a), channel_id=1, source_target_pairs={{0,3},{1,0},{2,1},{3,2},{4,7},{5,4},{6,5},{7,6},{8,11},{9,8},{10,9... | collective-permute-start | bytes 165896 | tf_op jit(solution)/shard_map/while/body/ppermute | solution.py:348
  165.8 13.9 %all-to-all-start.1 = ((f32[32,1,1152]{2,1,0:T(1,128)}), f32[32,1,1152]{2,1,0:T(1,128)S(1)}, u32[]{:S(2)}, u32[]{:S(2)}) async-start(f32[32,1,1152]{2,1,0:T(1,128)} %bitcast.29), calls=%async_computation.1 | async-start | bytes 294912 | tf_op jit(solution)/shard_map/while/body/all_to_all | solution.py:354
  183.8 5.9 %collective-permute-start.2 = (bf16[72,384]{1,0:T(8,128)(2,1)S(1)}, bf16[72,384]{1,0:T(8,128)(2,1)S(1)}, u32[]{:S(2)}, u32[]{:S(2)}) collective-permute-start(bf16[72,384]{1,0:T(8,128)(2,1)S(1)} %update.5.a), channel_id=1, source_target_pairs={{0,1},{1,2},{2,3},{3,0},{4,5},{5,6},{6,7},{7,4},{8,9},{9,10},{10,1... | collective-permute-start | bytes 165896 | tf_op jit(solution)/shard_map/while/body/ppermute | solution.py:348
  183.9 5.8 %collective-permute-start.3 = (bf16[72,384]{1,0:T(8,128)(2,1)S(1)}, bf16[72,384]{1,0:T(8,128)(2,1)S(1)}, u32[]{:S(2)}, u32[]{:S(2)}) collective-permute-start(bf16[72,384]{1,0:T(8,128)(2,1)S(1)} %update.5.a), channel_id=1, source_target_pairs={{0,3},{1,0},{2,1},{3,2},{4,7},{5,4},{6,5},{7,6},{8,11},{9,8},{10,9... | collective-permute-start | bytes 165896 | tf_op jit(solution)/shard_map/while/body/ppermute | solution.py:348
  209.8 13.9 %all-to-all-start.1 = ((f32[32,1,1152]{2,1,0:T(1,128)}), f32[32,1,1152]{2,1,0:T(1,128)S(1)}, u32[]{:S(2)}, u32[]{:S(2)}) async-start(f32[32,1,1152]{2,1,0:T(1,128)} %bitcast.29), calls=%async_computation.1 | async-start | bytes 294912 | tf_op jit(solution)/shard_map/while/body/all_to_all | solution.py:354
  227.8 5.9 %collective-permute-start.2 = (bf16[72,384]{1,0:T(8,128)(2,1)S(1)}, bf16[72,384]{1,0:T(8,128)(2,1)S(1)}, u32[]{:S(2)}, u32[]{:S(2)}) collective-permute-start(bf16[72,384]{1,0:T(8,128)(2,1)S(1)} %update.5.a), channel_id=1, source_target_pairs={{0,1},{1,2},{2,3},{3,0},{4,5},{5,6},{6,7},{7,4},{8,9},{9,10},{10,1... | collective-permute-start | bytes 165896 | tf_op jit(solution)/shard_map/while/body/ppermute | solution.py:348
  227.9 5.8 %collective-permute-start.3 = (bf16[72,384]{1,0:T(8,128)(2,1)S(1)}, bf16[72,384]{1,0:T(8,128)(2,1)S(1)}, u32[]{:S(2)}, u32[]{:S(2)}) collective-permute-start(bf16[72,384]{1,0:T(8,128)(2,1)S(1)} %update.5.a), channel_id=1, source_target_pairs={{0,3},{1,0},{2,1},{3,2},{4,7},{5,4},{6,5},{7,6},{8,11},{9,8},{10,9... | collective-permute-start | bytes 165896 | tf_op jit(solution)/shard_map/while/body/ppermute | solution.py:348
  230.6 4.5 %collective-permute-start.4 = (bf16[72,384]{1,0:T(8,128)(2,1)S(1)}, bf16[72,384]{1,0:T(8,128)(2,1)S(1)}, u32[]{:S(2)}, u32[]{:S(2)}) collective-permute-start(bf16[72,384]{1,0:T(8,128)(2,1)S(1)} %update.5.a), channel_id=1, source_target_pairs={{0,2},{1,3},{2,0},{3,1},{4,6},{5,7},{6,4},{7,5},{8,10},{9,11},{10,... | collective-permute-start | bytes 165896 | tf_op jit(solution)/shard_map/while/body/ppermute | solution.py:348
  253.9 13.9 %all-to-all-start.1 = ((f32[32,1,1152]{2,1,0:T(1,128)}), f32[32,1,1152]{2,1,0:T(1,128)S(1)}, u32[]{:S(2)}, u32[]{:S(2)}) async-start(f32[32,1,1152]{2,1,0:T(1,128)} %bitcast.29), calls=%async_computation.1 | async-start | bytes 294912 | tf_op jit(solution)/shard_map/while/body/all_to_all | solution.py:354
  271.9 5.9 %collective-permute-start.2 = (bf16[72,384]{1,0:T(8,128)(2,1)S(1)}, bf16[72,384]{1,0:T(8,128)(2,1)S(1)}, u32[]{:S(2)}, u32[]{:S(2)}) collective-permute-start(bf16[72,384]{1,0:T(8,128)(2,1)S(1)} %update.5.a), channel_id=1, source_target_pairs={{0,1},{1,2},{2,3},{3,0},{4,5},{5,6},{6,7},{7,4},{8,9},{9,10},{10,1... | collective-permute-start | bytes 165896 | tf_op jit(solution)/shard_map/while/body/ppermute | solution.py:348
  272.0 5.8 %collective-permute-start.3 = (bf16[72,384]{1,0:T(8,128)(2,1)S(1)}, bf16[72,384]{1,0:T(8,128)(2,1)S(1)}, u32[]{:S(2)}, u32[]{:S(2)}) collective-permute-start(bf16[72,384]{1,0:T(8,128)(2,1)S(1)} %update.5.a), channel_id=1, source_target_pairs={{0,3},{1,0},{2,1},{3,2},{4,7},{5,4},{6,5},{7,6},{8,11},{9,8},{10,9... | collective-permute-start | bytes 165896 | tf_op jit(solution)/shard_map/while/body/ppermute | solution.py:348
  315.0 5.8 %collective-permute-start.12 = (bf16[72,384]{1,0:T(8,128)(2,1)S(1)}, bf16[72,384]{1,0:T(8,128)(2,1)S(1)}, u32[]{:S(2)}, u32[]{:S(2)}) collective-permute-start(bf16[72,384]{1,0:T(8,128)(2,1)S(1)} %update.4.a), channel_id=1, source_target_pairs={{0,1},{1,2},{2,3},{3,0},{4,5},{5,6},{6,7},{7,4},{8,9},{9,10},{10,1... | collective-permute-start | bytes 165896 | tf_op jit(solution)/shard_map/ppermute | solution.py:348
  315.1 5.7 %collective-permute-start.13 = (bf16[72,384]{1,0:T(8,128)(2,1)S(1)}, bf16[72,384]{1,0:T(8,128)(2,1)S(1)}, u32[]{:S(2)}, u32[]{:S(2)}) collective-permute-start(bf16[72,384]{1,0:T(8,128)(2,1)S(1)} %update.4.a), channel_id=1, source_target_pairs={{0,3},{1,0},{2,1},{3,2},{4,7},{5,4},{6,5},{7,6},{8,11},{9,8},{10,9... | collective-permute-start | bytes 165896 | tf_op jit(solution)/shard_map/ppermute | solution.py:348
  317.7 4.5 %collective-permute-start.14 = (bf16[72,384]{1,0:T(8,128)(2,1)S(1)}, bf16[72,384]{1,0:T(8,128)(2,1)S(1)}, u32[]{:S(2)}, u32[]{:S(2)}) collective-permute-start(bf16[72,384]{1,0:T(8,128)(2,1)S(1)} %update.4.a), channel_id=1, source_target_pairs={{0,2},{1,3},{2,0},{3,1},{4,6},{5,7},{6,4},{7,5},{8,10},{9,11},{10,... | collective-permute-start | bytes 165896 | tf_op jit(solution)/shard_map/ppermute | solution.py:348
  (24 other events, 105.7 us)

commit v8 on v6

--- a/solution.py
+++ b/solution.py
@@ -104,24 +104,23 @@
 
 def stepped_from(parts, previous, inverse, batch, left=0.0):
     comps, genes = previous.shape
-    total = sum(part[:comps, :genes].astype(f32) for part in parts) + left
+    total = sum(part[:comps, :genes] for part in parts) + left
     stepped = previous + STEP_RATE * (total * (1.0 / batch))
     if inverse is not None:
         stepped = lax.dot_general(inverse, stepped, NN, precision=HIGH, preferred_element_type=f32)
     return stepped
 
 
-def pair_rows(part, start, genes):
-    return part[start : start + 1, :genes].astype(f32) + part[start + 1 : start + 2, :genes].astype(f32)
+def row_of(part, start, genes):
+    return part[start : start + 1, :genes]
 
 
 def between_groups(parts, comps, genes, batch):
-    sums = [pair_rows(part, comps + 2, genes) for part in parts]
+    sums = [row_of(part, comps + 1, genes) for part in parts]
     mean = sum(sums) * (1.0 / batch)
     total = jnp.zeros((comps, genes), f32)
     for part, own in zip(parts, sums):
-        totals = part[:comps, genes : genes + 1].astype(f32) + part[:comps, genes + 1 : genes + 2].astype(f32)
-        total = total + totals * (own * (len(parts) / batch) - mean)
+        total = total + part[:comps, genes : genes + 1] * (own * (len(parts) / batch) - mean)
     return total
 
 
@@ -134,7 +133,7 @@
         left = 0.0 if normalised else between_groups(parts, comps, genes, batch)
         stepped = stepped_from(parts, previous_ref[...], inverse, batch, left)
         stepped_ref[...] = stepped
-        mean = sum(pair_rows(part, comps, genes) for part in parts) * (1.0 / batch)
+        mean = sum(row_of(part, comps, genes) for part in parts) * (1.0 / batch)
         mean_ref[...] = mean
         shift = jnp.sum(stepped * mean, axis=1, keepdims=True)
         pack_partial(stepped, tile_ref[...], shift, core_ref[0] == 0, keep_ref, send_ref)
@@ -200,21 +199,14 @@
         totals = jnp.sum(scores, axis=1, keepdims=True)
         mean = mean_ref[...] * (1.0 / cells) if cells else mean_ref[...]
         raw = both[:comps] + both[comps:] - totals * mean
-        rest = out_ref.shape[0] - comps - 4
-        tall = jnp.concatenate(
-            [
-                raw.astype(bf16),
-                split_pair(next_ref[...]),
-                split_pair(mean_ref[...]),
-                jnp.zeros((rest, genes), bf16),
-            ],
-            axis=0,
+        rest = out_ref.shape[0] - comps - 2
+        out_ref[:comps, :] = jnp.concatenate(
+            [raw, jnp.broadcast_to(totals, (comps, width - genes))], axis=1
         )
-        high = totals.astype(bf16)
-        low = (totals - high.astype(f32)).astype(bf16)
-        side = jnp.concatenate([high, low, jnp.zeros((comps, width - genes - 2), bf16)], axis=1)
-        side = jnp.concatenate([side, jnp.zeros((tall.shape[0] - comps, width - genes), bf16)], axis=0)
-        out_ref[...] = jnp.concatenate([tall, side], axis=1)
+        side = jnp.zeros((1, width - genes), f32)
+        out_ref[comps : comps + 1, :] = jnp.concatenate([next_ref[...], side], axis=1)
+        out_ref[comps + 1 : comps + 2, :] = jnp.concatenate([mean_ref[...], side], axis=1)
+        out_ref[comps + 2 :, :] = jnp.zeros((rest, width), f32)
 
     return kernel
 
@@ -358,7 +350,7 @@
     square = jax.ShapeDtypeStruct((comps, comps), f32)
     local = jax.ShapeDtypeStruct((comps, genes), f32)
     row = jax.ShapeDtypeStruct((1, genes), f32)
-    shared = jax.ShapeDtypeStruct((comps + 8, width), bf16)
+    shared = jax.ShapeDtypeStruct((comps + 8, width), f32)
 
     chunk = local_pool // 8
     keep, send = vmem_call(

time: 340 us -> 351 us (1.032)
  waiting for transfers between devices: 38.9 us -> 48.3 us
    ppermute x21, waiting for transfers between devices: 3.19 us -> 12.6 us  [round_cells(): lax.ppermute(value, 'cell', [(i, (i + k) % cell_devices) for i in range(c...]
    ppermute x21, starting transfers between devices: 26.3 us -> 30 us  [round_cells(): lax.ppermute(value, 'cell', [(i, (i + k) % cell_devices) for i in range(c...]
  transfers between devices with their start and end apart: 44 -> 44, of which waited for: 27 -> 29; matrix products, arithmetic and copies ran while one was open for 14% -> 13% of each run, Pallas kernels for 5% -> 5%
where the time goes in v8:
time: 351 us; the launch traced here: 350 us
  blocking collectives  115 us (33%)
  starting transfers between devices  100 us (28%)
  waiting for transfers between devices  48.3 us (14%)
  local copies, waits for them, and re-layouts  45.6 us (13%)
  Pallas kernels  38.8 us (11%)
    all_to_all x8, blocking collectives, exchange(): lax.all_to_all(pieces, 'gene', 0, 0, tiled=True, axis_index_groups=same_c...  115 us
    gather x6, local copies, waits for them, and re-layouts, tile_of(): return jnp.take(pool_by_cell, picks, axis=0, mode='clip')  39.8 us
    pallas_call x38, Pallas kernels, run(): return call(*args[:core], *near, *args[last:])  38.8 us
    all_to_all x7, starting transfers between devices, exchange(): lax.all_to_all(pieces, 'gene', 0, 0, tiled=True, axis_index_groups=same_c...  37.4 us
    ppermute x16, starting transfers between devices, swap_cores(): lax.ppermute(value, 'gene', [(i, i ^ 1) for i in range(gene_devices)])  33.1 us
    ppermute x21, starting transfers between devices, round_cells(): lax.ppermute(value, 'cell', [(i, (i + k) % cell_devices) for i in range(c...  30 us
    all_to_all x7, waiting for transfers between devices, exchange(): lax.all_to_all(pieces, 'gene', 0, 0, tiled=True, axis_index_groups=same_c...  21.9 us
    ppermute x16, waiting for transfers between devices, swap_cores(): lax.ppermute(value, 'gene', [(i, i ^ 1) for i in range(gene_devices)])  13.9 us
  transfers between devices with their start and end apart: 44, of which 29 were waited for; matrix products, arithmetic and copies ran while one was open for 13% of the time, Pallas kernels for 5%

profile of v8, /device:TPU:1, one launch (start us, length us, event | category | flops | bytes accessed | tf_op | source)
XLA Modules:
  0.0 350.3 jit_solution(8820265690784817650)
XLA Ops:
  0.0 4.8 %first.1 = (f32[288,128]{1,0:T(8,128)S(1)}, f32[288,128]{1,0:T(8,128)S(1)}) custom-call(s32[1]{0:T(128)} %bitcast.5.core_ref, s32[1]{0:T(128)} %bitcast.6.cell_ref, f32[64,320]{1,0:T(8,128)} %previous_ref.1, s32[7,1024]{1,0:T(8,128)} %picks_ref.1, bf16[320,4096]{1,0:T(8,128)(2,1)} %pool_ref.1), custom_call_target="tpu_custom_call" | custom-call | tf_op jit(solution)/shard_map/first/pallas_call | solution.py:35
  9.8 9.3 %all-to-all-start.2 = ((f32[32,1,1152]{2,1,0:T(1,128)}), f32[32,1,1152]{2,1,0:T(1,128)S(1)}, u32[]{:S(2)}, u32[]{:S(2)}) async-start(f32[32,1,1152]{2,1,0:T(1,128)} %bitcast.7), calls=%async_computation.2 | async-start | bytes 294912 | tf_op jit(solution)/shard_map/all_to_all | solution.py:346
  22.0 6.3 %all-to-all-done.2 = f32[32,1,1152]{2,1,0:T(1,128)S(1)} async-done(((f32[32,1,1152]{2,1,0:T(1,128)}), f32[32,1,1152]{2,1,0:T(1,128)S(1)}, u32[]{:S(2)}, u32[]{:S(2)}) %all-to-all-start.2) | async-done | bytes 147488 | tf_op jit(solution)/shard_map/all_to_all | solution.py:346
  29.0 4.7 %all-to-all-start.3 = ((f32[32,1,1152]{2,1,0:T(1,128)}), f32[32,1,1152]{2,1,0:T(1,128)S(1)}, u32[]{:S(2)}, u32[]{:S(2)}) async-start(f32[32,1,1152]{2,1,0:T(1,128)} %bitcast.9), calls=%async_computation.3 | async-start | bytes 294912 | tf_op jit(solution)/shard_map/all_to_all | solution.py:346
  33.7 9.5 %gather_fusion.1 = bf16[2048,320]{1,0:T(8,128)(2,1)S(1)} fusion(bf16[4096,320]{1,0:T(8,128)(2,1)} %bitcast.47, s32[2048]{0:T(1024)S(1)} %bitcast_clamp_fusion), kind=kCustom, calls=%fused_computation.1 | custom fusion | bytes 2629632 | tf_op jit(solution)/shard_map/jit(_take)/gather | solution.py:330
  57.7 226.8 %while.20 = (s32[]{:T(128)}, f32[288,128]{1,0:T(8,128)S(1)}, f32[288,128]{1,0:T(8,128)S(1)}, f32[64,320]{1,0:T(8,128)S(1)}, f32[1,320]{1,0:T(1,128)S(1)}, /*inde...) while((s32[]{:T(128)}, f32[288,128]{1,0:T(8,128)S(1)}, ...), condition=%wide.region_4.5_spmd, body=%wide.region_2.4_spmd.sunk | while | flops 1000656064 | bytes 6709387 | solution.py:408
  59.8 18.5 %all_to_all.46 = f32[32,1,1152]{2,1,0:T(1,128)S(1)} all-to-all(f32[32,1,1152]{2,1,0:T(1,128)S(1)} %bitcast.34), channel_id=1, replica_groups={{0,8,16,24,32,40,48,56,64,72,80,88,96,104,112,120,128,136,144,152,160,1..., dimensions={0} | all-to-all | bytes 294912 | tf_op jit(solution)/shard_map/while/body/all_to_all | solution.py:346
  79.0 4.7 %all-to-all-start.1 = ((f32[32,1,1152]{2,1,0:T(1,128)}), f32[32,1,1152]{2,1,0:T(1,128)S(1)}, u32[]{:S(2)}, u32[]{:S(2)}) async-start(f32[32,1,1152]{2,1,0:T(1,128)} %bitcast.29), calls=%async_computation.1 | async-start | bytes 294912 | tf_op jit(solution)/shard_map/while/body/all_to_all | solution.py:346
  83.6 6.1 %gather_fusion = bf16[1024,320]{1,0:T(8,128)(2,1)S(1)} fusion(bf16[4096,320]{1,0:T(8,128)(2,1)} %get-tuple-element.285, s32[1024]{0:T(1024)S(1)} %broadcast_clamp_fusion.2), kind=kCustom, calls=%fused_computation.clone.1 | custom fusion | bytes 1314816 | tf_op jit(solution)/shard_map/while/body/jit(_take)/gather | solution.py:330
  108.5 14.2 %all_to_all.46 = f32[32,1,1152]{2,1,0:T(1,128)S(1)} all-to-all(f32[32,1,1152]{2,1,0:T(1,128)S(1)} %bitcast.34), channel_id=1, replica_groups={{0,8,16,24,32,40,48,56,64,72,80,88,96,104,112,120,128,136,144,152,160,1..., dimensions={0} | all-to-all | bytes 294912 | tf_op jit(solution)/shard_map/while/body/all_to_all | solution.py:346
  123.4 4.7 %all-to-all-start.1 = ((f32[32,1,1152]{2,1,0:T(1,128)}), f32[32,1,1152]{2,1,0:T(1,128)S(1)}, u32[]{:S(2)}, u32[]{:S(2)}) async-start(f32[32,1,1152]{2,1,0:T(1,128)} %bitcast.29), calls=%async_computation.1 | async-start | bytes 294912 | tf_op jit(solution)/shard_map/while/body/all_to_all | solution.py:346
  128.1 6.1 %gather_fusion = bf16[1024,320]{1,0:T(8,128)(2,1)S(1)} fusion(bf16[4096,320]{1,0:T(8,128)(2,1)} %get-tuple-element.285, s32[1024]{0:T(1024)S(1)} %broadcast_clamp_fusion.2), kind=kCustom, calls=%fused_computation.clone.1 | custom fusion | bytes 1314816 | tf_op jit(solution)/shard_map/while/body/jit(_take)/gather | solution.py:330
  153.3 14.2 %all_to_all.46 = f32[32,1,1152]{2,1,0:T(1,128)S(1)} all-to-all(f32[32,1,1152]{2,1,0:T(1,128)S(1)} %bitcast.34), channel_id=1, replica_groups={{0,8,16,24,32,40,48,56,64,72,80,88,96,104,112,120,128,136,144,152,160,1..., dimensions={0} | all-to-all | bytes 294912 | tf_op jit(solution)/shard_map/while/body/all_to_all | solution.py:346
  168.1 4.7 %all-to-all-start.1 = ((f32[32,1,1152]{2,1,0:T(1,128)}), f32[32,1,1152]{2,1,0:T(1,128)S(1)}, u32[]{:S(2)}, u32[]{:S(2)}) async-start(f32[32,1,1152]{2,1,0:T(1,128)} %bitcast.29), calls=%async_computation.1 | async-start | bytes 294912 | tf_op jit(solution)/shard_map/while/body/all_to_all | solution.py:346
  172.8 6.1 %gather_fusion = bf16[1024,320]{1,0:T(8,128)(2,1)S(1)} fusion(bf16[4096,320]{1,0:T(8,128)(2,1)} %get-tuple-element.285, s32[1024]{0:T(1024)S(1)} %broadcast_clamp_fusion.2), kind=kCustom, calls=%fused_computation.clone.1 | custom fusion | bytes 1314816 | tf_op jit(solution)/shard_map/while/body/jit(_take)/gather | solution.py:330
  197.7 14.2 %all_to_all.46 = f32[32,1,1152]{2,1,0:T(1,128)S(1)} all-to-all(f32[32,1,1152]{2,1,0:T(1,128)S(1)} %bitcast.34), channel_id=1, replica_groups={{0,8,16,24,32,40,48,56,64,72,80,88,96,104,112,120,128,136,144,152,160,1..., dimensions={0} | all-to-all | bytes 294912 | tf_op jit(solution)/shard_map/while/body/all_to_all | solution.py:346
  212.5 4.7 %all-to-all-start.1 = ((f32[32,1,1152]{2,1,0:T(1,128)}), f32[32,1,1152]{2,1,0:T(1,128)S(1)}, u32[]{:S(2)}, u32[]{:S(2)}) async-start(f32[32,1,1152]{2,1,0:T(1,128)} %bitcast.29), calls=%async_computation.1 | async-start | bytes 294912 | tf_op jit(solution)/shard_map/while/body/all_to_all | solution.py:346
  217.2 6.1 %gather_fusion = bf16[1024,320]{1,0:T(8,128)(2,1)S(1)} fusion(bf16[4096,320]{1,0:T(8,128)(2,1)} %get-tuple-element.285, s32[1024]{0:T(1024)S(1)} %broadcast_clamp_fusion.2), kind=kCustom, calls=%fused_computation.clone.1 | custom fusion | bytes 1314816 | tf_op jit(solution)/shard_map/while/body/jit(_take)/gather | solution.py:330
  242.4 14.2 %all_to_all.46 = f32[32,1,1152]{2,1,0:T(1,128)S(1)} all-to-all(f32[32,1,1152]{2,1,0:T(1,128)S(1)} %bitcast.34), channel_id=1, replica_groups={{0,8,16,24,32,40,48,56,64,72,80,88,96,104,112,120,128,136,144,152,160,1..., dimensions={0} | all-to-all | bytes 294912 | tf_op jit(solution)/shard_map/while/body/all_to_all | solution.py:346
  257.3 4.7 %all-to-all-start.1 = ((f32[32,1,1152]{2,1,0:T(1,128)}), f32[32,1,1152]{2,1,0:T(1,128)S(1)}, u32[]{:S(2)}, u32[]{:S(2)}) async-start(f32[32,1,1152]{2,1,0:T(1,128)} %bitcast.29), calls=%async_computation.1 | async-start | bytes 294912 | tf_op jit(solution)/shard_map/while/body/all_to_all | solution.py:346
  262.0 6.1 %gather_fusion = bf16[1024,320]{1,0:T(8,128)(2,1)S(1)} fusion(bf16[4096,320]{1,0:T(8,128)(2,1)} %get-tuple-element.285, s32[1024]{0:T(1024)S(1)} %broadcast_clamp_fusion.2), kind=kCustom, calls=%fused_computation.clone.1 | custom fusion | bytes 1314816 | tf_op jit(solution)/shard_map/while/body/jit(_take)/gather | solution.py:330
  286.8 14.2 %all_to_all.43 = f32[32,1,1152]{2,1,0:T(1,128)S(1)} all-to-all(f32[32,1,1152]{2,1,0:T(1,128)S(1)} %bitcast.41), channel_id=1, replica_groups={{0,8,16,24,32,40,48,56,64,72,80,88,96,104,112,120,128,136,144,152,160,1..., dimensions={0} | all-to-all | bytes 294912 | tf_op jit(solution)/shard_map/all_to_all | solution.py:346
  301.0 13.7 %all_to_all.44 = f32[32,1,1152]{2,1,0:T(1,128)S(1)} all-to-all(f32[32,1,1152]{2,1,0:T(1,128)S(1)} %bitcast.45), channel_id=1, replica_groups={{0,8,16,24,32,40,48,56,64,72,80,88,96,104,112,120,128,136,144,152,160,1..., dimensions={0} | all-to-all | bytes 294912 | tf_op jit(solution)/shard_map/all_to_all | solution.py:346
  330.3 12.5 %all_to_all.45 = f32[32,1,1152]{2,1,0:T(1,128)S(1)} all-to-all(f32[32,1,1152]{2,1,0:T(1,128)S(1)} %bitcast.43), channel_id=1, replica_groups={{0,8,16,24,32,40,48,56,64,72,80,88,96,104,112,120,128,136,144,152,160,1..., dimensions={0} | all-to-all | bytes 294912 | tf_op jit(solution)/shard_map/all_to_all | solution.py:346
  (163 shorter events, 145.9 us)
Async XLA Ops:
  9.8 18.5 %all-to-all-start.2 = ((f32[32,1,1152]{2,1,0:T(1,128)}), f32[32,1,1152]{2,1,0:T(1,128)S(1)}, u32[]{:S(2)}, u32[]{:S(2)}) async-start(f32[32,1,1152]{2,1,0:T(1,128)} %bitcast.7), calls=%async_computation.2 | async-start | bytes 294912 | tf_op jit(solution)/shard_map/all_to_all | solution.py:346
  29.0 14.5 %all-to-all-start.3 = ((f32[32,1,1152]{2,1,0:T(1,128)}), f32[32,1,1152]{2,1,0:T(1,128)S(1)}, u32[]{:S(2)}, u32[]{:S(2)}) async-start(f32[32,1,1152]{2,1,0:T(1,128)} %bitcast.9), calls=%async_computation.3 | async-start | bytes 294912 | tf_op jit(solution)/shard_map/all_to_all | solution.py:346
  47.7 6.0 %collective-permute-start.7 = (f32[72,384]{1,0:T(8,128)S(1)}, f32[72,384]{1,0:T(8,128)S(1)}, u32[]{:S(2)}, u32[]{:S(2)}) collective-permute-start(f32[72,384]{1,0:T(8,128)S(1)} %update.3.a), channel_id=1, source_target_pairs={{0,1},{1,2},{2,3},{3,0},{4,5},{5,6},{6,7},{7,4},{8,9},{9,10},{10,1... | collective-permute-start | bytes 331784 | tf_op jit(solution)/shard_map/ppermute | solution.py:340
  49.1 8.1 %collective-permute-start.8 = (f32[72,384]{1,0:T(8,128)S(1)}, f32[72,384]{1,0:T(8,128)S(1)}, u32[]{:S(2)}, u32[]{:S(2)}) collective-permute-start(f32[72,384]{1,0:T(8,128)S(1)} %update.3.a), channel_id=1, source_target_pairs={{0,2},{1,3},{2,0},{3,1},{4,6},{5,7},{6,4},{7,5},{8,10},{9,11},{10,... | collective-permute-start | bytes 331784 | tf_op jit(solution)/shard_map/ppermute | solution.py:340
  51.7 5.5 %collective-permute-start.9 = (f32[72,384]{1,0:T(8,128)S(1)}, f32[72,384]{1,0:T(8,128)S(1)}, u32[]{:S(2)}, u32[]{:S(2)}) collective-permute-start(f32[72,384]{1,0:T(8,128)S(1)} %update.3.a), channel_id=1, source_target_pairs={{0,3},{1,0},{2,1},{3,2},{4,7},{5,4},{6,5},{7,6},{8,11},{9,8},{10,9... | collective-permute-start | bytes 331784 | tf_op jit(solution)/shard_map/ppermute | solution.py:340
  79.0 13.9 %all-to-all-start.1 = ((f32[32,1,1152]{2,1,0:T(1,128)}), f32[32,1,1152]{2,1,0:T(1,128)S(1)}, u32[]{:S(2)}, u32[]{:S(2)}) async-start(f32[32,1,1152]{2,1,0:T(1,128)} %bitcast.29), calls=%async_computation.1 | async-start | bytes 294912 | tf_op jit(solution)/shard_map/while/body/all_to_all | solution.py:346
  97.0 7.6 %collective-permute-start.2 = (f32[72,384]{1,0:T(8,128)S(1)}, f32[72,384]{1,0:T(8,128)S(1)}, u32[]{:S(2)}, u32[]{:S(2)}) collective-permute-start(f32[72,384]{1,0:T(8,128)S(1)} %update.5.a), channel_id=1, source_target_pairs={{0,1},{1,2},{2,3},{3,0},{4,5},{5,6},{6,7},{7,4},{8,9},{9,10},{10,1... | collective-permute-start | bytes 331784 | tf_op jit(solution)/shard_map/while/body/ppermute | solution.py:340
  98.0 7.3 %collective-permute-start.3 = (f32[72,384]{1,0:T(8,128)S(1)}, f32[72,384]{1,0:T(8,128)S(1)}, u32[]{:S(2)}, u32[]{:S(2)}) collective-permute-start(f32[72,384]{1,0:T(8,128)S(1)} %update.5.a), channel_id=1, source_target_pairs={{0,2},{1,3},{2,0},{3,1},{4,6},{5,7},{6,4},{7,5},{8,10},{9,11},{10,... | collective-permute-start | bytes 331784 | tf_op jit(solution)/shard_map/while/body/ppermute | solution.py:340
  100.1 5.2 %collective-permute-start.4 = (f32[72,384]{1,0:T(8,128)S(1)}, f32[72,384]{1,0:T(8,128)S(1)}, u32[]{:S(2)}, u32[]{:S(2)}) collective-permute-start(f32[72,384]{1,0:T(8,128)S(1)} %update.5.a), channel_id=1, source_target_pairs={{0,3},{1,0},{2,1},{3,2},{4,7},{5,4},{6,5},{7,6},{8,11},{9,8},{10,9... | collective-permute-start | bytes 331784 | tf_op jit(solution)/shard_map/while/body/ppermute | solution.py:340
  123.4 13.9 %all-to-all-start.1 = ((f32[32,1,1152]{2,1,0:T(1,128)}), f32[32,1,1152]{2,1,0:T(1,128)S(1)}, u32[]{:S(2)}, u32[]{:S(2)}) async-start(f32[32,1,1152]{2,1,0:T(1,128)} %bitcast.29), calls=%async_computation.1 | async-start | bytes 294912 | tf_op jit(solution)/shard_map/while/body/all_to_all | solution.py:346
  141.4 7.6 %collective-permute-start.2 = (f32[72,384]{1,0:T(8,128)S(1)}, f32[72,384]{1,0:T(8,128)S(1)}, u32[]{:S(2)}, u32[]{:S(2)}) collective-permute-start(f32[72,384]{1,0:T(8,128)S(1)} %update.5.a), channel_id=1, source_target_pairs={{0,1},{1,2},{2,3},{3,0},{4,5},{5,6},{6,7},{7,4},{8,9},{9,10},{10,1... | collective-permute-start | bytes 331784 | tf_op jit(solution)/shard_map/while/body/ppermute | solution.py:340
  142.9 7.3 %collective-permute-start.3 = (f32[72,384]{1,0:T(8,128)S(1)}, f32[72,384]{1,0:T(8,128)S(1)}, u32[]{:S(2)}, u32[]{:S(2)}) collective-permute-start(f32[72,384]{1,0:T(8,128)S(1)} %update.5.a), channel_id=1, source_target_pairs={{0,2},{1,3},{2,0},{3,1},{4,6},{5,7},{6,4},{7,5},{8,10},{9,11},{10,... | collective-permute-start | bytes 331784 | tf_op jit(solution)/shard_map/while/body/ppermute | solution.py:340
  145.1 5.2 %collective-permute-start.4 = (f32[72,384]{1,0:T(8,128)S(1)}, f32[72,384]{1,0:T(8,128)S(1)}, u32[]{:S(2)}, u32[]{:S(2)}) collective-permute-start(f32[72,384]{1,0:T(8,128)S(1)} %update.5.a), channel_id=1, source_target_pairs={{0,3},{1,0},{2,1},{3,2},{4,7},{5,4},{6,5},{7,6},{8,11},{9,8},{10,9... | collective-permute-start | bytes 331784 | tf_op jit(solution)/shard_map/while/body/ppermute | solution.py:340
  168.1 13.9 %all-to-all-start.1 = ((f32[32,1,1152]{2,1,0:T(1,128)}), f32[32,1,1152]{2,1,0:T(1,128)S(1)}, u32[]{:S(2)}, u32[]{:S(2)}) async-start(f32[32,1,1152]{2,1,0:T(1,128)} %bitcast.29), calls=%async_computation.1 | async-start | bytes 294912 | tf_op jit(solution)/shard_map/while/body/all_to_all | solution.py:346
  186.2 7.3 %collective-permute-start.2 = (f32[72,384]{1,0:T(8,128)S(1)}, f32[72,384]{1,0:T(8,128)S(1)}, u32[]{:S(2)}, u32[]{:S(2)}) collective-permute-start(f32[72,384]{1,0:T(8,128)S(1)} %update.5.a), channel_id=1, source_target_pairs={{0,1},{1,2},{2,3},{3,0},{4,5},{5,6},{6,7},{7,4},{8,9},{9,10},{10,1... | collective-permute-start | bytes 331784 | tf_op jit(solution)/shard_map/while/body/ppermute | solution.py:340
  187.3 7.3 %collective-permute-start.3 = (f32[72,384]{1,0:T(8,128)S(1)}, f32[72,384]{1,0:T(8,128)S(1)}, u32[]{:S(2)}, u32[]{:S(2)}) collective-permute-start(f32[72,384]{1,0:T(8,128)S(1)} %update.5.a), channel_id=1, source_target_pairs={{0,2},{1,3},{2,0},{3,1},{4,6},{5,7},{6,4},{7,5},{8,10},{9,11},{10,... | collective-permute-start | bytes 331784 | tf_op jit(solution)/shard_map/while/body/ppermute | solution.py:340
  212.5 13.9 %all-to-all-start.1 = ((f32[32,1,1152]{2,1,0:T(1,128)}), f32[32,1,1152]{2,1,0:T(1,128)S(1)}, u32[]{:S(2)}, u32[]{:S(2)}) async-start(f32[32,1,1152]{2,1,0:T(1,128)} %bitcast.29), calls=%async_computation.1 | async-start | bytes 294912 | tf_op jit(solution)/shard_map/while/body/all_to_all | solution.py:346
  230.6 7.3 %collective-permute-start.2 = (f32[72,384]{1,0:T(8,128)S(1)}, f32[72,384]{1,0:T(8,128)S(1)}, u32[]{:S(2)}, u32[]{:S(2)}) collective-permute-start(f32[72,384]{1,0:T(8,128)S(1)} %update.5.a), channel_id=1, source_target_pairs={{0,1},{1,2},{2,3},{3,0},{4,5},{5,6},{6,7},{7,4},{8,9},{9,10},{10,1... | collective-permute-start | bytes 331784 | tf_op jit(solution)/shard_map/while/body/ppermute | solution.py:340
  232.1 7.3 %collective-permute-start.3 = (f32[72,384]{1,0:T(8,128)S(1)}, f32[72,384]{1,0:T(8,128)S(1)}, u32[]{:S(2)}, u32[]{:S(2)}) collective-permute-start(f32[72,384]{1,0:T(8,128)S(1)} %update.5.a), channel_id=1, source_target_pairs={{0,2},{1,3},{2,0},{3,1},{4,6},{5,7},{6,4},{7,5},{8,10},{9,11},{10,... | collective-permute-start | bytes 331784 | tf_op jit(solution)/shard_map/while/body/ppermute | solution.py:340
  257.3 13.9 %all-to-all-start.1 = ((f32[32,1,1152]{2,1,0:T(1,128)}), f32[32,1,1152]{2,1,0:T(1,128)S(1)}, u32[]{:S(2)}, u32[]{:S(2)}) async-start(f32[32,1,1152]{2,1,0:T(1,128)} %bitcast.29), calls=%async_computation.1 | async-start | bytes 294912 | tf_op jit(solution)/shard_map/while/body/all_to_all | solution.py:346
  275.3 7.0 %collective-permute-start.2 = (f32[72,384]{1,0:T(8,128)S(1)}, f32[72,384]{1,0:T(8,128)S(1)}, u32[]{:S(2)}, u32[]{:S(2)}) collective-permute-start(f32[72,384]{1,0:T(8,128)S(1)} %update.5.a), channel_id=1, source_target_pairs={{0,1},{1,2},{2,3},{3,0},{4,5},{5,6},{6,7},{7,4},{8,9},{9,10},{10,1... | collective-permute-start | bytes 331784 | tf_op jit(solution)/shard_map/while/body/ppermute | solution.py:340
  276.5 7.3 %collective-permute-start.3 = (f32[72,384]{1,0:T(8,128)S(1)}, f32[72,384]{1,0:T(8,128)S(1)}, u32[]{:S(2)}, u32[]{:S(2)}) collective-permute-start(f32[72,384]{1,0:T(8,128)S(1)} %update.5.a), channel_id=1, source_target_pairs={{0,2},{1,3},{2,0},{3,1},{4,6},{5,7},{6,4},{7,5},{8,10},{9,11},{10,... | collective-permute-start | bytes 331784 | tf_op jit(solution)/shard_map/while/body/ppermute | solution.py:340
  318.7 6.9 %collective-permute-start.12 = (f32[72,384]{1,0:T(8,128)S(1)}, f32[72,384]{1,0:T(8,128)S(1)}, u32[]{:S(2)}, u32[]{:S(2)}) collective-permute-start(f32[72,384]{1,0:T(8,128)S(1)} %update.4.a), channel_id=1, source_target_pairs={{0,1},{1,2},{2,3},{3,0},{4,5},{5,6},{6,7},{7,4},{8,9},{9,10},{10,1... | collective-permute-start | bytes 331784 | tf_op jit(solution)/shard_map/ppermute | solution.py:340
  319.9 7.7 %collective-permute-start.13 = (f32[72,384]{1,0:T(8,128)S(1)}, f32[72,384]{1,0:T(8,128)S(1)}, u32[]{:S(2)}, u32[]{:S(2)}) collective-permute-start(f32[72,384]{1,0:T(8,128)S(1)} %update.4.a), channel_id=1, source_target_pairs={{0,2},{1,3},{2,0},{3,1},{4,6},{5,7},{6,4},{7,5},{8,10},{9,11},{10,... | collective-permute-start | bytes 331784 | tf_op jit(solution)/shard_map/ppermute | solution.py:340
  (24 other events, 105.9 us)

commit v9 on v8

--- a/solution.py
+++ b/solution.py
@@ -115,6 +115,11 @@
     return part[start : start + 1, :genes]
 
 
+def spare_row(part, genes):
+    spare = part.shape[1] - genes
+    return jnp.concatenate([part[i : i + 1, genes:] for i in range(genes // spare)], axis=1)
+
+
 def between_groups(parts, comps, genes, batch):
     sums = [row_of(part, comps + 1, genes) for part in parts]
     mean = sum(sums) * (1.0 / batch)
@@ -133,7 +138,9 @@
         left = 0.0 if normalised else between_groups(parts, comps, genes, batch)
         stepped = stepped_from(parts, previous_ref[...], inverse, batch, left)
         stepped_ref[...] = stepped
-        mean = sum(row_of(part, comps, genes) for part in parts) * (1.0 / batch)
+        mean = sum(
+            spare_row(part, genes) if normalised else row_of(part, comps, genes) for part in parts
+        ) * (1.0 / batch)
         mean_ref[...] = mean
         shift = jnp.sum(stepped * mean, axis=1, keepdims=True)
         pack_partial(stepped, tile_ref[...], shift, core_ref[0] == 0, keep_ref, send_ref)
@@ -199,14 +206,19 @@
         totals = jnp.sum(scores, axis=1, keepdims=True)
         mean = mean_ref[...] * (1.0 / cells) if cells else mean_ref[...]
         raw = both[:comps] + both[comps:] - totals * mean
-        rest = out_ref.shape[0] - comps - 2
-        out_ref[:comps, :] = jnp.concatenate(
-            [raw, jnp.broadcast_to(totals, (comps, width - genes))], axis=1
-        )
-        side = jnp.zeros((1, width - genes), f32)
-        out_ref[comps : comps + 1, :] = jnp.concatenate([next_ref[...], side], axis=1)
-        out_ref[comps + 1 : comps + 2, :] = jnp.concatenate([mean_ref[...], side], axis=1)
-        out_ref[comps + 2 :, :] = jnp.zeros((rest, width), f32)
+        spare = width - genes
+        if cells:
+            side = jnp.zeros((1, spare), f32)
+            rest = out_ref.shape[0] - comps - 2
+            out_ref[:comps, :] = jnp.concatenate([raw, jnp.broadcast_to(totals, (comps, spare))], axis=1)
+            out_ref[comps : comps + 1, :] = jnp.concatenate([next_ref[...], side], axis=1)
+            out_ref[comps + 1 : comps + 2, :] = jnp.concatenate([mean_ref[...], side], axis=1)
+            out_ref[comps + 2 :, :] = jnp.zeros((rest, width), f32)
+        else:
+            sums = next_ref[...]
+            pieces = [sums[:, i : i + spare] for i in range(0, genes, spare)]
+            pieces.append(jnp.zeros((comps - len(pieces), spare), f32))
+            out_ref[...] = jnp.concatenate([raw, jnp.concatenate(pieces, axis=0)], axis=1)
 
     return kernel
 
@@ -350,7 +362,6 @@
     square = jax.ShapeDtypeStruct((comps, comps), f32)
     local = jax.ShapeDtypeStruct((comps, genes), f32)
     row = jax.ShapeDtypeStruct((1, genes), f32)
-    shared = jax.ShapeDtypeStruct((comps + 8, width), f32)
 
     chunk = local_pool // 8
     keep, send = vmem_call(
@@ -376,6 +387,7 @@
         return mine, swap_cores(mine), later
 
     def change_of(mine, other, tile, mean, next_sums, own=None):
+        shared = jax.ShapeDtypeStruct((comps + 8 if own else comps, width), f32)
         change = vmem_call(make_update(half, rows, own), shared, 5, name="update")(
             core, mine, other, tile, mean, next_sums
         )

time: 351 us -> 348 us (level)
  transfers between devices with their start and end apart: 44 -> 44, of which waited for: 29 -> 32; matrix products, arithmetic and copies ran while one was open for 13% -> 13% of each run, Pallas kernels for 5% -> 5%
where the time goes in v9:
time: 348 us; the launch traced here: 347 us
  blocking collectives  115 us (33%)
  starting transfers between devices  99.6 us (29%)
  waiting for transfers between devices  46 us (13%)
  local copies, waits for them, and re-layouts  45.6 us (13%)
  Pallas kernels  38.8 us (11%)
    all_to_all x8, blocking collectives, exchange(): lax.all_to_all(pieces, 'gene', 0, 0, tiled=True, axis_index_groups=same_c...  115 us
    gather x6, local copies, waits for them, and re-layouts, tile_of(): return jnp.take(pool_by_cell, picks, axis=0, mode='clip')  39.8 us
    pallas_call x38, Pallas kernels, run(): return call(*args[:core], *near, *args[last:])  38.8 us
    all_to_all x7, starting transfers between devices, exchange(): lax.all_to_all(pieces, 'gene', 0, 0, tiled=True, axis_index_groups=same_c...  37.4 us
    ppermute x16, starting transfers between devices, swap_cores(): lax.ppermute(value, 'gene', [(i, i ^ 1) for i in range(gene_devices)])  32.7 us
    ppermute x21, starting transfers between devices, round_cells(): lax.ppermute(value, 'cell', [(i, (i + k) % cell_devices) for i in range(c...  29.6 us
    all_to_all x7, waiting for transfers between devices, exchange(): lax.all_to_all(pieces, 'gene', 0, 0, tiled=True, axis_index_groups=same_c...  21.9 us
    ppermute x16, waiting for transfers between devices, swap_cores(): lax.ppermute(value, 'gene', [(i, i ^ 1) for i in range(gene_devices)])  13.9 us
  transfers between devices with their start and end apart: 44, of which 32 were waited for; matrix products, arithmetic and copies ran while one was open for 13% of the time, Pallas kernels for 5%

profile of v9, /device:TPU:1, one launch (start us, length us, event | category | flops | bytes accessed | tf_op | source)
XLA Modules:
  0.0 347.1 jit_solution(17366230678665664915)
XLA Ops:
  0.0 4.8 %first.1 = (f32[288,128]{1,0:T(8,128)S(1)}, f32[288,128]{1,0:T(8,128)S(1)}) custom-call(s32[1]{0:T(128)} %bitcast.5.core_ref, s32[1]{0:T(128)} %bitcast.6.cell_ref, f32[64,320]{1,0:T(8,128)} %previous_ref.1, s32[7,1024]{1,0:T(8,128)} %picks_ref.1, bf16[320,4096]{1,0:T(8,128)(2,1)} %pool_ref.1), custom_call_target="tpu_custom_call" | custom-call | tf_op jit(solution)/shard_map/first/pallas_call | solution.py:35
  9.8 9.3 %all-to-all-start.2 = ((f32[32,1,1152]{2,1,0:T(1,128)}), f32[32,1,1152]{2,1,0:T(1,128)S(1)}, u32[]{:S(2)}, u32[]{:S(2)}) async-start(f32[32,1,1152]{2,1,0:T(1,128)} %bitcast.7), calls=%async_computation.2 | async-start | bytes 294912 | tf_op jit(solution)/shard_map/all_to_all | solution.py:358
  22.0 6.3 %all-to-all-done.2 = f32[32,1,1152]{2,1,0:T(1,128)S(1)} async-done(((f32[32,1,1152]{2,1,0:T(1,128)}), f32[32,1,1152]{2,1,0:T(1,128)S(1)}, u32[]{:S(2)}, u32[]{:S(2)}) %all-to-all-start.2) | async-done | bytes 147488 | tf_op jit(solution)/shard_map/all_to_all | solution.py:358
  29.0 4.7 %all-to-all-start.3 = ((f32[32,1,1152]{2,1,0:T(1,128)}), f32[32,1,1152]{2,1,0:T(1,128)S(1)}, u32[]{:S(2)}, u32[]{:S(2)}) async-start(f32[32,1,1152]{2,1,0:T(1,128)} %bitcast.9), calls=%async_computation.3 | async-start | bytes 294912 | tf_op jit(solution)/shard_map/all_to_all | solution.py:358
  33.7 9.5 %gather_fusion.1 = bf16[2048,320]{1,0:T(8,128)(2,1)S(1)} fusion(bf16[4096,320]{1,0:T(8,128)(2,1)} %bitcast.47, s32[2048]{0:T(1024)S(1)} %bitcast_clamp_fusion), kind=kCustom, calls=%fused_computation.1 | custom fusion | bytes 2629632 | tf_op jit(solution)/shard_map/jit(_take)/gather | solution.py:342
  57.7 224.3 %while.20 = (s32[]{:T(128)}, f32[288,128]{1,0:T(8,128)S(1)}, f32[288,128]{1,0:T(8,128)S(1)}, f32[64,320]{1,0:T(8,128)S(1)}, f32[1,320]{1,0:T(1,128)S(1)}, /*inde...) while((s32[]{:T(128)}, f32[288,128]{1,0:T(8,128)S(1)}, ...), condition=%wide.region_4.5_spmd, body=%wide.region_2.4_spmd.sunk | while | flops 1000656064 | bytes 6561931 | solution.py:420
  59.8 18.5 %all_to_all.46 = f32[32,1,1152]{2,1,0:T(1,128)S(1)} all-to-all(f32[32,1,1152]{2,1,0:T(1,128)S(1)} %bitcast.34), channel_id=1, replica_groups={{0,8,16,24,32,40,48,56,64,72,80,88,96,104,112,120,128,136,144,152,160,1..., dimensions={0} | all-to-all | bytes 294912 | tf_op jit(solution)/shard_map/while/body/all_to_all | solution.py:358
  79.0 4.7 %all-to-all-start.1 = ((f32[32,1,1152]{2,1,0:T(1,128)}), f32[32,1,1152]{2,1,0:T(1,128)S(1)}, u32[]{:S(2)}, u32[]{:S(2)}) async-start(f32[32,1,1152]{2,1,0:T(1,128)} %bitcast.29), calls=%async_computation.1 | async-start | bytes 294912 | tf_op jit(solution)/shard_map/while/body/all_to_all | solution.py:358
  83.6 6.1 %gather_fusion = bf16[1024,320]{1,0:T(8,128)(2,1)S(1)} fusion(bf16[4096,320]{1,0:T(8,128)(2,1)} %get-tuple-element.285, s32[1024]{0:T(1024)S(1)} %broadcast_clamp_fusion.2), kind=kCustom, calls=%fused_computation.clone.1 | custom fusion | bytes 1314816 | tf_op jit(solution)/shard_map/while/body/jit(_take)/gather | solution.py:342
  108.0 14.2 %all_to_all.46 = f32[32,1,1152]{2,1,0:T(1,128)S(1)} all-to-all(f32[32,1,1152]{2,1,0:T(1,128)S(1)} %bitcast.34), channel_id=1, replica_groups={{0,8,16,24,32,40,48,56,64,72,80,88,96,104,112,120,128,136,144,152,160,1..., dimensions={0} | all-to-all | bytes 294912 | tf_op jit(solution)/shard_map/while/body/all_to_all | solution.py:358
  122.9 4.7 %all-to-all-start.1 = ((f32[32,1,1152]{2,1,0:T(1,128)}), f32[32,1,1152]{2,1,0:T(1,128)S(1)}, u32[]{:S(2)}, u32[]{:S(2)}) async-start(f32[32,1,1152]{2,1,0:T(1,128)} %bitcast.29), calls=%async_computation.1 | async-start | bytes 294912 | tf_op jit(solution)/shard_map/while/body/all_to_all | solution.py:358
  127.6 6.1 %gather_fusion = bf16[1024,320]{1,0:T(8,128)(2,1)S(1)} fusion(bf16[4096,320]{1,0:T(8,128)(2,1)} %get-tuple-element.285, s32[1024]{0:T(1024)S(1)} %broadcast_clamp_fusion.2), kind=kCustom, calls=%fused_computation.clone.1 | custom fusion | bytes 1314816 | tf_op jit(solution)/shard_map/while/body/jit(_take)/gather | solution.py:342
  152.3 14.2 %all_to_all.46 = f32[32,1,1152]{2,1,0:T(1,128)S(1)} all-to-all(f32[32,1,1152]{2,1,0:T(1,128)S(1)} %bitcast.34), channel_id=1, replica_groups={{0,8,16,24,32,40,48,56,64,72,80,88,96,104,112,120,128,136,144,152,160,1..., dimensions={0} | all-to-all | bytes 294912 | tf_op jit(solution)/shard_map/while/body/all_to_all | solution.py:358
  167.1 4.7 %all-to-all-start.1 = ((f32[32,1,1152]{2,1,0:T(1,128)}), f32[32,1,1152]{2,1,0:T(1,128)S(1)}, u32[]{:S(2)}, u32[]{:S(2)}) async-start(f32[32,1,1152]{2,1,0:T(1,128)} %bitcast.29), calls=%async_computation.1 | async-start | bytes 294912 | tf_op jit(solution)/shard_map/while/body/all_to_all | solution.py:358
  171.8 6.1 %gather_fusion = bf16[1024,320]{1,0:T(8,128)(2,1)S(1)} fusion(bf16[4096,320]{1,0:T(8,128)(2,1)} %get-tuple-element.285, s32[1024]{0:T(1024)S(1)} %broadcast_clamp_fusion.2), kind=kCustom, calls=%fused_computation.clone.1 | custom fusion | bytes 1314816 | tf_op jit(solution)/shard_map/while/body/jit(_take)/gather | solution.py:342
  196.2 14.2 %all_to_all.46 = f32[32,1,1152]{2,1,0:T(1,128)S(1)} all-to-all(f32[32,1,1152]{2,1,0:T(1,128)S(1)} %bitcast.34), channel_id=1, replica_groups={{0,8,16,24,32,40,48,56,64,72,80,88,96,104,112,120,128,136,144,152,160,1..., dimensions={0} | all-to-all | bytes 294912 | tf_op jit(solution)/shard_map/while/body/all_to_all | solution.py:358
  211.1 4.7 %all-to-all-start.1 = ((f32[32,1,1152]{2,1,0:T(1,128)}), f32[32,1,1152]{2,1,0:T(1,128)S(1)}, u32[]{:S(2)}, u32[]{:S(2)}) async-start(f32[32,1,1152]{2,1,0:T(1,128)} %bitcast.29), calls=%async_computation.1 | async-start | bytes 294912 | tf_op jit(solution)/shard_map/while/body/all_to_all | solution.py:358
  215.8 6.1 %gather_fusion = bf16[1024,320]{1,0:T(8,128)(2,1)S(1)} fusion(bf16[4096,320]{1,0:T(8,128)(2,1)} %get-tuple-element.285, s32[1024]{0:T(1024)S(1)} %broadcast_clamp_fusion.2), kind=kCustom, calls=%fused_computation.clone.1 | custom fusion | bytes 1314816 | tf_op jit(solution)/shard_map/while/body/jit(_take)/gather | solution.py:342
  240.4 14.2 %all_to_all.46 = f32[32,1,1152]{2,1,0:T(1,128)S(1)} all-to-all(f32[32,1,1152]{2,1,0:T(1,128)S(1)} %bitcast.34), channel_id=1, replica_groups={{0,8,16,24,32,40,48,56,64,72,80,88,96,104,112,120,128,136,144,152,160,1..., dimensions={0} | all-to-all | bytes 294912 | tf_op jit(solution)/shard_map/while/body/all_to_all | solution.py:358
  255.2 4.7 %all-to-all-start.1 = ((f32[32,1,1152]{2,1,0:T(1,128)}), f32[32,1,1152]{2,1,0:T(1,128)S(1)}, u32[]{:S(2)}, u32[]{:S(2)}) async-start(f32[32,1,1152]{2,1,0:T(1,128)} %bitcast.29), calls=%async_computation.1 | async-start | bytes 294912 | tf_op jit(solution)/shard_map/while/body/all_to_all | solution.py:358
  259.9 6.1 %gather_fusion = bf16[1024,320]{1,0:T(8,128)(2,1)S(1)} fusion(bf16[4096,320]{1,0:T(8,128)(2,1)} %get-tuple-element.285, s32[1024]{0:T(1024)S(1)} %broadcast_clamp_fusion.2), kind=kCustom, calls=%fused_computation.clone.1 | custom fusion | bytes 1314816 | tf_op jit(solution)/shard_map/while/body/jit(_take)/gather | solution.py:342
  284.3 14.2 %all_to_all.43 = f32[32,1,1152]{2,1,0:T(1,128)S(1)} all-to-all(f32[32,1,1152]{2,1,0:T(1,128)S(1)} %bitcast.41), channel_id=1, replica_groups={{0,8,16,24,32,40,48,56,64,72,80,88,96,104,112,120,128,136,144,152,160,1..., dimensions={0} | all-to-all | bytes 294912 | tf_op jit(solution)/shard_map/all_to_all | solution.py:358
  298.4 13.7 %all_to_all.44 = f32[32,1,1152]{2,1,0:T(1,128)S(1)} all-to-all(f32[32,1,1152]{2,1,0:T(1,128)S(1)} %bitcast.45), channel_id=1, replica_groups={{0,8,16,24,32,40,48,56,64,72,80,88,96,104,112,120,128,136,144,152,160,1..., dimensions={0} | all-to-all | bytes 294912 | tf_op jit(solution)/shard_map/all_to_all | solution.py:358
  327.2 12.5 %all_to_all.45 = f32[32,1,1152]{2,1,0:T(1,128)S(1)} all-to-all(f32[32,1,1152]{2,1,0:T(1,128)S(1)} %bitcast.43), channel_id=1, replica_groups={{0,8,16,24,32,40,48,56,64,72,80,88,96,104,112,120,128,136,144,152,160,1..., dimensions={0} | all-to-all | bytes 294912 | tf_op jit(solution)/shard_map/all_to_all | solution.py:358
  (163 shorter events, 142.8 us)
Async XLA Ops:
  9.8 18.5 %all-to-all-start.2 = ((f32[32,1,1152]{2,1,0:T(1,128)}), f32[32,1,1152]{2,1,0:T(1,128)S(1)}, u32[]{:S(2)}, u32[]{:S(2)}) async-start(f32[32,1,1152]{2,1,0:T(1,128)} %bitcast.7), calls=%async_computation.2 | async-start | bytes 294912 | tf_op jit(solution)/shard_map/all_to_all | solution.py:358
  29.0 14.5 %all-to-all-start.3 = ((f32[32,1,1152]{2,1,0:T(1,128)}), f32[32,1,1152]{2,1,0:T(1,128)S(1)}, u32[]{:S(2)}, u32[]{:S(2)}) async-start(f32[32,1,1152]{2,1,0:T(1,128)} %bitcast.9), calls=%async_computation.3 | async-start | bytes 294912 | tf_op jit(solution)/shard_map/all_to_all | solution.py:358
  47.7 6.0 %collective-permute-start.7 = (f32[72,384]{1,0:T(8,128)S(1)}, f32[72,384]{1,0:T(8,128)S(1)}, u32[]{:S(2)}, u32[]{:S(2)}) collective-permute-start(f32[72,384]{1,0:T(8,128)S(1)} %update.3.a), channel_id=1, source_target_pairs={{0,1},{1,2},{2,3},{3,0},{4,5},{5,6},{6,7},{7,4},{8,9},{9,10},{10,1... | collective-permute-start | bytes 331784 | tf_op jit(solution)/shard_map/ppermute | solution.py:352
  49.1 8.1 %collective-permute-start.8 = (f32[72,384]{1,0:T(8,128)S(1)}, f32[72,384]{1,0:T(8,128)S(1)}, u32[]{:S(2)}, u32[]{:S(2)}) collective-permute-start(f32[72,384]{1,0:T(8,128)S(1)} %update.3.a), channel_id=1, source_target_pairs={{0,2},{1,3},{2,0},{3,1},{4,6},{5,7},{6,4},{7,5},{8,10},{9,11},{10,... | collective-permute-start | bytes 331784 | tf_op jit(solution)/shard_map/ppermute | solution.py:352
  51.7 5.5 %collective-permute-start.9 = (f32[72,384]{1,0:T(8,128)S(1)}, f32[72,384]{1,0:T(8,128)S(1)}, u32[]{:S(2)}, u32[]{:S(2)}) collective-permute-start(f32[72,384]{1,0:T(8,128)S(1)} %update.3.a), channel_id=1, source_target_pairs={{0,3},{1,0},{2,1},{3,2},{4,7},{5,4},{6,5},{7,6},{8,11},{9,8},{10,9... | collective-permute-start | bytes 331784 | tf_op jit(solution)/shard_map/ppermute | solution.py:352
  79.0 13.9 %all-to-all-start.1 = ((f32[32,1,1152]{2,1,0:T(1,128)}), f32[32,1,1152]{2,1,0:T(1,128)S(1)}, u32[]{:S(2)}, u32[]{:S(2)}) async-start(f32[32,1,1152]{2,1,0:T(1,128)} %bitcast.29), calls=%async_computation.1 | async-start | bytes 294912 | tf_op jit(solution)/shard_map/while/body/all_to_all | solution.py:358
  97.0 7.6 %collective-permute-start.2 = (f32[64,384]{1,0:T(8,128)S(1)}, f32[64,384]{1,0:T(8,128)S(1)}, u32[]{:S(2)}, u32[]{:S(2)}) collective-permute-start(f32[64,384]{1,0:T(8,128)S(1)} %update.5.a), channel_id=1, source_target_pairs={{0,1},{1,2},{2,3},{3,0},{4,5},{5,6},{6,7},{7,4},{8,9},{9,10},{10,1... | collective-permute-start | bytes 294920 | tf_op jit(solution)/shard_map/while/body/ppermute | solution.py:352
  98.0 6.7 %collective-permute-start.3 = (f32[64,384]{1,0:T(8,128)S(1)}, f32[64,384]{1,0:T(8,128)S(1)}, u32[]{:S(2)}, u32[]{:S(2)}) collective-permute-start(f32[64,384]{1,0:T(8,128)S(1)} %update.5.a), channel_id=1, source_target_pairs={{0,2},{1,3},{2,0},{3,1},{4,6},{5,7},{6,4},{7,5},{8,10},{9,11},{10,... | collective-permute-start | bytes 294920 | tf_op jit(solution)/shard_map/while/body/ppermute | solution.py:352
  100.1 4.8 %collective-permute-start.4 = (f32[64,384]{1,0:T(8,128)S(1)}, f32[64,384]{1,0:T(8,128)S(1)}, u32[]{:S(2)}, u32[]{:S(2)}) collective-permute-start(f32[64,384]{1,0:T(8,128)S(1)} %update.5.a), channel_id=1, source_target_pairs={{0,3},{1,0},{2,1},{3,2},{4,7},{5,4},{6,5},{7,6},{8,11},{9,8},{10,9... | collective-permute-start | bytes 294920 | tf_op jit(solution)/shard_map/while/body/ppermute | solution.py:352
  122.9 13.9 %all-to-all-start.1 = ((f32[32,1,1152]{2,1,0:T(1,128)}), f32[32,1,1152]{2,1,0:T(1,128)S(1)}, u32[]{:S(2)}, u32[]{:S(2)}) async-start(f32[32,1,1152]{2,1,0:T(1,128)} %bitcast.29), calls=%async_computation.1 | async-start | bytes 294912 | tf_op jit(solution)/shard_map/while/body/all_to_all | solution.py:358
  140.9 7.6 %collective-permute-start.2 = (f32[64,384]{1,0:T(8,128)S(1)}, f32[64,384]{1,0:T(8,128)S(1)}, u32[]{:S(2)}, u32[]{:S(2)}) collective-permute-start(f32[64,384]{1,0:T(8,128)S(1)} %update.5.a), channel_id=1, source_target_pairs={{0,1},{1,2},{2,3},{3,0},{4,5},{5,6},{6,7},{7,4},{8,9},{9,10},{10,1... | collective-permute-start | bytes 294920 | tf_op jit(solution)/shard_map/while/body/ppermute | solution.py:352
  142.4 6.9 %collective-permute-start.3 = (f32[64,384]{1,0:T(8,128)S(1)}, f32[64,384]{1,0:T(8,128)S(1)}, u32[]{:S(2)}, u32[]{:S(2)}) collective-permute-start(f32[64,384]{1,0:T(8,128)S(1)} %update.5.a), channel_id=1, source_target_pairs={{0,2},{1,3},{2,0},{3,1},{4,6},{5,7},{6,4},{7,5},{8,10},{9,11},{10,... | collective-permute-start | bytes 294920 | tf_op jit(solution)/shard_map/while/body/ppermute | solution.py:352
  167.1 13.9 %all-to-all-start.1 = ((f32[32,1,1152]{2,1,0:T(1,128)}), f32[32,1,1152]{2,1,0:T(1,128)S(1)}, u32[]{:S(2)}, u32[]{:S(2)}) async-start(f32[32,1,1152]{2,1,0:T(1,128)} %bitcast.29), calls=%async_computation.1 | async-start | bytes 294912 | tf_op jit(solution)/shard_map/while/body/all_to_all | solution.py:358
  185.2 7.2 %collective-permute-start.2 = (f32[64,384]{1,0:T(8,128)S(1)}, f32[64,384]{1,0:T(8,128)S(1)}, u32[]{:S(2)}, u32[]{:S(2)}) collective-permute-start(f32[64,384]{1,0:T(8,128)S(1)} %update.5.a), channel_id=1, source_target_pairs={{0,1},{1,2},{2,3},{3,0},{4,5},{5,6},{6,7},{7,4},{8,9},{9,10},{10,1... | collective-permute-start | bytes 294920 | tf_op jit(solution)/shard_map/while/body/ppermute | solution.py:352
  186.3 6.8 %collective-permute-start.3 = (f32[64,384]{1,0:T(8,128)S(1)}, f32[64,384]{1,0:T(8,128)S(1)}, u32[]{:S(2)}, u32[]{:S(2)}) collective-permute-start(f32[64,384]{1,0:T(8,128)S(1)} %update.5.a), channel_id=1, source_target_pairs={{0,2},{1,3},{2,0},{3,1},{4,6},{5,7},{6,4},{7,5},{8,10},{9,11},{10,... | collective-permute-start | bytes 294920 | tf_op jit(solution)/shard_map/while/body/ppermute | solution.py:352
  188.5 4.8 %collective-permute-start.4 = (f32[64,384]{1,0:T(8,128)S(1)}, f32[64,384]{1,0:T(8,128)S(1)}, u32[]{:S(2)}, u32[]{:S(2)}) collective-permute-start(f32[64,384]{1,0:T(8,128)S(1)} %update.5.a), channel_id=1, source_target_pairs={{0,3},{1,0},{2,1},{3,2},{4,7},{5,4},{6,5},{7,6},{8,11},{9,8},{10,9... | collective-permute-start | bytes 294920 | tf_op jit(solution)/shard_map/while/body/ppermute | solution.py:352
  211.1 13.9 %all-to-all-start.1 = ((f32[32,1,1152]{2,1,0:T(1,128)}), f32[32,1,1152]{2,1,0:T(1,128)S(1)}, u32[]{:S(2)}, u32[]{:S(2)}) async-start(f32[32,1,1152]{2,1,0:T(1,128)} %bitcast.29), calls=%async_computation.1 | async-start | bytes 294912 | tf_op jit(solution)/shard_map/while/body/all_to_all | solution.py:358
  229.1 7.2 %collective-permute-start.2 = (f32[64,384]{1,0:T(8,128)S(1)}, f32[64,384]{1,0:T(8,128)S(1)}, u32[]{:S(2)}, u32[]{:S(2)}) collective-permute-start(f32[64,384]{1,0:T(8,128)S(1)} %update.5.a), channel_id=1, source_target_pairs={{0,1},{1,2},{2,3},{3,0},{4,5},{5,6},{6,7},{7,4},{8,9},{9,10},{10,1... | collective-permute-start | bytes 294920 | tf_op jit(solution)/shard_map/while/body/ppermute | solution.py:352
  230.4 6.9 %collective-permute-start.3 = (f32[64,384]{1,0:T(8,128)S(1)}, f32[64,384]{1,0:T(8,128)S(1)}, u32[]{:S(2)}, u32[]{:S(2)}) collective-permute-start(f32[64,384]{1,0:T(8,128)S(1)} %update.5.a), channel_id=1, source_target_pairs={{0,2},{1,3},{2,0},{3,1},{4,6},{5,7},{6,4},{7,5},{8,10},{9,11},{10,... | collective-permute-start | bytes 294920 | tf_op jit(solution)/shard_map/while/body/ppermute | solution.py:352
  255.2 13.9 %all-to-all-start.1 = ((f32[32,1,1152]{2,1,0:T(1,128)}), f32[32,1,1152]{2,1,0:T(1,128)S(1)}, u32[]{:S(2)}, u32[]{:S(2)}) async-start(f32[32,1,1152]{2,1,0:T(1,128)} %bitcast.29), calls=%async_computation.1 | async-start | bytes 294912 | tf_op jit(solution)/shard_map/while/body/all_to_all | solution.py:358
  273.2 6.9 %collective-permute-start.2 = (f32[64,384]{1,0:T(8,128)S(1)}, f32[64,384]{1,0:T(8,128)S(1)}, u32[]{:S(2)}, u32[]{:S(2)}) collective-permute-start(f32[64,384]{1,0:T(8,128)S(1)} %update.5.a), channel_id=1, source_target_pairs={{0,1},{1,2},{2,3},{3,0},{4,5},{5,6},{6,7},{7,4},{8,9},{9,10},{10,1... | collective-permute-start | bytes 294920 | tf_op jit(solution)/shard_map/while/body/ppermute | solution.py:352
  274.3 6.9 %collective-permute-start.3 = (f32[64,384]{1,0:T(8,128)S(1)}, f32[64,384]{1,0:T(8,128)S(1)}, u32[]{:S(2)}, u32[]{:S(2)}) collective-permute-start(f32[64,384]{1,0:T(8,128)S(1)} %update.5.a), channel_id=1, source_target_pairs={{0,2},{1,3},{2,0},{3,1},{4,6},{5,7},{6,4},{7,5},{8,10},{9,11},{10,... | collective-permute-start | bytes 294920 | tf_op jit(solution)/shard_map/while/body/ppermute | solution.py:352
  316.2 6.8 %collective-permute-start.12 = (f32[64,384]{1,0:T(8,128)S(1)}, f32[64,384]{1,0:T(8,128)S(1)}, u32[]{:S(2)}, u32[]{:S(2)}) collective-permute-start(f32[64,384]{1,0:T(8,128)S(1)} %update.4.a), channel_id=1, source_target_pairs={{0,1},{1,2},{2,3},{3,0},{4,5},{5,6},{6,7},{7,4},{8,9},{9,10},{10,1... | collective-permute-start | bytes 294920 | tf_op jit(solution)/shard_map/ppermute | solution.py:352
  317.2 7.2 %collective-permute-start.13 = (f32[64,384]{1,0:T(8,128)S(1)}, f32[64,384]{1,0:T(8,128)S(1)}, u32[]{:S(2)}, u32[]{:S(2)}) collective-permute-start(f32[64,384]{1,0:T(8,128)S(1)} %update.4.a), channel_id=1, source_target_pairs={{0,2},{1,3},{2,0},{3,1},{4,6},{5,7},{6,4},{7,5},{8,10},{9,11},{10,... | collective-permute-start | bytes 294920 | tf_op jit(solution)/shard_map/ppermute | solution.py:352
  (24 other events, 103.5 us)

commit v10 on v9

--- a/solution.py
+++ b/solution.py
@@ -350,7 +350,7 @@
     def round_cells(value):
         return [value] + [
             lax.ppermute(value, "cell", [(i, (i + k) % cell_devices) for i in range(cell_devices)])
-            for k in range(1, cell_devices)
+            for k in range(cell_devices - 1, 0, -1)
         ]
 
     def exchange(value):

time: 348 us -> 350 us (level)
  waiting for transfers between devices: 46 us -> 68.7 us
  starting transfers between devices: 99.6 us -> 78.5 us
    ppermute x21, waiting for transfers between devices: 10.3 us -> 33 us  [round_cells(): lax.ppermute(value, 'cell', [(i, (i + k) % cell_devices) for i in range(c...]
    ppermute x21, starting transfers between devices: 29.6 us -> 13.1 us  [round_cells(): lax.ppermute(value, 'cell', [(i, (i + k) % cell_devices) for i in range(c...]
    ppermute x16, starting transfers between devices: 32.7 us -> 28 us  [swap_cores(): lax.ppermute(value, 'gene', [(i, i ^ 1) for i in range(gene_devices)])]
  transfers between devices with their start and end apart: 44 -> 44, of which waited for: 32 -> 36; matrix products, arithmetic and copies ran while one was open for 13% -> 13% of each run, Pallas kernels for 5% -> 5%
where the time goes in v10:
time: 350 us; the launch traced here: 349 us
  blocking collectives  115 us (33%)
  starting transfers between devices  78.5 us (22%)
  waiting for transfers between devices  68.7 us (20%)
  local copies, waits for them, and re-layouts  45.6 us (13%)
  Pallas kernels  38.8 us (11%)
    all_to_all x8, blocking collectives, exchange(): lax.all_to_all(pieces, 'gene', 0, 0, tiled=True, axis_index_groups=same_c...  115 us
    gather x6, local copies, waits for them, and re-layouts, tile_of(): return jnp.take(pool_by_cell, picks, axis=0, mode='clip')  39.8 us
    pallas_call x38, Pallas kernels, run(): return call(*args[:core], *near, *args[last:])  38.8 us
    all_to_all x7, starting transfers between devices, exchange(): lax.all_to_all(pieces, 'gene', 0, 0, tiled=True, axis_index_groups=same_c...  37.4 us
    ppermute x21, waiting for transfers between devices, round_cells(): lax.ppermute(value, 'cell', [(i, (i + k) % cell_devices) for i in range(c...  33 us
    ppermute x16, starting transfers between devices, swap_cores(): lax.ppermute(value, 'gene', [(i, i ^ 1) for i in range(gene_devices)])  28 us
    all_to_all x7, waiting for transfers between devices, exchange(): lax.all_to_all(pieces, 'gene', 0, 0, tiled=True, axis_index_groups=same_c...  21.9 us
    ppermute x16, waiting for transfers between devices, swap_cores(): lax.ppermute(value, 'gene', [(i, i ^ 1) for i in range(gene_devices)])  13.9 us
  transfers between devices with their start and end apart: 44, of which 36 were waited for; matrix products, arithmetic and copies ran while one was open for 13% of the time, Pallas kernels for 5%

profile of v10, /device:TPU:1, one launch (start us, length us, event | category | flops | bytes accessed | tf_op | source)
XLA Modules:
  0.0 348.8 jit_solution(2509569965494269279)
XLA Ops:
  0.0 4.8 %first.1 = (f32[288,128]{1,0:T(8,128)S(1)}, f32[288,128]{1,0:T(8,128)S(1)}) custom-call(s32[1]{0:T(128)} %bitcast.5.core_ref, s32[1]{0:T(128)} %bitcast.6.cell_ref, f32[64,320]{1,0:T(8,128)} %previous_ref.1, s32[7,1024]{1,0:T(8,128)} %picks_ref.1, bf16[320,4096]{1,0:T(8,128)(2,1)} %pool_ref.1), custom_call_target="tpu_custom_call" | custom-call | tf_op jit(solution)/shard_map/first/pallas_call | solution.py:35
  9.8 9.3 %all-to-all-start.2 = ((f32[32,1,1152]{2,1,0:T(1,128)}), f32[32,1,1152]{2,1,0:T(1,128)S(1)}, u32[]{:S(2)}, u32[]{:S(2)}) async-start(f32[32,1,1152]{2,1,0:T(1,128)} %bitcast.7), calls=%async_computation.2 | async-start | bytes 294912 | tf_op jit(solution)/shard_map/all_to_all | solution.py:358
  22.0 6.3 %all-to-all-done.2 = f32[32,1,1152]{2,1,0:T(1,128)S(1)} async-done(((f32[32,1,1152]{2,1,0:T(1,128)}), f32[32,1,1152]{2,1,0:T(1,128)S(1)}, u32[]{:S(2)}, u32[]{:S(2)}) %all-to-all-start.2) | async-done | bytes 147488 | tf_op jit(solution)/shard_map/all_to_all | solution.py:358
  29.0 4.7 %all-to-all-start.3 = ((f32[32,1,1152]{2,1,0:T(1,128)}), f32[32,1,1152]{2,1,0:T(1,128)S(1)}, u32[]{:S(2)}, u32[]{:S(2)}) async-start(f32[32,1,1152]{2,1,0:T(1,128)} %bitcast.9), calls=%async_computation.3 | async-start | bytes 294912 | tf_op jit(solution)/shard_map/all_to_all | solution.py:358
  33.7 9.5 %gather_fusion.1 = bf16[2048,320]{1,0:T(8,128)(2,1)S(1)} fusion(bf16[4096,320]{1,0:T(8,128)(2,1)} %bitcast.47, s32[2048]{0:T(1024)S(1)} %bitcast_clamp_fusion), kind=kCustom, calls=%fused_computation.1 | custom fusion | bytes 2629632 | tf_op jit(solution)/shard_map/jit(_take)/gather | solution.py:342
  59.9 224.4 %while.20 = (s32[]{:T(128)}, f32[288,128]{1,0:T(8,128)S(1)}, f32[288,128]{1,0:T(8,128)S(1)}, f32[64,320]{1,0:T(8,128)S(1)}, f32[1,320]{1,0:T(1,128)S(1)}, /*inde...) while((s32[]{:T(128)}, f32[288,128]{1,0:T(8,128)S(1)}, ...), condition=%wide.region_4.5_spmd, body=%wide.region_2.4_spmd.sunk | while | flops 1000656064 | bytes 6561931 | solution.py:420
  61.6 18.5 %all_to_all.46 = f32[32,1,1152]{2,1,0:T(1,128)S(1)} all-to-all(f32[32,1,1152]{2,1,0:T(1,128)S(1)} %bitcast.34), channel_id=1, replica_groups={{0,8,16,24,32,40,48,56,64,72,80,88,96,104,112,120,128,136,144,152,160,1..., dimensions={0} | all-to-all | bytes 294912 | tf_op jit(solution)/shard_map/while/body/all_to_all | solution.py:358
  80.7 4.7 %all-to-all-start.1 = ((f32[32,1,1152]{2,1,0:T(1,128)}), f32[32,1,1152]{2,1,0:T(1,128)S(1)}, u32[]{:S(2)}, u32[]{:S(2)}) async-start(f32[32,1,1152]{2,1,0:T(1,128)} %bitcast.29), calls=%async_computation.1 | async-start | bytes 294912 | tf_op jit(solution)/shard_map/while/body/all_to_all | solution.py:358
  85.4 6.1 %gather_fusion = bf16[1024,320]{1,0:T(8,128)(2,1)S(1)} fusion(bf16[4096,320]{1,0:T(8,128)(2,1)} %get-tuple-element.285, s32[1024]{0:T(1024)S(1)} %broadcast_clamp_fusion.2), kind=kCustom, calls=%fused_computation.clone.1 | custom fusion | bytes 1314816 | tf_op jit(solution)/shard_map/while/body/jit(_take)/gather | solution.py:342
  109.8 14.2 %all_to_all.46 = f32[32,1,1152]{2,1,0:T(1,128)S(1)} all-to-all(f32[32,1,1152]{2,1,0:T(1,128)S(1)} %bitcast.34), channel_id=1, replica_groups={{0,8,16,24,32,40,48,56,64,72,80,88,96,104,112,120,128,136,144,152,160,1..., dimensions={0} | all-to-all | bytes 294912 | tf_op jit(solution)/shard_map/while/body/all_to_all | solution.py:358
  124.6 4.7 %all-to-all-start.1 = ((f32[32,1,1152]{2,1,0:T(1,128)}), f32[32,1,1152]{2,1,0:T(1,128)S(1)}, u32[]{:S(2)}, u32[]{:S(2)}) async-start(f32[32,1,1152]{2,1,0:T(1,128)} %bitcast.29), calls=%async_computation.1 | async-start | bytes 294912 | tf_op jit(solution)/shard_map/while/body/all_to_all | solution.py:358
  129.3 6.1 %gather_fusion = bf16[1024,320]{1,0:T(8,128)(2,1)S(1)} fusion(bf16[4096,320]{1,0:T(8,128)(2,1)} %get-tuple-element.285, s32[1024]{0:T(1024)S(1)} %broadcast_clamp_fusion.2), kind=kCustom, calls=%fused_computation.clone.1 | custom fusion | bytes 1314816 | tf_op jit(solution)/shard_map/while/body/jit(_take)/gather | solution.py:342
  154.0 14.2 %all_to_all.46 = f32[32,1,1152]{2,1,0:T(1,128)S(1)} all-to-all(f32[32,1,1152]{2,1,0:T(1,128)S(1)} %bitcast.34), channel_id=1, replica_groups={{0,8,16,24,32,40,48,56,64,72,80,88,96,104,112,120,128,136,144,152,160,1..., dimensions={0} | all-to-all | bytes 294912 | tf_op jit(solution)/shard_map/while/body/all_to_all | solution.py:358
  168.8 4.7 %all-to-all-start.1 = ((f32[32,1,1152]{2,1,0:T(1,128)}), f32[32,1,1152]{2,1,0:T(1,128)S(1)}, u32[]{:S(2)}, u32[]{:S(2)}) async-start(f32[32,1,1152]{2,1,0:T(1,128)} %bitcast.29), calls=%async_computation.1 | async-start | bytes 294912 | tf_op jit(solution)/shard_map/while/body/all_to_all | solution.py:358
  173.5 6.1 %gather_fusion = bf16[1024,320]{1,0:T(8,128)(2,1)S(1)} fusion(bf16[4096,320]{1,0:T(8,128)(2,1)} %get-tuple-element.285, s32[1024]{0:T(1024)S(1)} %broadcast_clamp_fusion.2), kind=kCustom, calls=%fused_computation.clone.1 | custom fusion | bytes 1314816 | tf_op jit(solution)/shard_map/while/body/jit(_take)/gather | solution.py:342
  197.9 14.2 %all_to_all.46 = f32[32,1,1152]{2,1,0:T(1,128)S(1)} all-to-all(f32[32,1,1152]{2,1,0:T(1,128)S(1)} %bitcast.34), channel_id=1, replica_groups={{0,8,16,24,32,40,48,56,64,72,80,88,96,104,112,120,128,136,144,152,160,1..., dimensions={0} | all-to-all | bytes 294912 | tf_op jit(solution)/shard_map/while/body/all_to_all | solution.py:358
  212.7 4.7 %all-to-all-start.1 = ((f32[32,1,1152]{2,1,0:T(1,128)}), f32[32,1,1152]{2,1,0:T(1,128)S(1)}, u32[]{:S(2)}, u32[]{:S(2)}) async-start(f32[32,1,1152]{2,1,0:T(1,128)} %bitcast.29), calls=%async_computation.1 | async-start | bytes 294912 | tf_op jit(solution)/shard_map/while/body/all_to_all | solution.py:358
  217.4 6.1 %gather_fusion = bf16[1024,320]{1,0:T(8,128)(2,1)S(1)} fusion(bf16[4096,320]{1,0:T(8,128)(2,1)} %get-tuple-element.285, s32[1024]{0:T(1024)S(1)} %broadcast_clamp_fusion.2), kind=kCustom, calls=%fused_computation.clone.1 | custom fusion | bytes 1314816 | tf_op jit(solution)/shard_map/while/body/jit(_take)/gather | solution.py:342
  242.0 14.2 %all_to_all.46 = f32[32,1,1152]{2,1,0:T(1,128)S(1)} all-to-all(f32[32,1,1152]{2,1,0:T(1,128)S(1)} %bitcast.34), channel_id=1, replica_groups={{0,8,16,24,32,40,48,56,64,72,80,88,96,104,112,120,128,136,144,152,160,1..., dimensions={0} | all-to-all | bytes 294912 | tf_op jit(solution)/shard_map/while/body/all_to_all | solution.py:358
  256.9 4.7 %all-to-all-start.1 = ((f32[32,1,1152]{2,1,0:T(1,128)}), f32[32,1,1152]{2,1,0:T(1,128)S(1)}, u32[]{:S(2)}, u32[]{:S(2)}) async-start(f32[32,1,1152]{2,1,0:T(1,128)} %bitcast.29), calls=%async_computation.1 | async-start | bytes 294912 | tf_op jit(solution)/shard_map/while/body/all_to_all | solution.py:358
  261.6 6.1 %gather_fusion = bf16[1024,320]{1,0:T(8,128)(2,1)S(1)} fusion(bf16[4096,320]{1,0:T(8,128)(2,1)} %get-tuple-element.285, s32[1024]{0:T(1024)S(1)} %broadcast_clamp_fusion.2), kind=kCustom, calls=%fused_computation.clone.1 | custom fusion | bytes 1314816 | tf_op jit(solution)/shard_map/while/body/jit(_take)/gather | solution.py:342
  285.9 14.2 %all_to_all.43 = f32[32,1,1152]{2,1,0:T(1,128)S(1)} all-to-all(f32[32,1,1152]{2,1,0:T(1,128)S(1)} %bitcast.41), channel_id=1, replica_groups={{0,8,16,24,32,40,48,56,64,72,80,88,96,104,112,120,128,136,144,152,160,1..., dimensions={0} | all-to-all | bytes 294912 | tf_op jit(solution)/shard_map/all_to_all | solution.py:358
  300.1 13.7 %all_to_all.44 = f32[32,1,1152]{2,1,0:T(1,128)S(1)} all-to-all(f32[32,1,1152]{2,1,0:T(1,128)S(1)} %bitcast.45), channel_id=1, replica_groups={{0,8,16,24,32,40,48,56,64,72,80,88,96,104,112,120,128,136,144,152,160,1..., dimensions={0} | all-to-all | bytes 294912 | tf_op jit(solution)/shard_map/all_to_all | solution.py:358
  328.8 12.5 %all_to_all.45 = f32[32,1,1152]{2,1,0:T(1,128)S(1)} all-to-all(f32[32,1,1152]{2,1,0:T(1,128)S(1)} %bitcast.43), channel_id=1, replica_groups={{0,8,16,24,32,40,48,56,64,72,80,88,96,104,112,120,128,136,144,152,160,1..., dimensions={0} | all-to-all | bytes 294912 | tf_op jit(solution)/shard_map/all_to_all | solution.py:358
  (163 shorter events, 144.4 us)
Async XLA Ops:
  9.8 18.5 %all-to-all-start.2 = ((f32[32,1,1152]{2,1,0:T(1,128)}), f32[32,1,1152]{2,1,0:T(1,128)S(1)}, u32[]{:S(2)}, u32[]{:S(2)}) async-start(f32[32,1,1152]{2,1,0:T(1,128)} %bitcast.7), calls=%async_computation.2 | async-start | bytes 294912 | tf_op jit(solution)/shard_map/all_to_all | solution.py:358
  29.0 14.5 %all-to-all-start.3 = ((f32[32,1,1152]{2,1,0:T(1,128)}), f32[32,1,1152]{2,1,0:T(1,128)S(1)}, u32[]{:S(2)}, u32[]{:S(2)}) async-start(f32[32,1,1152]{2,1,0:T(1,128)} %bitcast.9), calls=%async_computation.3 | async-start | bytes 294912 | tf_op jit(solution)/shard_map/all_to_all | solution.py:358
  47.7 7.4 %collective-permute-start.7 = (f32[72,384]{1,0:T(8,128)S(1)}, f32[72,384]{1,0:T(8,128)S(1)}, u32[]{:S(2)}, u32[]{:S(2)}) collective-permute-start(f32[72,384]{1,0:T(8,128)S(1)} %update.3.a), channel_id=1, source_target_pairs={{0,3},{1,0},{2,1},{3,2},{4,7},{5,4},{6,5},{7,6},{8,11},{9,8},{10,9... | collective-permute-start | bytes 331784 | tf_op jit(solution)/shard_map/ppermute | solution.py:352
  50.5 5.8 %collective-permute-start.8 = (f32[72,384]{1,0:T(8,128)S(1)}, f32[72,384]{1,0:T(8,128)S(1)}, u32[]{:S(2)}, u32[]{:S(2)}) collective-permute-start(f32[72,384]{1,0:T(8,128)S(1)} %update.3.a), channel_id=1, source_target_pairs={{0,2},{1,3},{2,0},{3,1},{4,6},{5,7},{6,4},{7,5},{8,10},{9,11},{10,... | collective-permute-start | bytes 331784 | tf_op jit(solution)/shard_map/ppermute | solution.py:352
  50.9 8.5 %collective-permute-start.9 = (f32[72,384]{1,0:T(8,128)S(1)}, f32[72,384]{1,0:T(8,128)S(1)}, u32[]{:S(2)}, u32[]{:S(2)}) collective-permute-start(f32[72,384]{1,0:T(8,128)S(1)} %update.3.a), channel_id=1, source_target_pairs={{0,1},{1,2},{2,3},{3,0},{4,5},{5,6},{6,7},{7,4},{8,9},{9,10},{10,1... | collective-permute-start | bytes 331784 | tf_op jit(solution)/shard_map/ppermute | solution.py:352
  80.7 13.9 %all-to-all-start.1 = ((f32[32,1,1152]{2,1,0:T(1,128)}), f32[32,1,1152]{2,1,0:T(1,128)S(1)}, u32[]{:S(2)}, u32[]{:S(2)}) async-start(f32[32,1,1152]{2,1,0:T(1,128)} %bitcast.29), calls=%async_computation.1 | async-start | bytes 294912 | tf_op jit(solution)/shard_map/while/body/all_to_all | solution.py:358
  98.8 4.7 %collective-permute-start.2 = (f32[64,384]{1,0:T(8,128)S(1)}, f32[64,384]{1,0:T(8,128)S(1)}, u32[]{:S(2)}, u32[]{:S(2)}) collective-permute-start(f32[64,384]{1,0:T(8,128)S(1)} %update.5.a), channel_id=1, source_target_pairs={{0,3},{1,0},{2,1},{3,2},{4,7},{5,4},{6,5},{7,6},{8,11},{9,8},{10,9... | collective-permute-start | bytes 294920 | tf_op jit(solution)/shard_map/while/body/ppermute | solution.py:352
  99.1 5.0 %collective-permute-start.3 = (f32[64,384]{1,0:T(8,128)S(1)}, f32[64,384]{1,0:T(8,128)S(1)}, u32[]{:S(2)}, u32[]{:S(2)}) collective-permute-start(f32[64,384]{1,0:T(8,128)S(1)} %update.5.a), channel_id=1, source_target_pairs={{0,2},{1,3},{2,0},{3,1},{4,6},{5,7},{6,4},{7,5},{8,10},{9,11},{10,... | collective-permute-start | bytes 294920 | tf_op jit(solution)/shard_map/while/body/ppermute | solution.py:352
  99.5 8.0 %collective-permute-start.4 = (f32[64,384]{1,0:T(8,128)S(1)}, f32[64,384]{1,0:T(8,128)S(1)}, u32[]{:S(2)}, u32[]{:S(2)}) collective-permute-start(f32[64,384]{1,0:T(8,128)S(1)} %update.5.a), channel_id=1, source_target_pairs={{0,1},{1,2},{2,3},{3,0},{4,5},{5,6},{6,7},{7,4},{8,9},{9,10},{10,1... | collective-permute-start | bytes 294920 | tf_op jit(solution)/shard_map/while/body/ppermute | solution.py:352
  124.6 13.9 %all-to-all-start.1 = ((f32[32,1,1152]{2,1,0:T(1,128)}), f32[32,1,1152]{2,1,0:T(1,128)S(1)}, u32[]{:S(2)}, u32[]{:S(2)}) async-start(f32[32,1,1152]{2,1,0:T(1,128)} %bitcast.29), calls=%async_computation.1 | async-start | bytes 294912 | tf_op jit(solution)/shard_map/while/body/all_to_all | solution.py:358
  143.3 5.1 %collective-permute-start.3 = (f32[64,384]{1,0:T(8,128)S(1)}, f32[64,384]{1,0:T(8,128)S(1)}, u32[]{:S(2)}, u32[]{:S(2)}) collective-permute-start(f32[64,384]{1,0:T(8,128)S(1)} %update.5.a), channel_id=1, source_target_pairs={{0,2},{1,3},{2,0},{3,1},{4,6},{5,7},{6,4},{7,5},{8,10},{9,11},{10,... | collective-permute-start | bytes 294920 | tf_op jit(solution)/shard_map/while/body/ppermute | solution.py:352
  143.6 8.0 %collective-permute-start.4 = (f32[64,384]{1,0:T(8,128)S(1)}, f32[64,384]{1,0:T(8,128)S(1)}, u32[]{:S(2)}, u32[]{:S(2)}) collective-permute-start(f32[64,384]{1,0:T(8,128)S(1)} %update.5.a), channel_id=1, source_target_pairs={{0,1},{1,2},{2,3},{3,0},{4,5},{5,6},{6,7},{7,4},{8,9},{9,10},{10,1... | collective-permute-start | bytes 294920 | tf_op jit(solution)/shard_map/while/body/ppermute | solution.py:352
  168.8 13.9 %all-to-all-start.1 = ((f32[32,1,1152]{2,1,0:T(1,128)}), f32[32,1,1152]{2,1,0:T(1,128)S(1)}, u32[]{:S(2)}, u32[]{:S(2)}) async-start(f32[32,1,1152]{2,1,0:T(1,128)} %bitcast.29), calls=%async_computation.1 | async-start | bytes 294912 | tf_op jit(solution)/shard_map/while/body/all_to_all | solution.py:358
  186.8 4.7 %collective-permute-start.2 = (f32[64,384]{1,0:T(8,128)S(1)}, f32[64,384]{1,0:T(8,128)S(1)}, u32[]{:S(2)}, u32[]{:S(2)}) collective-permute-start(f32[64,384]{1,0:T(8,128)S(1)} %update.5.a), channel_id=1, source_target_pairs={{0,3},{1,0},{2,1},{3,2},{4,7},{5,4},{6,5},{7,6},{8,11},{9,8},{10,9... | collective-permute-start | bytes 294920 | tf_op jit(solution)/shard_map/while/body/ppermute | solution.py:352
  187.2 5.0 %collective-permute-start.3 = (f32[64,384]{1,0:T(8,128)S(1)}, f32[64,384]{1,0:T(8,128)S(1)}, u32[]{:S(2)}, u32[]{:S(2)}) collective-permute-start(f32[64,384]{1,0:T(8,128)S(1)} %update.5.a), channel_id=1, source_target_pairs={{0,2},{1,3},{2,0},{3,1},{4,6},{5,7},{6,4},{7,5},{8,10},{9,11},{10,... | collective-permute-start | bytes 294920 | tf_op jit(solution)/shard_map/while/body/ppermute | solution.py:352
  187.5 8.1 %collective-permute-start.4 = (f32[64,384]{1,0:T(8,128)S(1)}, f32[64,384]{1,0:T(8,128)S(1)}, u32[]{:S(2)}, u32[]{:S(2)}) collective-permute-start(f32[64,384]{1,0:T(8,128)S(1)} %update.5.a), channel_id=1, source_target_pairs={{0,1},{1,2},{2,3},{3,0},{4,5},{5,6},{6,7},{7,4},{8,9},{9,10},{10,1... | collective-permute-start | bytes 294920 | tf_op jit(solution)/shard_map/while/body/ppermute | solution.py:352
  212.7 13.9 %all-to-all-start.1 = ((f32[32,1,1152]{2,1,0:T(1,128)}), f32[32,1,1152]{2,1,0:T(1,128)S(1)}, u32[]{:S(2)}, u32[]{:S(2)}) async-start(f32[32,1,1152]{2,1,0:T(1,128)} %bitcast.29), calls=%async_computation.1 | async-start | bytes 294912 | tf_op jit(solution)/shard_map/while/body/all_to_all | solution.py:358
  231.4 5.0 %collective-permute-start.3 = (f32[64,384]{1,0:T(8,128)S(1)}, f32[64,384]{1,0:T(8,128)S(1)}, u32[]{:S(2)}, u32[]{:S(2)}) collective-permute-start(f32[64,384]{1,0:T(8,128)S(1)} %update.5.a), channel_id=1, source_target_pairs={{0,2},{1,3},{2,0},{3,1},{4,6},{5,7},{6,4},{7,5},{8,10},{9,11},{10,... | collective-permute-start | bytes 294920 | tf_op jit(solution)/shard_map/while/body/ppermute | solution.py:352
  231.7 8.0 %collective-permute-start.4 = (f32[64,384]{1,0:T(8,128)S(1)}, f32[64,384]{1,0:T(8,128)S(1)}, u32[]{:S(2)}, u32[]{:S(2)}) collective-permute-start(f32[64,384]{1,0:T(8,128)S(1)} %update.5.a), channel_id=1, source_target_pairs={{0,1},{1,2},{2,3},{3,0},{4,5},{5,6},{6,7},{7,4},{8,9},{9,10},{10,1... | collective-permute-start | bytes 294920 | tf_op jit(solution)/shard_map/while/body/ppermute | solution.py:352
  256.9 13.9 %all-to-all-start.1 = ((f32[32,1,1152]{2,1,0:T(1,128)}), f32[32,1,1152]{2,1,0:T(1,128)S(1)}, u32[]{:S(2)}, u32[]{:S(2)}) async-start(f32[32,1,1152]{2,1,0:T(1,128)} %bitcast.29), calls=%async_computation.1 | async-start | bytes 294912 | tf_op jit(solution)/shard_map/while/body/all_to_all | solution.py:358
  275.3 5.0 %collective-permute-start.3 = (f32[64,384]{1,0:T(8,128)S(1)}, f32[64,384]{1,0:T(8,128)S(1)}, u32[]{:S(2)}, u32[]{:S(2)}) collective-permute-start(f32[64,384]{1,0:T(8,128)S(1)} %update.5.a), channel_id=1, source_target_pairs={{0,2},{1,3},{2,0},{3,1},{4,6},{5,7},{6,4},{7,5},{8,10},{9,11},{10,... | collective-permute-start | bytes 294920 | tf_op jit(solution)/shard_map/while/body/ppermute | solution.py:352
  275.6 8.0 %collective-permute-start.4 = (f32[64,384]{1,0:T(8,128)S(1)}, f32[64,384]{1,0:T(8,128)S(1)}, u32[]{:S(2)}, u32[]{:S(2)}) collective-permute-start(f32[64,384]{1,0:T(8,128)S(1)} %update.5.a), channel_id=1, source_target_pairs={{0,1},{1,2},{2,3},{3,0},{4,5},{5,6},{6,7},{7,4},{8,9},{9,10},{10,1... | collective-permute-start | bytes 294920 | tf_op jit(solution)/shard_map/while/body/ppermute | solution.py:352
  318.5 5.0 %collective-permute-start.13 = (f32[64,384]{1,0:T(8,128)S(1)}, f32[64,384]{1,0:T(8,128)S(1)}, u32[]{:S(2)}, u32[]{:S(2)}) collective-permute-start(f32[64,384]{1,0:T(8,128)S(1)} %update.4.a), channel_id=1, source_target_pairs={{0,2},{1,3},{2,0},{3,1},{4,6},{5,7},{6,4},{7,5},{8,10},{9,11},{10,... | collective-permute-start | bytes 294920 | tf_op jit(solution)/shard_map/ppermute | solution.py:352
  318.8 8.0 %collective-permute-start.14 = (f32[64,384]{1,0:T(8,128)S(1)}, f32[64,384]{1,0:T(8,128)S(1)}, u32[]{:S(2)}, u32[]{:S(2)}) collective-permute-start(f32[64,384]{1,0:T(8,128)S(1)} %update.4.a), channel_id=1, source_target_pairs={{0,1},{1,2},{2,3},{3,0},{4,5},{5,6},{6,7},{7,4},{8,9},{9,10},{10,1... | collective-permute-start | bytes 294920 | tf_op jit(solution)/shard_map/ppermute | solution.py:352
  (24 other events, 101.0 us)
